TPU v7x, 32 devices: a whole 2x2x4 slice. The times are simulated.
32 devices in a mesh: tp: 4 (over z), cp: 8 (over y, x, core).
Axes of the slice: x: 2, y: 2, z: 4, core: 2. Of those that a mesh axis runs over, the one named last changes fastest.
Arguments:
- hidden: bfloat16 [4, 2048, 2560], P(None, 'cp')
- grad_out: bfloat16 [4, 2048, 2560], P(None, 'cp')
- w_dq: bfloat16 [2560, 768], replicated
- g_q: bfloat16 [768], replicated
- w_dkv: bfloat16 [2560, 288], replicated
- g_kv: bfloat16 [256], replicated
- w_uq: bfloat16 [768, 40, 96], P(None, 'tp')
- w_uk: bfloat16 [256, 40, 64], P(None, 'tp')
- w_uv: bfloat16 [256, 40, 64], P(None, 'tp')
- w_o: bfloat16 [40, 64, 2560], P('tp')
Outputs:
- output 1: bfloat16 [4, 2048, 2560], P(None, 'cp')
- output 2: bfloat16 [4, 2048, 2560], P(None, 'cp')
- output 3: float32 [2560, 768], replicated
- output 4: float32 [768], replicated
- output 5: float32 [2560, 288], replicated
- output 6: float32 [256], replicated
- output 7: float32 [768, 40, 96], P(None, 'tp')
- output 8: float32 [256, 40, 64], P(None, 'tp')
- output 9: float32 [256, 40, 64], P(None, 'tp')
- output 10: float32 [40, 64, 2560], P('tp')
All inputs are finite; a program needn't handle non-finite values.
Results may differ from a plain program's by a relative error of at most 0.01824.
Values are sent between devices in bfloat16 or wider.
A program may use at most 1 GiB of HBM per device.

v0:
```python
import jax
import jax.numpy as jnp
from jax import lax
from jax.sharding import PartitionSpec as P

EPS = 1e-6
THETA = 10000.0
NEG_BIG = -1e30


def layout_positions(seq_local, cp_size, cp_rank):
    half_len = seq_local // 2
    local_idx = jnp.arange(seq_local, dtype=jnp.int32)
    block_id = jnp.where(local_idx < half_len, cp_rank, 2 * cp_size - 1 - cp_rank)
    return block_id * half_len + local_idx % half_len


def rope_tables(positions, rope_dim):
    inv_freq = 1.0 / (THETA ** (jnp.arange(rope_dim // 2, dtype=jnp.float32) * 2.0 / rope_dim))
    angles = positions.astype(jnp.float32)[:, None] * inv_freq[None, :]
    return jnp.cos(angles), jnp.sin(angles)


def apply_rope(values, cos_tab, sin_tab):
    half_dim = values.shape[-1] // 2
    lead_half = values[..., :half_dim]
    tail_half = values[..., half_dim:]
    return jnp.concatenate([lead_half * cos_tab - tail_half * sin_tab, tail_half * cos_tab + lead_half * sin_tab], axis=-1)


def unrope(grad_vals, cos_tab, sin_tab):
    half_dim = grad_vals.shape[-1] // 2
    lead_half = grad_vals[..., :half_dim]
    tail_half = grad_vals[..., half_dim:]
    return jnp.concatenate([lead_half * cos_tab + tail_half * sin_tab, tail_half * cos_tab - lead_half * sin_tab], axis=-1)


def norm_f32(raw_vals, gain_vec):
    inv_rms = lax.rsqrt(jnp.mean(raw_vals * raw_vals, axis=-1, keepdims=True) + EPS)
    return raw_vals * inv_rms * gain_vec


def solution(mesh):
    cp_size = mesh.shape['cp']
    next_pairs = [(src_idx, (src_idx + 1) % cp_size) for src_idx in range(cp_size)]

    def per_device(hidden, grad_out, w_dq, g_q, w_dkv, g_kv, w_uq, w_uk, w_uv, w_o):
        cp_rank = lax.axis_index('cp')
        n_batch = hidden.shape[0]
        seq_local = hidden.shape[1]
        value_a6 = w_dq.shape[1]
        value_a7 = g_kv.shape[0]
        nope_dim = w_uk.shape[2]
        qk_dim = w_uq.shape[2]
        heads_dev = w_uq.shape[1]
        v_dim = w_uv.shape[2]
        score_scale = qk_dim ** -0.5
        positions = layout_positions(seq_local, cp_size, cp_rank)
        cos_tab, sin_tab = rope_tables(positions, qk_dim - nope_dim)
        cos_head = cos_tab[:, None, :]
        sin_head = sin_tab[:, None, :]

        cq_raw = jnp.einsum('btd,dq->btq', hidden, w_dq, preferred_element_type=jnp.float32).astype(jnp.bfloat16)
        kv_raw = jnp.einsum('btd,dc->btc', hidden, w_dkv, preferred_element_type=jnp.float32).astype(jnp.bfloat16)
        cq_f32 = cq_raw.astype(jnp.float32)
        ckv_f32 = kv_raw[..., :value_a7].astype(jnp.float32)
        gq_f32 = g_q.astype(jnp.float32)
        gkv_f32 = g_kv.astype(jnp.float32)
        c_q = norm_f32(cq_f32, gq_f32).astype(jnp.bfloat16)
        c_kv = norm_f32(ckv_f32, gkv_f32).astype(jnp.bfloat16)
        k_pe = apply_rope(kv_raw[..., value_a7:].astype(jnp.float32), cos_tab, sin_tab).astype(jnp.bfloat16)
        q_all = jnp.einsum('btq,qhe->bthe', c_q, w_uq, preferred_element_type=jnp.float32).astype(jnp.bfloat16)
        q_nope = q_all[..., :nope_dim]
        q_pe = apply_rope(q_all[..., nope_dim:].astype(jnp.float32), cos_head, sin_head).astype(jnp.bfloat16)
        k_nope = jnp.einsum('btc,chn->bthn', c_kv, w_uk, preferred_element_type=jnp.float32).astype(jnp.bfloat16)
        v_heads = jnp.einsum('btc,chv->bthv', c_kv, w_uv, preferred_element_type=jnp.float32).astype(jnp.bfloat16)

        def block_scores(kn_blk, kp_blk, src_rank):
            key_pos = layout_positions(seq_local, cp_size, src_rank)
            scores = jnp.einsum('bqhn,bkhn->bhqk', q_nope, kn_blk, preferred_element_type=jnp.float32) + jnp.einsum('bqhr,bkr->bhqk', q_pe, kp_blk, preferred_element_type=jnp.float32)
            return jnp.where(key_pos[None, :] <= positions[:, None], scores * score_scale, NEG_BIG)

        def attend(soft_stats, kn_blk, kp_blk, v_blk, src_rank):
            row_max, row_sum, out_acc = soft_stats
            scores = block_scores(kn_blk, kp_blk, src_rank)
            new_max = jnp.maximum(row_max, jnp.max(scores, axis=-1))
            rescale = jnp.exp(row_max - new_max)
            prob_blk = jnp.exp(scores - new_max[..., None])
            row_sum = row_sum * rescale + jnp.sum(prob_blk, axis=-1)
            out_acc = out_acc * rescale[..., None] + jnp.einsum('bhqk,bkhv->bhqv', prob_blk.astype(jnp.bfloat16), v_blk, preferred_element_type=jnp.float32)
            return new_max, row_sum, out_acc

        soft_stats = (jnp.full((n_batch, heads_dev, seq_local), NEG_BIG, jnp.float32), jnp.zeros((n_batch, heads_dev, seq_local), jnp.float32), jnp.zeros((n_batch, heads_dev, seq_local, v_dim), jnp.float32))
        soft_stats = attend(soft_stats, k_nope, k_pe, v_heads, cp_rank)

        def fwd_step(step_idx, loop_state):
            kn_blk, kp_blk, v_blk, soft_stats = loop_state
            kn_blk, kp_blk, v_blk = lax.ppermute((kn_blk, kp_blk, v_blk), 'cp', next_pairs)
            soft_stats = attend(soft_stats, kn_blk, kp_blk, v_blk, (cp_rank - step_idx) % cp_size)
            return kn_blk, kp_blk, v_blk, soft_stats

        loop_state = lax.fori_loop(1, cp_size, fwd_step, (k_nope, k_pe, v_heads, soft_stats))
        row_max, row_sum, out_acc = loop_state[3]
        o_heads = (out_acc / row_sum[..., None]).astype(jnp.bfloat16)
        log_sum = row_max + jnp.log(row_sum)
        attn_out = lax.psum(jnp.einsum('bhtv,hvd->btd', o_heads, w_o, preferred_element_type=jnp.float32), 'tp').astype(jnp.bfloat16)

        grad_o = jnp.einsum('btd,hvd->bhtv', grad_out, w_o, preferred_element_type=jnp.float32).astype(jnp.bfloat16)
        grad_w_o = jnp.einsum('bhtv,btd->hvd', o_heads, grad_out, preferred_element_type=jnp.float32)
        row_dot = jnp.einsum('bhtv,bhtv->bht', grad_o, o_heads, preferred_element_type=jnp.float32)

        def grad_block(kn_blk, kp_blk, v_blk, src_rank):
            prob_blk = jnp.exp(block_scores(kn_blk, kp_blk, src_rank) - log_sum[..., None])
            dv_part = jnp.einsum('bhqk,bhqv->bkhv', prob_blk.astype(jnp.bfloat16), grad_o, preferred_element_type=jnp.float32)
            dp_blk = jnp.einsum('bhqv,bkhv->bhqk', grad_o, v_blk, preferred_element_type=jnp.float32)
            ds_blk = (prob_blk * (dp_blk - row_dot[..., None]) * score_scale).astype(jnp.bfloat16)
            dqn_part = jnp.einsum('bhqk,bkhn->bqhn', ds_blk, kn_blk, preferred_element_type=jnp.float32)
            dqp_part = jnp.einsum('bhqk,bkr->bqhr', ds_blk, kp_blk, preferred_element_type=jnp.float32)
            dkn_part = jnp.einsum('bhqk,bqhn->bkhn', ds_blk, q_nope, preferred_element_type=jnp.float32)
            dkp_part = jnp.einsum('bhqk,bqhr->bkr', ds_blk, q_pe, preferred_element_type=jnp.float32)
            return dqn_part, dqp_part, dkn_part, dkp_part, dv_part

        own_parts = grad_block(k_nope, k_pe, v_heads, cp_rank)
        init_state = (k_nope, k_pe, v_heads, own_parts[2].astype(jnp.bfloat16), own_parts[3].astype(jnp.bfloat16), own_parts[4].astype(jnp.bfloat16), own_parts[0], own_parts[1])

        def bwd_step(step_idx, loop_state):
            kn_blk, kp_blk, v_blk, dkn_blk, dkp_blk, dv_blk, dq_nope, dq_pe = loop_state
            kn_blk, kp_blk, v_blk, dkn_blk, dkp_blk, dv_blk = lax.ppermute((kn_blk, kp_blk, v_blk, dkn_blk, dkp_blk, dv_blk), 'cp', next_pairs)
            step_parts = grad_block(kn_blk, kp_blk, v_blk, (cp_rank - step_idx) % cp_size)
            return (kn_blk, kp_blk, v_blk,
                    (dkn_blk.astype(jnp.float32) + step_parts[2]).astype(jnp.bfloat16),
                    (dkp_blk.astype(jnp.float32) + step_parts[3]).astype(jnp.bfloat16),
                    (dv_blk.astype(jnp.float32) + step_parts[4]).astype(jnp.bfloat16),
                    dq_nope + step_parts[0], dq_pe + step_parts[1])

        loop_state = lax.fori_loop(1, cp_size, bwd_step, init_state)
        grad_k_nope, grad_k_pe, grad_v = lax.ppermute((loop_state[3], loop_state[4], loop_state[5]), 'cp', next_pairs)
        grad_q = jnp.concatenate([loop_state[6], unrope(loop_state[7], cos_head, sin_head)], axis=-1).astype(jnp.bfloat16)

        grad_w_uq = jnp.einsum('btq,bthe->qhe', c_q, grad_q, preferred_element_type=jnp.float32)
        grad_w_uk = jnp.einsum('btc,bthn->chn', c_kv, grad_k_nope, preferred_element_type=jnp.float32)
        grad_w_uv = jnp.einsum('btc,bthv->chv', c_kv, grad_v, preferred_element_type=jnp.float32)
        latent_part = jnp.concatenate([
            jnp.einsum('bthe,qhe->btq', grad_q, w_uq, preferred_element_type=jnp.float32),
            jnp.einsum('bthn,chn->btc', grad_k_nope, w_uk, preferred_element_type=jnp.float32) + jnp.einsum('bthv,chv->btc', grad_v, w_uv, preferred_element_type=jnp.float32),
            grad_k_pe.astype(jnp.float32)], axis=-1)
        latent_grad = lax.psum(latent_part, 'tp')

        norm_q_pull = jax.vjp(norm_f32, cq_f32, gq_f32)[1]
        grad_cq_raw, grad_g_q = norm_q_pull(latent_grad[..., :value_a6])
        norm_kv_pull = jax.vjp(norm_f32, ckv_f32, gkv_f32)[1]
        grad_ckv_raw, grad_g_kv = norm_kv_pull(latent_grad[..., value_a6:value_a6 + value_a7])
        grad_kv_raw = jnp.concatenate([grad_ckv_raw, unrope(latent_grad[..., value_a6 + value_a7:], cos_tab, sin_tab)], axis=-1).astype(jnp.bfloat16)
        grad_cq_raw = grad_cq_raw.astype(jnp.bfloat16)
        grad_w_dq = jnp.einsum('btd,btq->dq', hidden, grad_cq_raw, preferred_element_type=jnp.float32)
        grad_w_dkv = jnp.einsum('btd,btc->dc', hidden, grad_kv_raw, preferred_element_type=jnp.float32)
        grad_hidden = (jnp.einsum('btq,dq->btd', grad_cq_raw, w_dq, preferred_element_type=jnp.float32) + jnp.einsum('btc,dc->btd', grad_kv_raw, w_dkv, preferred_element_type=jnp.float32)).astype(jnp.bfloat16)
        weight_grads = lax.psum((grad_w_dq, grad_g_q, grad_w_dkv, grad_g_kv, grad_w_uq, grad_w_uk, grad_w_uv, grad_w_o), 'cp')
        return (attn_out, grad_hidden) + tuple(weight_grads)

    seq_spec = P(None, 'cp', None)
    full_spec = P()
    head_spec = P(None, 'tp', None)
    out_head_spec = P('tp', None, None)
    all_specs = (seq_spec, seq_spec, full_spec, full_spec, full_spec, full_spec, head_spec, head_spec, head_spec, out_head_spec)
    return jax.shard_map(per_device, mesh=mesh, in_specs=all_specs, out_specs=all_specs, check_vma=False)
```

profile of v0, /device:TPU:0, one launch (start us, length us, event | category | flops | bytes accessed | tf_op | source)
XLA Modules:
  0.0 1606.3 jit_solution(12280222047540519)
XLA Ops:
  34.5 8.0 fusion.126
  57.2 318.4 %while.60 = (s32[]{:T(128)}, bf16[4,256,10,64]{1,3,2,0:T(8,128)(2,1)}, bf16[4,256,32]{1,2,0:T(8,128)(2,1)}, bf16[4,256,10,64]{1,3,2,0:T(8,128)(2,1)}, f32[4,10,2...) while((s32[]{:T(128)}, ...), condition=%wide.region_7.8_spmd.clone.clone, body=%wide.region_4.7_spmd.clone.clone.sunk | while | flops 861234176 | bytes 105452016 | solution.py:102
  60.4 16.1 %collective-permute-done.1 = bf16[4,256,32]{1,2,0:T(8,128)(2,1)S(1)} collective-permute-done((bf16[4,256,32]{1,2,0:T(8,128)(2,1)}, bf16[4,256,32]{1,2,0:T(8,128)(2,1)S(1)}, u32[]{:S(2)}, u32[]{:S(2)}) %collective-permute-start.1) | collective-permute-done | bytes 65568 | tf_op jit(solution)/shard_map/while/body/eval_jaxpr/ppermute | solution.py:98
  104.9 17.0 %collective-permute-done.1 = bf16[4,256,32]{1,2,0:T(8,128)(2,1)S(1)} collective-permute-done((bf16[4,256,32]{1,2,0:T(8,128)(2,1)}, bf16[4,256,32]{1,2,0:T(8,128)(2,1)S(1)}, u32[]{:S(2)}, u32[]{:S(2)}) %collective-permute-start.1) | collective-permute-done | bytes 65568 | tf_op jit(solution)/shard_map/while/body/eval_jaxpr/ppermute | solution.py:98
  149.3 17.9 %collective-permute-done.1 = bf16[4,256,32]{1,2,0:T(8,128)(2,1)S(1)} collective-permute-done((bf16[4,256,32]{1,2,0:T(8,128)(2,1)}, bf16[4,256,32]{1,2,0:T(8,128)(2,1)S(1)}, u32[]{:S(2)}, u32[]{:S(2)}) %collective-permute-start.1) | collective-permute-done | bytes 65568 | tf_op jit(solution)/shard_map/while/body/eval_jaxpr/ppermute | solution.py:98
  194.6 17.9 %collective-permute-done.1 = bf16[4,256,32]{1,2,0:T(8,128)(2,1)S(1)} collective-permute-done((bf16[4,256,32]{1,2,0:T(8,128)(2,1)}, bf16[4,256,32]{1,2,0:T(8,128)(2,1)S(1)}, u32[]{:S(2)}, u32[]{:S(2)}) %collective-permute-start.1) | collective-permute-done | bytes 65568 | tf_op jit(solution)/shard_map/while/body/eval_jaxpr/ppermute | solution.py:98
  239.9 17.9 %collective-permute-done.1 = bf16[4,256,32]{1,2,0:T(8,128)(2,1)S(1)} collective-permute-done((bf16[4,256,32]{1,2,0:T(8,128)(2,1)}, bf16[4,256,32]{1,2,0:T(8,128)(2,1)S(1)}, u32[]{:S(2)}, u32[]{:S(2)}) %collective-permute-start.1) | collective-permute-done | bytes 65568 | tf_op jit(solution)/shard_map/while/body/eval_jaxpr/ppermute | solution.py:98
  285.3 17.9 %collective-permute-done.1 = bf16[4,256,32]{1,2,0:T(8,128)(2,1)S(1)} collective-permute-done((bf16[4,256,32]{1,2,0:T(8,128)(2,1)}, bf16[4,256,32]{1,2,0:T(8,128)(2,1)S(1)}, u32[]{:S(2)}, u32[]{:S(2)}) %collective-permute-start.1) | collective-permute-done | bytes 65568 | tf_op jit(solution)/shard_map/while/body/eval_jaxpr/ppermute | solution.py:98
  330.6 17.9 %collective-permute-done.1 = bf16[4,256,32]{1,2,0:T(8,128)(2,1)S(1)} collective-permute-done((bf16[4,256,32]{1,2,0:T(8,128)(2,1)}, bf16[4,256,32]{1,2,0:T(8,128)(2,1)S(1)}, u32[]{:S(2)}, u32[]{:S(2)}) %collective-permute-start.1) | collective-permute-done | bytes 65568 | tf_op jit(solution)/shard_map/while/body/eval_jaxpr/ppermute | solution.py:98
  375.7 7.3 fusion.77
  401.8 583.3 %while.61 = (s32[]{:T(128)}, bf16[4,256,10,64]{1,3,2,0:T(8,128)(2,1)}, bf16[4,256,32]{1,2,0:T(8,128)(2,1)}, bf16[4,256,10,64]{1,3,2,0:T(8,128)(2,1)}, bf16[4,256...) while((s32[]{:T(128)}, ...), condition=%wide.region_10.11_spmd.clone.clone, body=%wide.region_9.10_spmd.clone.clone.sunk | while | flops 2209715200 | bytes 174150416 | solution.py:136
  406.2 15.1 collective-permute-done.4
  435.6 28.0 %collective-permute-done.5 = bf16[4,256,10,64]{1,3,2,0:T(8,128)(2,1)S(1)} collective-permute-done((bf16[4,256,10,64]{1,3,2,0:T(8,128)(2,1)}, bf16[4,256,10,64]{1,3,2,0:T(8,128)(2,1)S(1)}, u32[]{:S(2)}, u32[]{:S(2)}) %collective-permute-start.5) | collective-permute-done | bytes 1310752 | tf_op jit(solution)/shard_map/while/body/eval_jaxpr/ppermute | solution.py:128
  489.5 15.2 collective-permute-done.4
  518.9 28.0 %collective-permute-done.5 = bf16[4,256,10,64]{1,3,2,0:T(8,128)(2,1)S(1)} collective-permute-done((bf16[4,256,10,64]{1,3,2,0:T(8,128)(2,1)}, bf16[4,256,10,64]{1,3,2,0:T(8,128)(2,1)S(1)}, u32[]{:S(2)}, u32[]{:S(2)}) %collective-permute-start.5) | collective-permute-done | bytes 1310752 | tf_op jit(solution)/shard_map/while/body/eval_jaxpr/ppermute | solution.py:128
  572.8 15.2 collective-permute-done.4
  602.2 28.0 %collective-permute-done.5 = bf16[4,256,10,64]{1,3,2,0:T(8,128)(2,1)S(1)} collective-permute-done((bf16[4,256,10,64]{1,3,2,0:T(8,128)(2,1)}, bf16[4,256,10,64]{1,3,2,0:T(8,128)(2,1)S(1)}, u32[]{:S(2)}, u32[]{:S(2)}) %collective-permute-start.5) | collective-permute-done | bytes 1310752 | tf_op jit(solution)/shard_map/while/body/eval_jaxpr/ppermute | solution.py:128
  656.1 15.2 collective-permute-done.4
  685.5 28.0 %collective-permute-done.5 = bf16[4,256,10,64]{1,3,2,0:T(8,128)(2,1)S(1)} collective-permute-done((bf16[4,256,10,64]{1,3,2,0:T(8,128)(2,1)}, bf16[4,256,10,64]{1,3,2,0:T(8,128)(2,1)S(1)}, u32[]{:S(2)}, u32[]{:S(2)}) %collective-permute-start.5) | collective-permute-done | bytes 1310752 | tf_op jit(solution)/shard_map/while/body/eval_jaxpr/ppermute | solution.py:128
  739.4 15.2 collective-permute-done.4
  768.8 28.0 %collective-permute-done.5 = bf16[4,256,10,64]{1,3,2,0:T(8,128)(2,1)S(1)} collective-permute-done((bf16[4,256,10,64]{1,3,2,0:T(8,128)(2,1)}, bf16[4,256,10,64]{1,3,2,0:T(8,128)(2,1)S(1)}, u32[]{:S(2)}, u32[]{:S(2)}) %collective-permute-start.5) | collective-permute-done | bytes 1310752 | tf_op jit(solution)/shard_map/while/body/eval_jaxpr/ppermute | solution.py:128
  822.7 15.2 collective-permute-done.4
  852.1 28.0 %collective-permute-done.5 = bf16[4,256,10,64]{1,3,2,0:T(8,128)(2,1)S(1)} collective-permute-done((bf16[4,256,10,64]{1,3,2,0:T(8,128)(2,1)}, bf16[4,256,10,64]{1,3,2,0:T(8,128)(2,1)S(1)}, u32[]{:S(2)}, u32[]{:S(2)}) %collective-permute-start.5) | collective-permute-done | bytes 1310752 | tf_op jit(solution)/shard_map/while/body/eval_jaxpr/ppermute | solution.py:128
  906.0 15.2 collective-permute-done.4
  935.4 28.0 %collective-permute-done.5 = bf16[4,256,10,64]{1,3,2,0:T(8,128)(2,1)S(1)} collective-permute-done((bf16[4,256,10,64]{1,3,2,0:T(8,128)(2,1)}, bf16[4,256,10,64]{1,3,2,0:T(8,128)(2,1)S(1)}, u32[]{:S(2)}, u32[]{:S(2)}) %collective-permute-start.5) | collective-permute-done | bytes 1310752 | tf_op jit(solution)/shard_map/while/body/eval_jaxpr/ppermute | solution.py:128
  990.0 27.8 %collective-permute-done.11 = bf16[4,256,32]{1,2,0:T(8,128)(2,1)S(1)} collective-permute-done((bf16[4,256,32]{1,2,0:T(8,128)(2,1)}, bf16[4,256,32]{1,2,0:T(8,128)(2,1)S(1)}, u32[]{:S(2)}, u32[]{:S(2)}) %collective-permute-start.11) | collective-permute-done | bytes 65568 | tf_op jit(solution)/shard_map/ppermute | solution.py:137
  1023.3 8.5 convolution_bitcast_fusion.2
  1043.8 138.5 %all-reduce.6.cloned.1.call-done = f32[4,256,1056]{1,2,0:T(8,128)} async-done(((f32[4,256,1056]{1,2,0:T(8,128)}), f32[4,256,1056]{1,2,0:T(8,128)}) %all-reduce.6.cloned.1.call-update) | async-done | bytes 4325392 | tf_op jit(solution)/shard_map/psum | solution.py:147
  1188.1 9.9 convolution_bitcast_fusion.3
  1202.5 351.0 %all-reduce.9 = bf16[4,256,2560]{2,1,0:T(8,128)(2,1)} all-reduce(f32[4,256,2560]{2,1,0:T(8,128)} %convolution_bitcast_fusion.2), channel_id=1, replica_groups=mesh['tp'=4,'cp'=8] {'tp'}, use_global_device_ids=true, to_apply=%region_8.9 | all-reduce | flops 2621440 | bytes 15728640 | tf_op jit(solution)/shard_map/psum | solution.py:106
  1553.4 12.8 all-reduce
  1578.0 9.1 copy.45
  (665 shorter events, 591.5 us)
Async XLA Ops:
  7.2 1175.1 %all-reduce.6.cloned.1.call-start = ((), (), s32[]{:S(2)}) async-start(), calls=%async_computation | async-start | bytes 8650752 | tf_op jit(solution)/shard_map/psum | solution.py:147
  193.9 37.8 %collective-permute-start.2 = (bf16[4,256,10,64]{1,3,2,0:T(8,128)(2,1)}, bf16[4,256,10,64]{1,3,2,0:T(8,128)(2,1)}, u32[]{:S(2)}, u32[]{:S(2)}) collective-permute-start(bf16[4,256,10,64]{1,3,2,0:T(8,128)(2,1)} %get-tuple-element.1177), channel_id=1, source_target_pairs={{0,1},{1,2},{2,3},{3,4},{4,5},{5,6},{6,7},{7,0},{8,9},{9,10},{10,1... | collective-permute-start | bytes 3932168 | tf_op jit(solution)/shard_map/while/body/eval_jaxpr/ppermute | solution.py:98
  239.2 37.8 %collective-permute-start.2 = (bf16[4,256,10,64]{1,3,2,0:T(8,128)(2,1)}, bf16[4,256,10,64]{1,3,2,0:T(8,128)(2,1)}, u32[]{:S(2)}, u32[]{:S(2)}) collective-permute-start(bf16[4,256,10,64]{1,3,2,0:T(8,128)(2,1)} %get-tuple-element.1177), channel_id=1, source_target_pairs={{0,1},{1,2},{2,3},{3,4},{4,5},{5,6},{6,7},{7,0},{8,9},{9,10},{10,1... | collective-permute-start | bytes 3932168 | tf_op jit(solution)/shard_map/while/body/eval_jaxpr/ppermute | solution.py:98
  402.1 68.0 %collective-permute-start.7 = (bf16[4,256,32]{1,2,0:T(8,128)(2,1)}, bf16[4,256,32]{1,2,0:T(8,128)(2,1)S(1)}, u32[]{:S(2)}, u32[]{:S(2)}) collective-permute-start(bf16[4,256,32]{1,2,0:T(8,128)(2,1)} %get-tuple-element.1232), channel_id=1, source_target_pairs={{0,1},{1,2},{2,3},{3,4},{4,5},{5,6},{6,7},{7,0},{8,9},{9,10},{10,1... | collective-permute-start | bytes 196616 | tf_op jit(solution)/shard_map/while/body/eval_jaxpr/ppermute | solution.py:128
  402.6 69.0 %collective-permute-start.8 = (bf16[4,256,10,64]{1,3,2,0:T(8,128)(2,1)}, bf16[4,256,10,64]{1,3,2,0:T(8,128)(2,1)}, u32[]{:S(2)}, u32[]{:S(2)}) collective-permute-start(bf16[4,256,10,64]{1,3,2,0:T(8,128)(2,1)} %get-tuple-element.1233), channel_id=1, source_target_pairs={{0,1},{1,2},{2,3},{3,4},{4,5},{5,6},{6,7},{7,0},{8,9},{9,10},{10,1... | collective-permute-start | bytes 3932168 | tf_op jit(solution)/shard_map/while/body/eval_jaxpr/ppermute | solution.py:128
  406.0 69.1 %collective-permute-start.6 = (bf16[4,256,10,64]{1,3,2,0:T(8,128)(2,1)}, bf16[4,256,10,64]{1,3,2,0:T(8,128)(2,1)}, u32[]{:S(2)}, u32[]{:S(2)}) collective-permute-start(bf16[4,256,10,64]{1,3,2,0:T(8,128)(2,1)} %get-tuple-element.1231), channel_id=1, source_target_pairs={{0,1},{1,2},{2,3},{3,4},{4,5},{5,6},{6,7},{7,0},{8,9},{9,10},{10,1... | collective-permute-start | bytes 3932168 | tf_op jit(solution)/shard_map/while/body/eval_jaxpr/ppermute | solution.py:128
  421.4 42.1 %collective-permute-start.5 = (bf16[4,256,10,64]{1,3,2,0:T(8,128)(2,1)}, bf16[4,256,10,64]{1,3,2,0:T(8,128)(2,1)S(1)}, u32[]{:S(2)}, u32[]{:S(2)}) collective-permute-start(bf16[4,256,10,64]{1,3,2,0:T(8,128)(2,1)} %get-tuple-element.1230), channel_id=1, source_target_pairs={{0,1},{1,2},{2,3},{3,4},{4,5},{5,6},{6,7},{7,0},{8,9},{9,10},{10,1... | collective-permute-start | bytes 3932168 | tf_op jit(solution)/shard_map/while/body/eval_jaxpr/ppermute | solution.py:128
  485.3 68.0 %collective-permute-start.7 = (bf16[4,256,32]{1,2,0:T(8,128)(2,1)}, bf16[4,256,32]{1,2,0:T(8,128)(2,1)S(1)}, u32[]{:S(2)}, u32[]{:S(2)}) collective-permute-start(bf16[4,256,32]{1,2,0:T(8,128)(2,1)} %get-tuple-element.1232), channel_id=1, source_target_pairs={{0,1},{1,2},{2,3},{3,4},{4,5},{5,6},{6,7},{7,0},{8,9},{9,10},{10,1... | collective-permute-start | bytes 196616 | tf_op jit(solution)/shard_map/while/body/eval_jaxpr/ppermute | solution.py:128
  485.9 69.0 %collective-permute-start.8 = (bf16[4,256,10,64]{1,3,2,0:T(8,128)(2,1)}, bf16[4,256,10,64]{1,3,2,0:T(8,128)(2,1)}, u32[]{:S(2)}, u32[]{:S(2)}) collective-permute-start(bf16[4,256,10,64]{1,3,2,0:T(8,128)(2,1)} %get-tuple-element.1233), channel_id=1, source_target_pairs={{0,1},{1,2},{2,3},{3,4},{4,5},{5,6},{6,7},{7,0},{8,9},{9,10},{10,1... | collective-permute-start | bytes 3932168 | tf_op jit(solution)/shard_map/while/body/eval_jaxpr/ppermute | solution.py:128
  489.3 69.1 %collective-permute-start.6 = (bf16[4,256,10,64]{1,3,2,0:T(8,128)(2,1)}, bf16[4,256,10,64]{1,3,2,0:T(8,128)(2,1)}, u32[]{:S(2)}, u32[]{:S(2)}) collective-permute-start(bf16[4,256,10,64]{1,3,2,0:T(8,128)(2,1)} %get-tuple-element.1231), channel_id=1, source_target_pairs={{0,1},{1,2},{2,3},{3,4},{4,5},{5,6},{6,7},{7,0},{8,9},{9,10},{10,1... | collective-permute-start | bytes 3932168 | tf_op jit(solution)/shard_map/while/body/eval_jaxpr/ppermute | solution.py:128
  504.7 42.1 %collective-permute-start.5 = (bf16[4,256,10,64]{1,3,2,0:T(8,128)(2,1)}, bf16[4,256,10,64]{1,3,2,0:T(8,128)(2,1)S(1)}, u32[]{:S(2)}, u32[]{:S(2)}) collective-permute-start(bf16[4,256,10,64]{1,3,2,0:T(8,128)(2,1)} %get-tuple-element.1230), channel_id=1, source_target_pairs={{0,1},{1,2},{2,3},{3,4},{4,5},{5,6},{6,7},{7,0},{8,9},{9,10},{10,1... | collective-permute-start | bytes 3932168 | tf_op jit(solution)/shard_map/while/body/eval_jaxpr/ppermute | solution.py:128
  568.6 68.0 %collective-permute-start.7 = (bf16[4,256,32]{1,2,0:T(8,128)(2,1)}, bf16[4,256,32]{1,2,0:T(8,128)(2,1)S(1)}, u32[]{:S(2)}, u32[]{:S(2)}) collective-permute-start(bf16[4,256,32]{1,2,0:T(8,128)(2,1)} %get-tuple-element.1232), channel_id=1, source_target_pairs={{0,1},{1,2},{2,3},{3,4},{4,5},{5,6},{6,7},{7,0},{8,9},{9,10},{10,1... | collective-permute-start | bytes 196616 | tf_op jit(solution)/shard_map/while/body/eval_jaxpr/ppermute | solution.py:128
  569.2 69.1 %collective-permute-start.8 = (bf16[4,256,10,64]{1,3,2,0:T(8,128)(2,1)}, bf16[4,256,10,64]{1,3,2,0:T(8,128)(2,1)}, u32[]{:S(2)}, u32[]{:S(2)}) collective-permute-start(bf16[4,256,10,64]{1,3,2,0:T(8,128)(2,1)} %get-tuple-element.1233), channel_id=1, source_target_pairs={{0,1},{1,2},{2,3},{3,4},{4,5},{5,6},{6,7},{7,0},{8,9},{9,10},{10,1... | collective-permute-start | bytes 3932168 | tf_op jit(solution)/shard_map/while/body/eval_jaxpr/ppermute | solution.py:128
  572.6 69.1 %collective-permute-start.6 = (bf16[4,256,10,64]{1,3,2,0:T(8,128)(2,1)}, bf16[4,256,10,64]{1,3,2,0:T(8,128)(2,1)}, u32[]{:S(2)}, u32[]{:S(2)}) collective-permute-start(bf16[4,256,10,64]{1,3,2,0:T(8,128)(2,1)} %get-tuple-element.1231), channel_id=1, source_target_pairs={{0,1},{1,2},{2,3},{3,4},{4,5},{5,6},{6,7},{7,0},{8,9},{9,10},{10,1... | collective-permute-start | bytes 3932168 | tf_op jit(solution)/shard_map/while/body/eval_jaxpr/ppermute | solution.py:128
  588.0 42.1 %collective-permute-start.5 = (bf16[4,256,10,64]{1,3,2,0:T(8,128)(2,1)}, bf16[4,256,10,64]{1,3,2,0:T(8,128)(2,1)S(1)}, u32[]{:S(2)}, u32[]{:S(2)}) collective-permute-start(bf16[4,256,10,64]{1,3,2,0:T(8,128)(2,1)} %get-tuple-element.1230), channel_id=1, source_target_pairs={{0,1},{1,2},{2,3},{3,4},{4,5},{5,6},{6,7},{7,0},{8,9},{9,10},{10,1... | collective-permute-start | bytes 3932168 | tf_op jit(solution)/shard_map/while/body/eval_jaxpr/ppermute | solution.py:128
  651.9 68.0 %collective-permute-start.7 = (bf16[4,256,32]{1,2,0:T(8,128)(2,1)}, bf16[4,256,32]{1,2,0:T(8,128)(2,1)S(1)}, u32[]{:S(2)}, u32[]{:S(2)}) collective-permute-start(bf16[4,256,32]{1,2,0:T(8,128)(2,1)} %get-tuple-element.1232), channel_id=1, source_target_pairs={{0,1},{1,2},{2,3},{3,4},{4,5},{5,6},{6,7},{7,0},{8,9},{9,10},{10,1... | collective-permute-start | bytes 196616 | tf_op jit(solution)/shard_map/while/body/eval_jaxpr/ppermute | solution.py:128
  652.5 69.1 %collective-permute-start.8 = (bf16[4,256,10,64]{1,3,2,0:T(8,128)(2,1)}, bf16[4,256,10,64]{1,3,2,0:T(8,128)(2,1)}, u32[]{:S(2)}, u32[]{:S(2)}) collective-permute-start(bf16[4,256,10,64]{1,3,2,0:T(8,128)(2,1)} %get-tuple-element.1233), channel_id=1, source_target_pairs={{0,1},{1,2},{2,3},{3,4},{4,5},{5,6},{6,7},{7,0},{8,9},{9,10},{10,1... | collective-permute-start | bytes 3932168 | tf_op jit(solution)/shard_map/while/body/eval_jaxpr/ppermute | solution.py:128
  655.9 69.1 %collective-permute-start.6 = (bf16[4,256,10,64]{1,3,2,0:T(8,128)(2,1)}, bf16[4,256,10,64]{1,3,2,0:T(8,128)(2,1)}, u32[]{:S(2)}, u32[]{:S(2)}) collective-permute-start(bf16[4,256,10,64]{1,3,2,0:T(8,128)(2,1)} %get-tuple-element.1231), channel_id=1, source_target_pairs={{0,1},{1,2},{2,3},{3,4},{4,5},{5,6},{6,7},{7,0},{8,9},{9,10},{10,1... | collective-permute-start | bytes 3932168 | tf_op jit(solution)/shard_map/while/body/eval_jaxpr/ppermute | solution.py:128
  671.3 42.1 %collective-permute-start.5 = (bf16[4,256,10,64]{1,3,2,0:T(8,128)(2,1)}, bf16[4,256,10,64]{1,3,2,0:T(8,128)(2,1)S(1)}, u32[]{:S(2)}, u32[]{:S(2)}) collective-permute-start(bf16[4,256,10,64]{1,3,2,0:T(8,128)(2,1)} %get-tuple-element.1230), channel_id=1, source_target_pairs={{0,1},{1,2},{2,3},{3,4},{4,5},{5,6},{6,7},{7,0},{8,9},{9,10},{10,1... | collective-permute-start | bytes 3932168 | tf_op jit(solution)/shard_map/while/body/eval_jaxpr/ppermute | solution.py:128
  735.2 68.0 %collective-permute-start.7 = (bf16[4,256,32]{1,2,0:T(8,128)(2,1)}, bf16[4,256,32]{1,2,0:T(8,128)(2,1)S(1)}, u32[]{:S(2)}, u32[]{:S(2)}) collective-permute-start(bf16[4,256,32]{1,2,0:T(8,128)(2,1)} %get-tuple-element.1232), channel_id=1, source_target_pairs={{0,1},{1,2},{2,3},{3,4},{4,5},{5,6},{6,7},{7,0},{8,9},{9,10},{10,1... | collective-permute-start | bytes 196616 | tf_op jit(solution)/shard_map/while/body/eval_jaxpr/ppermute | solution.py:128
  735.8 69.1 %collective-permute-start.8 = (bf16[4,256,10,64]{1,3,2,0:T(8,128)(2,1)}, bf16[4,256,10,64]{1,3,2,0:T(8,128)(2,1)}, u32[]{:S(2)}, u32[]{:S(2)}) collective-permute-start(bf16[4,256,10,64]{1,3,2,0:T(8,128)(2,1)} %get-tuple-element.1233), channel_id=1, source_target_pairs={{0,1},{1,2},{2,3},{3,4},{4,5},{5,6},{6,7},{7,0},{8,9},{9,10},{10,1... | collective-permute-start | bytes 3932168 | tf_op jit(solution)/shard_map/while/body/eval_jaxpr/ppermute | solution.py:128
  739.2 69.1 %collective-permute-start.6 = (bf16[4,256,10,64]{1,3,2,0:T(8,128)(2,1)}, bf16[4,256,10,64]{1,3,2,0:T(8,128)(2,1)}, u32[]{:S(2)}, u32[]{:S(2)}) collective-permute-start(bf16[4,256,10,64]{1,3,2,0:T(8,128)(2,1)} %get-tuple-element.1231), channel_id=1, source_target_pairs={{0,1},{1,2},{2,3},{3,4},{4,5},{5,6},{6,7},{7,0},{8,9},{9,10},{10,1... | collective-permute-start | bytes 3932168 | tf_op jit(solution)/shard_map/while/body/eval_jaxpr/ppermute | solution.py:128
  754.6 42.1 %collective-permute-start.5 = (bf16[4,256,10,64]{1,3,2,0:T(8,128)(2,1)}, bf16[4,256,10,64]{1,3,2,0:T(8,128)(2,1)S(1)}, u32[]{:S(2)}, u32[]{:S(2)}) collective-permute-start(bf16[4,256,10,64]{1,3,2,0:T(8,128)(2,1)} %get-tuple-element.1230), channel_id=1, source_target_pairs={{0,1},{1,2},{2,3},{3,4},{4,5},{5,6},{6,7},{7,0},{8,9},{9,10},{10,1... | collective-permute-start | bytes 3932168 | tf_op jit(solution)/shard_map/while/body/eval_jaxpr/ppermute | solution.py:128
  818.5 68.0 %collective-permute-start.7 = (bf16[4,256,32]{1,2,0:T(8,128)(2,1)}, bf16[4,256,32]{1,2,0:T(8,128)(2,1)S(1)}, u32[]{:S(2)}, u32[]{:S(2)}) collective-permute-start(bf16[4,256,32]{1,2,0:T(8,128)(2,1)} %get-tuple-element.1232), channel_id=1, source_target_pairs={{0,1},{1,2},{2,3},{3,4},{4,5},{5,6},{6,7},{7,0},{8,9},{9,10},{10,1... | collective-permute-start | bytes 196616 | tf_op jit(solution)/shard_map/while/body/eval_jaxpr/ppermute | solution.py:128
  819.1 69.1 %collective-permute-start.8 = (bf16[4,256,10,64]{1,3,2,0:T(8,128)(2,1)}, bf16[4,256,10,64]{1,3,2,0:T(8,128)(2,1)}, u32[]{:S(2)}, u32[]{:S(2)}) collective-permute-start(bf16[4,256,10,64]{1,3,2,0:T(8,128)(2,1)} %get-tuple-element.1233), channel_id=1, source_target_pairs={{0,1},{1,2},{2,3},{3,4},{4,5},{5,6},{6,7},{7,0},{8,9},{9,10},{10,1... | collective-permute-start | bytes 3932168 | tf_op jit(solution)/shard_map/while/body/eval_jaxpr/ppermute | solution.py:128
  822.5 69.1 %collective-permute-start.6 = (bf16[4,256,10,64]{1,3,2,0:T(8,128)(2,1)}, bf16[4,256,10,64]{1,3,2,0:T(8,128)(2,1)}, u32[]{:S(2)}, u32[]{:S(2)}) collective-permute-start(bf16[4,256,10,64]{1,3,2,0:T(8,128)(2,1)} %get-tuple-element.1231), channel_id=1, source_target_pairs={{0,1},{1,2},{2,3},{3,4},{4,5},{5,6},{6,7},{7,0},{8,9},{9,10},{10,1... | collective-permute-start | bytes 3932168 | tf_op jit(solution)/shard_map/while/body/eval_jaxpr/ppermute | solution.py:128
  837.9 42.1 %collective-permute-start.5 = (bf16[4,256,10,64]{1,3,2,0:T(8,128)(2,1)}, bf16[4,256,10,64]{1,3,2,0:T(8,128)(2,1)S(1)}, u32[]{:S(2)}, u32[]{:S(2)}) collective-permute-start(bf16[4,256,10,64]{1,3,2,0:T(8,128)(2,1)} %get-tuple-element.1230), channel_id=1, source_target_pairs={{0,1},{1,2},{2,3},{3,4},{4,5},{5,6},{6,7},{7,0},{8,9},{9,10},{10,1... | collective-permute-start | bytes 3932168 | tf_op jit(solution)/shard_map/while/body/eval_jaxpr/ppermute | solution.py:128
  901.8 68.0 %collective-permute-start.7 = (bf16[4,256,32]{1,2,0:T(8,128)(2,1)}, bf16[4,256,32]{1,2,0:T(8,128)(2,1)S(1)}, u32[]{:S(2)}, u32[]{:S(2)}) collective-permute-start(bf16[4,256,32]{1,2,0:T(8,128)(2,1)} %get-tuple-element.1232), channel_id=1, source_target_pairs={{0,1},{1,2},{2,3},{3,4},{4,5},{5,6},{6,7},{7,0},{8,9},{9,10},{10,1... | collective-permute-start | bytes 196616 | tf_op jit(solution)/shard_map/while/body/eval_jaxpr/ppermute | solution.py:128
  902.4 69.1 %collective-permute-start.8 = (bf16[4,256,10,64]{1,3,2,0:T(8,128)(2,1)}, bf16[4,256,10,64]{1,3,2,0:T(8,128)(2,1)}, u32[]{:S(2)}, u32[]{:S(2)}) collective-permute-start(bf16[4,256,10,64]{1,3,2,0:T(8,128)(2,1)} %get-tuple-element.1233), channel_id=1, source_target_pairs={{0,1},{1,2},{2,3},{3,4},{4,5},{5,6},{6,7},{7,0},{8,9},{9,10},{10,1... | collective-permute-start | bytes 3932168 | tf_op jit(solution)/shard_map/while/body/eval_jaxpr/ppermute | solution.py:128
  905.8 69.1 %collective-permute-start.6 = (bf16[4,256,10,64]{1,3,2,0:T(8,128)(2,1)}, bf16[4,256,10,64]{1,3,2,0:T(8,128)(2,1)}, u32[]{:S(2)}, u32[]{:S(2)}) collective-permute-start(bf16[4,256,10,64]{1,3,2,0:T(8,128)(2,1)} %get-tuple-element.1231), channel_id=1, source_target_pairs={{0,1},{1,2},{2,3},{3,4},{4,5},{5,6},{6,7},{7,0},{8,9},{9,10},{10,1... | collective-permute-start | bytes 3932168 | tf_op jit(solution)/shard_map/while/body/eval_jaxpr/ppermute | solution.py:128
  921.2 42.1 %collective-permute-start.5 = (bf16[4,256,10,64]{1,3,2,0:T(8,128)(2,1)}, bf16[4,256,10,64]{1,3,2,0:T(8,128)(2,1)S(1)}, u32[]{:S(2)}, u32[]{:S(2)}) collective-permute-start(bf16[4,256,10,64]{1,3,2,0:T(8,128)(2,1)} %get-tuple-element.1230), channel_id=1, source_target_pairs={{0,1},{1,2},{2,3},{3,4},{4,5},{5,6},{6,7},{7,0},{8,9},{9,10},{10,1... | collective-permute-start | bytes 3932168 | tf_op jit(solution)/shard_map/while/body/eval_jaxpr/ppermute | solution.py:128
  1023.0 555.0 %all-reduce.8.cloned.1.call-start = ((), (), s32[]{:S(2)}) async-start(), calls=%async_computation.1 | async-start | bytes 43253760 | tf_op jit(solution)/shard_map/psum | solution.py:158
  (183 other events, 2034.7 us)
Sparse Core Ops, SparseCore 0:
  1023.1 159.1 all-reduce.5
  1202.6 267.8 all-reduce.7
where the time goes:
time: 1620 us; the launch traced here: 1610 us
  waiting for transfers between devices  591 us (36%)
  matrix products  433 us (27%)
  blocking collectives  364 us (22%)
  local copies, waits for them, and re-layouts  125 us (8%)
  other arithmetic  39.3 us (2%)
  starting transfers between devices  36.7 us (2%)
    psum x1, blocking collectives, per_device(): lax.psum(jnp.einsum('bhtv,hvd->btd', o_heads, w_o, preferred_element_type...  351 us
    ppermute x42, waiting for transfers between devices, bwd_step(): lax.ppermute((kn_blk, kp_blk, v_blk, dkn_blk, dkp_blk, dv_blk), 'cp', nex...  302 us
    psum x1, waiting for transfers between devices, per_device(): latent_grad = lax.psum(latent_part, 'tp')  139 us
    ppermute x21, waiting for transfers between devices, fwd_step(): lax.ppermute((kn_blk, kp_blk, v_blk), 'cp', next_pairs)  123 us
    dot_general x15, matrix products, block_scores(): jnp.einsum('bqhn,bkhn->bhqk', q_nope, kn_blk, preferred_element_type=jnp....  99.8 us
    dot_general x15, matrix products, block_scores(): jnp.einsum('bqhr,bkr->bhqk', q_pe, kp_blk, preferred_element_type=jnp.flo...  99.1 us
    while x189, local copies, waits for them, and re-layouts  92.5 us
  transfers between devices with their start and end apart: 68, of which 23 were waited for; matrix products, arithmetic and copies ran while one was open for 22% of the time, Pallas kernels for 0%

commit v1 on v0

v1 whole, which is shorter than its diff:
```python
import functools
import math

import jax
import jax.numpy as jnp
from jax import lax
from jax.experimental import pallas as pl
from jax.experimental.pallas import tpu as pltpu
from jax.sharding import PartitionSpec as P

EPS = 1e-6
THETA = 10000.0
NEG_BIG = -1e30
BF = jnp.bfloat16
F32 = jnp.float32
NT = (((1,), (1,)), ((), ()))
TN = (((0,), (0,)), ((), ()))
NN = (((1,), (0,)), ((), ()))
HB, QB, CH, SEQ = 128, 256, 512, 2048
HD, KD, LAT, QL = 64, 160, 288, 768
NBLK, NCP, NTP, NPAIR = 16, 8, 4, 5
TOK, DM, HV, QW, ALL = 1024, 2560, 640, 1280, 1056
RH = 16


def dot(a, b, dims):
    return lax.dot_general(a, b, dims, preferred_element_type=F32)


def owner(blk):
    if blk < NCP:
        return blk, slice(0, HB)
    return NBLK - 1 - blk, slice(HB, QB)


def attn_kernel(r_ref, q_ref, do_ref, wk_ref, wv_ref, cos_ref, sin_ref, *rest):
    kv_ref, o_ref, dq_ref, dw_ref, dkv_ref, ckv, ckvt, kcat, vv, s_scr, dp_scr, dk_acc, dv_acc, dckv, dkpe, qbd, dobd = rest
    b = pl.program_id(0)
    p = pl.program_id(1)
    n_pair = pl.num_programs(1)
    r = r_ref[0]
    scale = 96.0 ** -0.5
    c2 = scale * math.log2(math.e)

    @pl.when(p == 0)
    def _():
        for blk in range(NBLK):
            rows = slice(blk * HB, (blk + 1) * HB)
            dev, part = owner(blk)
            ckv[rows, :] = kv_ref[dev, 0, part, 0:QB]
            kcat[rows, HB:KD] = kv_ref[dev, 0, part, QB:LAT]
        for i in range(4):
            ckvt[:, i * CH:(i + 1) * CH] = ckv[i * CH:(i + 1) * CH, :].T
        dckv[...] = jnp.zeros_like(dckv)
        dkpe[...] = jnp.zeros_like(dkpe)

    wkv = jnp.concatenate([wk_ref[...], wv_ref[...]], axis=1)
    for i in range(4):
        rows = slice(i * CH, (i + 1) * CH)
        kv = dot(ckv[rows, :], wkv, NN).astype(BF)
        kcat[rows, 0:HB] = kv[:, 0:HB]
        vv[rows, :] = kv[:, HB:QB]

    cos_t = cos_ref[...]
    sin_t = sin_ref[...]
    lane = lax.broadcasted_iota(jnp.int32, (HB, HB), 1)
    zero = jnp.zeros((HB, HB), BF)
    qpt = q_ref[0, :, HB:QB].astype(F32).T
    roped = []
    for h in range(2):
        u1 = qpt[h * 32:h * 32 + 16, :]
        u2 = qpt[h * 32 + 16:h * 32 + 32, :]
        roped.append(u1 * cos_t - u2 * sin_t)
        roped.append(u2 * cos_t + u1 * sin_t)
    qpe = jnp.concatenate(roped + [jnp.zeros((HD, QB), F32)], axis=0).T.astype(BF)
    for s in range(2):
        rows = slice(s * HB, (s + 1) * HB)
        qn = q_ref[0, rows, 0:HB]
        gg = do_ref[0, rows, :]
        qbd[s, 0:HB, 0:HB] = jnp.where(lane < HD, qn, zero)
        qbd[s, HB:QB, 0:HB] = jnp.where(lane < HD, zero, qn)
        qbd[s, 0:HB, HB:KD] = qpe[rows, 0:32]
        qbd[s, HB:QB, HB:KD] = qpe[rows, 32:64]
        dobd[s, 0:HB, :] = jnp.where(lane < HD, gg, zero)
        dobd[s, HB:QB, :] = jnp.where(lane < HD, zero, gg)

    low = r < 4
    sel3 = jnp.where(low, 1, 0)
    chunks = [(1, 0), (1, 1), (1, 2), (sel3, jnp.where(low, 3, 0)), (0, jnp.where(low, 0, 1))]

    def keys(c):
        kc = chunks[c][1]
        if isinstance(kc, int):
            return slice(kc * CH, (kc + 1) * CH)
        return pl.ds(pl.multiple_of(kc * CH, CH), CH)

    diff = (lax.broadcasted_iota(jnp.int32, (CH, QB), 0)
            - lax.rem(lax.broadcasted_iota(jnp.int32, (CH, QB), 1), HB))
    maxes = []
    for c in range(5):
        sel, kc = chunks[c]
        s = dot(kcat[keys(c), :], qbd[sel], NT)
        if c >= 2:
            blk = jnp.where(sel == 1, 15 - r, r)
            s = jnp.where(diff <= blk * HB - kc * CH, s, NEG_BIG)
        s_scr[c] = s
        maxes.append(jnp.max(s, axis=0, keepdims=True))

    def join(vals, op, ident):
        ident = jnp.full_like(vals[3], ident)
        top = op(op(op(vals[0], vals[1]), vals[2]), jnp.where(low, vals[3], ident))
        bot = op(vals[4], jnp.where(low, ident, vals[3]))
        return [top, top, top, jnp.where(low, top, bot), bot]

    m = join(maxes, jnp.maximum, NEG_BIG)
    sums, dots = [], []
    for c in range(5):
        sel, kc = chunks[c]
        e = jnp.exp2((s_scr[c] - m[c]) * c2)
        s_scr[c] = e
        sums.append(jnp.sum(e, axis=0, keepdims=True))
        dp = dot(vv[keys(c), :], dobd[sel], NT)
        dp_scr[c] = dp
        dots.append(jnp.sum(e * dp, axis=0, keepdims=True))
    total = join(sums, jnp.add, 0.0)
    inv = [1.0 / t for t in total]
    dsum = join(dots, jnp.add, 0.0)
    delta = [d * i for d, i in zip(dsum, inv)]
    ots, dqts = [], []
    dk_acc[3 * CH:SEQ, :] = jnp.zeros((CH, KD), F32)
    dv_acc[3 * CH:SEQ, :] = jnp.zeros((CH, HB), F32)
    for c in range(5):
        sel, kc = chunks[c]
        pr = s_scr[c] * inv[c]
        pb = pr.astype(BF)
        ds = (pr * (dp_scr[c] - delta[c])).astype(BF)
        ots.append(dot(vv[keys(c), :], pb, TN))
        dqts.append(dot(kcat[keys(c), :], ds, TN))
        dv = dot(pb, dobd[sel], NN)
        dk = dot(ds, qbd[sel], NN)
        if c < 3:
            dk_acc[keys(c), :] = dk
            dv_acc[keys(c), :] = dv
        else:
            dk_acc[keys(c), :] += dk
            dv_acc[keys(c), :] += dv
    ot = join(ots, jnp.add, 0.0)
    dqt = join(dqts, jnp.add, 0.0)
    for s in range(2):
        rows = slice(s * HB, (s + 1) * HB)
        a = ot[0 if s == 1 else 4]
        o_ref[0, rows, :] = jnp.concatenate([a[0:HD, 0:HB], a[HD:HB, HB:QB]], axis=0).T.astype(BF)
        g = dqt[0 if s == 1 else 4] * scale
        dq_ref[0, rows, 0:HB] = jnp.concatenate([g[0:HD, 0:HB], g[HD:HB, HB:QB]], axis=0).T.astype(BF)
        pe = []
        for h in range(2):
            g1 = g[128:144, h * HB:(h + 1) * HB]
            g2 = g[144:160, h * HB:(h + 1) * HB]
            ct = cos_t[:, rows]
            st = sin_t[:, rows]
            pe.append(g1 * ct + g2 * st)
            pe.append(g2 * ct - g1 * st)
        dq_ref[0, rows, HB:QB] = jnp.concatenate(pe + [jnp.zeros((HD, HB), F32)], axis=0).T.astype(BF)

    dwt = jnp.zeros((QB, QB), F32)
    for i in range(4):
        rows = slice(i * CH, (i + 1) * CH)
        dkv = jnp.concatenate([(dk_acc[rows, 0:HB] * scale).astype(BF), dv_acc[rows, :].astype(BF)], axis=1)
        dkpe[rows, :] += dk_acc[rows, HB:KD] * scale
        dckv[rows, :] += dot(dkv, wkv, NT)
        dwt = dwt + dot(ckvt[:, rows], dkv, NN)

    @pl.when(b == 0)
    def _():
        dw_ref[p] = dwt

    @pl.when(b > 0)
    def _():
        dw_ref[p] += dwt

    @pl.when(p == n_pair - 1)
    def _():
        for blk in range(NBLK):
            rows = slice(blk * HB, (blk + 1) * HB)
            dev, part = owner(blk)
            dkv_ref[dev, 0, part, 0:QB] = dckv[rows, :].astype(BF)
            dkv_ref[dev, 0, part, QB:LAT] = dkpe[rows, :].astype(BF)


def attention(rank, q, do, wk, wv, cos_t, sin_t, kv, b0, nb):
    pair_blk = lambda w: pl.BlockSpec((1, QB, w), lambda b, p, *_: (b0 + b, 0, p))
    out_blk = lambda w: pl.BlockSpec((1, QB, w), lambda b, p, *_: (b, 0, p))
    w_blk = pl.BlockSpec((QB, HB), lambda b, p, *_: (0, p))
    full = pl.BlockSpec((16, QB), lambda b, p, *_: (0, 0))
    kv_blk = pl.BlockSpec((NCP, 1, QB, LAT), lambda b, p, *_: (0, b0 + b, 0, 0))
    dkv_blk = pl.BlockSpec((NCP, 1, QB, LAT), lambda b, p, *_: (0, b, 0, 0))
    grid_spec = pltpu.PrefetchScalarGridSpec(
        num_scalar_prefetch=1,
        grid=(nb, NPAIR),
        in_specs=[pair_blk(QB), pair_blk(HB), w_blk, w_blk, full, full, kv_blk],
        out_specs=[out_blk(HB), out_blk(QB), pl.BlockSpec((NPAIR, QB, QB), lambda b, p, *_: (0, 0, 0)), dkv_blk],
        scratch_shapes=[
            pltpu.VMEM((SEQ, QB), BF), pltpu.VMEM((QB, SEQ), BF), pltpu.VMEM((SEQ, KD), BF), pltpu.VMEM((SEQ, HB), BF),
            pltpu.VMEM((5, CH, QB), F32), pltpu.VMEM((5, CH, QB), F32),
            pltpu.VMEM((SEQ, KD), F32), pltpu.VMEM((SEQ, HB), F32),
            pltpu.VMEM((SEQ, QB), F32), pltpu.VMEM((SEQ, 32), F32),
            pltpu.VMEM((2, QB, KD), BF), pltpu.VMEM((2, QB, HB), BF),
        ])
    return pl.pallas_call(
        attn_kernel,
        grid_spec=grid_spec,
        out_shape=[jax.ShapeDtypeStruct((nb, QB, HV), BF), jax.ShapeDtypeStruct((nb, QB, QW), BF), jax.ShapeDtypeStruct((NPAIR, QB, QB), F32),
                   jax.ShapeDtypeStruct((NCP, nb, QB, LAT), BF)],
        compiler_params=pltpu.CompilerParams(vmem_limit_bytes=50 * 1024 * 1024),
        cost_estimate=pl.CostEstimate(flops=nb * 20_000_000_000, bytes_accessed=nb * 8_000_000, transcendentals=0),
        name="attn",
    )(rank, q, do, wk, wv, cos_t, sin_t, kv)


def plane_kernel(n_arr, reduce, gather, n_z, *refs):
    ins, refs = refs[:n_arr], refs[n_arr:]
    outs, refs = refs[:n_arr], refs[n_arr:]
    r = lax.axis_index('cp')
    z = lax.axis_index('tp')
    send, recv, scratch = refs[0], refs[1], refs[2:]
    peers = {1: {'cp': r ^ 1}, 2: {'cp': r ^ 2}, 4: {'cp': r ^ 4}}
    barrier = pltpu.get_barrier_semaphore()
    targets = list(peers.values()) + [{'tp': lax.rem(z + d, NTP)} for d in range(1, n_z)]
    for t in targets:
        pl.semaphore_signal(barrier, inc=1, device_id=t, device_id_type=pl.DeviceIdType.MESH)
    pl.semaphore_wait(barrier, len(targets))
    count = [0]
    started = []

    def copy(src, dst, target):
        k = count[0]
        count[0] += 1
        c = pltpu.make_async_remote_copy(src_ref=src, dst_ref=dst, send_sem=send.at[k], recv_sem=recv.at[k],
                                         device_id=target, device_id_type=pl.DeviceIdType.MESH)
        c.start()
        started.append(c)
        return c

    work = []
    for i in range(n_arr):
        w = {'in': ins[i], 'out': outs[i]}
        if reduce:
            w['rc'], w['sb'], w['rd'], w['rx'], w['ry'] = scratch[:5]
            scratch = scratch[5:]
            rows = w['rd'].shape[0]
        else:
            rows = ins[i].shape[0]
        if gather:
            w['g'] = scratch[0]
            scratch = scratch[1:]
        w['a'] = slice(0, (rows // 2 + RH - 1) // RH * RH)
        w['b'] = slice(w['a'].stop, rows)
        work.append(w)
    if reduce:
        for w in work:
            w['c'] = [None] * 4
        for k in (3, 1, 2, 0):
            for w in work:
                w['c'][k] = copy(w['in'].at[r ^ (2 * k + 1)], w['rc'].at[k], peers[1])

        def local(w, k):
            w['c'][k].wait_recv()
            return w['in'][r ^ (2 * k)].astype(F32) + w['rc'][k].astype(F32)

        for w in work:
            w['sb'][3] = local(w, 3).astype(BF)
            w['da'] = copy(w['sb'].at[3, w['a']], w['rd'].at[w['a']], peers[2])
            w['db'] = copy(w['sb'].at[3, w['b']], w['rd'].at[w['b']], peers[4])
        for w in work:
            w['sb'][1] = local(w, 1).astype(BF)
            w['xa'] = copy(w['sb'].at[1, w['a']], w['rx'].at[w['a']], peers[2])
            w['sb'][2] = local(w, 2).astype(BF)
            w['yb'] = copy(w['sb'].at[2, w['b']], w['ry'].at[w['b']], peers[4])
        for w in work:
            w['da'].wait_recv()
            w['sb'][2, w['a']] = (w['sb'][2, w['a']].astype(F32) + w['rd'][w['a']].astype(F32)).astype(BF)
            w['ya'] = copy(w['sb'].at[2, w['a']], w['ry'].at[w['a']], peers[4])
            w['db'].wait_recv()
            w['sb'][1, w['b']] = (w['sb'][1, w['b']].astype(F32) + w['rd'][w['b']].astype(F32)).astype(BF)
            w['xb'] = copy(w['sb'].at[1, w['b']], w['rx'].at[w['b']], peers[2])
        for w in work:
            base = local(w, 0)
            for name in ('xa', 'yb', 'ya', 'xb'):
                w[name].wait_recv()
            total = base + w['rx'][...].astype(F32) + w['ry'][...].astype(F32)
            if gather:
                w['g'][z * NCP * (n_z > 1) + r] = total.astype(BF)
            else:
                w['out'][...] = total
    elif gather:
        for w in work:
            w['g'][r] = w['in'][...]
    if gather:
        def fan(w, zz):
            own = w['g'].at[zz + r]
            return {'zz': zz, 2: copy(own, own, peers[2]), 4: copy(own, own, peers[4]), 1: copy(own, own, peers[1])}

        flows = []
        z_copies = []
        for w in work:
            if n_z > 1:
                own = w['g'].at[z * NCP + r]
                z_copies.append([copy(own, own, {'tp': lax.rem(z + d, NTP)}) for d in range(1, n_z)])
            flows.append([fan(w, z * NCP if n_z > 1 else 0)])
        for d in range(n_z):
            for i, w in enumerate(work):
                f = flows[i][d]
                gx, gy = w['g'].at[f['zz'] + (r ^ 2)], w['g'].at[f['zz'] + (r ^ 4)]
                f[2].wait_recv()
                f['dy'] = copy(gx.at[w['b']], gx.at[w['b']], peers[4])
                f['cx'] = copy(gx, gx, peers[1])
                f[4].wait_recv()
                f['dx'] = copy(gy.at[w['a']], gy.at[w['a']], peers[2])
                f['cy'] = copy(gy, gy, peers[1])
                if d + 1 < n_z:
                    z_copies[i][d].wait_recv()
                    flows[i].append(fan(w, lax.rem(z + NTP - (d + 1), NTP) * NCP))
        for d in range(n_z):
            for i, w in enumerate(work):
                f = flows[i][d]
                f['dy'].wait_recv()
                f['dx'].wait_recv()
                gd = w['g'].at[f['zz'] + (r ^ 6)]
                f['cd'] = copy(gd, gd, peers[1])
        for d in range(n_z):
            for i, w in enumerate(work):
                f = flows[i][d]
                for name in (1, 'cx', 'cy', 'cd'):
                    f[name].wait_recv()
        for w in work:
            w['out'][...] = w['g'][...]
    for c in started:
        c.wait_send()


def plane(arrs, cid, reduce, gather, n_z=1):
    scratch, shapes = [], []
    n_copy = 0
    for v in arrs:
        n, m = v.shape[-2:]
        if reduce:
            scratch += [pltpu.VMEM((4, n, m), BF), pltpu.VMEM((4, n, m), BF)] + [pltpu.VMEM((n, m), BF)] * 3
            n_copy += 10
        if gather:
            scratch.append(pltpu.VMEM((NCP * n_z, n, m), BF))
            shapes.append(jax.ShapeDtypeStruct((NCP * n_z, n, m), BF))
            n_copy += 8 * n_z + n_z - 1
        else:
            shapes.append(jax.ShapeDtypeStruct((n, m), F32))
    vmem = pl.BlockSpec(memory_space=pltpu.VMEM)
    return pl.pallas_call(
        functools.partial(plane_kernel, len(arrs), reduce, gather, n_z),
        out_shape=shapes,
        in_specs=[vmem] * len(arrs),
        out_specs=[vmem] * len(arrs),
        scratch_shapes=[pltpu.SemaphoreType.DMA((n_copy,)), pltpu.SemaphoreType.DMA((n_copy,))] + scratch,
        compiler_params=pltpu.CompilerParams(collective_id=cid, has_side_effects=True, vmem_limit_bytes=60 * TOK * TOK),
        cost_estimate=pl.CostEstimate(flops=30_000_000_000, bytes_accessed=10_000_000, transcendentals=0),
        name="plane",
    )(*arrs)


def zshift(v, d):
    return lax.ppermute(v, 'tp', [(i, (i + d) % NTP) for i in range(NTP)])


def zgather(v, z):
    rel = [v] + [zshift(v, d) for d in range(1, NTP)]
    return [lax.select_n((z - j) % NTP, *rel) for j in range(NTP)]


def norm_f32(raw_vals, gain_vec):
    inv_rms = lax.rsqrt(jnp.mean(raw_vals * raw_vals, axis=-1, keepdims=True) + EPS)
    return raw_vals * inv_rms * gain_vec


def solution(mesh):
    def per_device(hidden, grad_out, w_dq, g_q, w_dkv, g_kv, w_uq, w_uk, w_uv, w_o):
        rank = lax.axis_index('cp')
        z = lax.axis_index('tp')
        x2 = hidden.reshape(TOK, DM)
        dy2 = grad_out.reshape(TOK, DM)
        half = 16
        inv_freq = 1.0 / (THETA ** (jnp.arange(half, dtype=F32) * 2.0 / 32))
        idx = jnp.arange(QB, dtype=jnp.int32)
        positions = jnp.where(idx < HB, rank, NBLK - 1 - rank) * HB + idx % HB
        angles = positions.astype(F32)[:, None] * inv_freq[None, :]
        cos_tab, sin_tab = jnp.cos(angles), jnp.sin(angles)
        cos_t, sin_t = cos_tab.T, sin_tab.T
        gq = g_q.astype(F32)
        gkv = g_kv.astype(F32)

        kv_raw = dot(x2, w_dkv, NN).astype(BF)
        ckv_f32 = kv_raw[:, :QB].astype(F32)
        c_kv = norm_f32(ckv_f32, gkv).astype(BF)
        pe = kv_raw[:, QB:].astype(F32).reshape(4, QB, 32)
        pe1, pe2 = pe[..., :half], pe[..., half:]
        k_pe = jnp.concatenate([pe1 * cos_tab - pe2 * sin_tab, pe2 * cos_tab + pe1 * sin_tab], axis=-1).astype(BF)
        kv, = plane([jnp.concatenate([c_kv, k_pe.reshape(TOK, 32)], axis=-1)], 0, False, True)
        kv = kv.reshape(NCP, 4, QB, LAT)

        wo2 = w_o.reshape(HV, DM)
        wo_slice, kv = lax.optimization_barrier((lax.dynamic_slice_in_dim(wo2, rank * 80, 80, 0), kv))
        wo_all = lax.all_gather(wo_slice, ('tp', 'cp'), axis=0, tiled=True)

        cq_raw = dot(x2, w_dq, NN).astype(BF)
        cq_f32 = cq_raw.astype(F32)
        c_q = norm_f32(cq_f32, gq).astype(BF)
        w_q = jnp.concatenate([w_uq[:, :, :HD].reshape(QL, NPAIR, HB), w_uq[:, :, HD:].reshape(QL, NPAIR, HD), jnp.zeros((QL, NPAIR, HD), BF)], axis=2).reshape(QL, QW)
        q = dot(c_q, w_q, NN).astype(BF).reshape(4, QB, QW)
        do = dot(dy2, wo2, NT).astype(BF).reshape(4, QB, HV)
        wk = w_uk.reshape(QB, HV)
        wv = w_uv.reshape(QB, HV)

        n_split = 2
        nb = 4 // n_split
        runs = [attention(rank.reshape(1), q, do, wk, wv, cos_t, sin_t, kv, i * nb, nb) for i in range(n_split)]
        o_all = [zgather(run[0], z) for run in runs]
        o_all = jnp.concatenate([jnp.concatenate(parts, axis=2) for parts in o_all], axis=0).reshape(TOK, NTP * HV)
        attn_out = dot(o_all, wo_all, NN).astype(BF).reshape(4, QB, DM)
        o = jnp.concatenate([run[0] for run in runs], axis=0).reshape(TOK, HV)
        dq = jnp.concatenate([run[1] for run in runs], axis=0).reshape(TOK, QW)
        dwkv = sum(run[2] for run in runs)
        dkv = jnp.concatenate([run[3] for run in runs], axis=1).reshape(NCP, TOK, LAT)

        dckv, = plane([dkv], 1, True, False)
        lat_q = dot(dq, w_q, NT)
        lat = jnp.concatenate([lat_q, dckv], axis=-1).reshape(4, QB, ALL)
        lat_bf = lat.astype(BF)
        own = lax.dynamic_index_in_dim(lat, z, 0, keepdims=False)
        for d in range(1, NTP):
            mine = lax.dynamic_index_in_dim(lat_bf, (z + d) % NTP, 0, keepdims=False)
            own = own + zshift(mine, d).astype(F32)

        cq_own = lax.dynamic_slice_in_dim(cq_f32, z * QB, QB, 0)
        ckv_own = lax.dynamic_slice_in_dim(ckv_f32, z * QB, QB, 0)
        g_cq, grad_g_q = jax.vjp(norm_f32, cq_own, gq)[1](own[:, :QL])
        g_ckv, grad_g_kv = jax.vjp(norm_f32, ckv_own, gkv)[1](own[:, QL:TOK])
        p1, p2 = own[:, TOK:TOK + half], own[:, TOK + half:]
        raw = jnp.concatenate([g_cq, g_ckv, p1 * cos_tab + p2 * sin_tab, p2 * cos_tab - p1 * sin_tab], axis=-1).astype(BF)
        raw_all = jnp.concatenate(zgather(raw, z), axis=0)

        x_slice = lax.dynamic_slice_in_dim(x2, z * HV, HV, 1)
        dwd = dot(x_slice, raw_all, TN).astype(BF).reshape(NCP, 80, ALL)
        dwd, = plane([dwd], 2, True, True, NTP)
        dwd = dwd.reshape(DM, ALL).astype(F32)
        w_d = jnp.concatenate([w_dq, w_dkv], axis=1)
        grad_hidden = dot(raw_all, w_d, NT).astype(BF).reshape(4, QB, DM)

        dwq = dot(c_q, dq, TN).astype(BF).reshape(NCP, 96, QW)
        dwkv = dwkv.transpose(1, 0, 2).reshape(NCP, 32, QW).astype(BF)
        dwo = dot(o, dy2, TN).astype(BF).reshape(NCP, 80, DM)
        dwq, dwkv, dwo = plane([dwq, dwkv, dwo], 3, True, True)
        grad_g_q, grad_g_kv = lax.psum((grad_g_q, grad_g_kv), ('tp', 'cp'))
        dwq = dwq.reshape(QL, NPAIR, QB).astype(F32)
        grad_uq = jnp.concatenate([dwq[:, :, :HB].reshape(QL, 10, HD), dwq[:, :, HB:HB + HD].reshape(QL, 10, 32)], axis=-1)
        dwkv = dwkv.reshape(QB, NPAIR, QB).astype(F32)
        grad_uk = dwkv[:, :, :HB].reshape(QB, 10, HD)
        grad_uv = dwkv[:, :, HB:].reshape(QB, 10, HD)
        return (attn_out, grad_hidden, dwd[:, :QL], grad_g_q, dwd[:, QL:], grad_g_kv, grad_uq, grad_uk, grad_uv, dwo.reshape(10, HD, DM).astype(F32))

    seq_spec = P(None, 'cp', None)
    full_spec = P()
    head_spec = P(None, 'tp', None)
    out_head_spec = P('tp', None, None)
    all_specs = (seq_spec, seq_spec, full_spec, full_spec, full_spec, full_spec, head_spec, head_spec, head_spec, out_head_spec)
    return jax.shard_map(per_device, mesh=mesh, in_specs=all_specs, out_specs=all_specs, check_vma=False)
```

time: 1620 us -> 656 us (0.40)
  waiting for transfers between devices: 591 us -> 26.3 us
  matrix products: 433 us -> 74.8 us
  Pallas kernels: 0 us -> 304 us
  blocking collectives: 364 us -> 76.6 us
  local copies, waits for them, and re-layouts: 125 us -> 88.4 us
  starting transfers between devices: 36.7 us -> 14.7 us
    ppermute x66 -> x12, waiting for transfers between devices: 453 us -> 26.2 us  [zshift(): return lax.ppermute(v, 'tp', [(i, (i + d) % NTP) for i in range(NTP)])]
    dot_general x104 -> x10, matrix products: 433 us -> 74.8 us  [dot(): return lax.dot_general(a, b, dims, preferred_element_type=F32)]
    pallas_call x0 -> x6, Pallas kernels: none -> 304 us  [the longest x4 207 us: plane(): pl.pallas_call(functools.partial(plane_kernel, len(arrs), reduce, gather,...]
    psum x2 -> x1, blocking collectives: 364 us -> 76.6 us  [per_device(): grad_g_q, grad_g_kv = lax.psum((grad_g_q, grad_g_kv), ('tp', 'cp'))]
    psum x2 -> x0, waiting for transfers between devices: 139 us -> none  [the longest x1 139 us: per_device(): latent_grad = lax.psum(latent_part, 'tp')]
    while x189 -> x0, local copies, waits for them, and re-layouts: 92.5 us -> none
    ppermute x66 -> x12, starting transfers between devices: 36.4 us -> 14.7 us  [zshift(): return lax.ppermute(v, 'tp', [(i, (i + d) % NTP) for i in range(NTP)])]
    reduce_sum x8 -> x0, other arithmetic: 19.4 us -> none  [attend(): row_sum = row_sum * rescale + jnp.sum(prob_blk, axis=-1)]
  transfers between devices with their start and end apart: 68 -> 13, of which waited for: 23 -> 2; matrix products, arithmetic and copies ran while one was open for 22% -> 22% of each run, Pallas kernels for 0% -> 34%
where the time goes in v1:
time: 656 us; the launch traced here: 643 us
  Pallas kernels  304 us (46%)
  local copies, waits for them, and re-layouts  88.4 us (13%)
  blocking collectives  76.6 us (12%)
  matrix products  74.8 us (11%)
  other arithmetic  43.5 us (7%)
  waiting for transfers between devices  26.3 us (4%)
  between operations  15.1 us (2%)
  starting transfers between devices  14.7 us (2%)
    pallas_call x4, Pallas kernels, plane(): pl.pallas_call(functools.partial(plane_kernel, len(arrs), reduce, gather,...  207 us
    pallas_call x2, Pallas kernels, attention(): pl.pallas_call(attn_kernel, grid_spec=grid_spec, out_shape=[jax.ShapeDtyp...  96.6 us
    psum x1, blocking collectives, per_device(): grad_g_q, grad_g_kv = lax.psum((grad_g_q, grad_g_kv), ('tp', 'cp'))  76.6 us
    dot_general x10, matrix products, dot(): return lax.dot_general(a, b, dims, preferred_element_type=F32)  74.8 us
    ppermute x12, waiting for transfers between devices, zshift(): return lax.ppermute(v, 'tp', [(i, (i + d) % NTP) for i in range(NTP)])  26.2 us
    unnamed x73, local copies, waits for them, and re-layouts  23 us
    ppermute x12, starting transfers between devices, zshift(): return lax.ppermute(v, 'tp', [(i, (i + d) % NTP) for i in range(NTP)])  14.7 us
  transfers between devices with their start and end apart: 13, of which 2 were waited for; matrix products, arithmetic and copies ran while one was open for 22% of the time, Pallas kernels for 34%

profile of v1, /device:TPU:0, one launch (start us, length us, event | category | flops | bytes accessed | tf_op | source)
XLA Modules:
  0.0 643.1 jit_solution(13071288945059039703)
XLA Ops:
  8.7 6.5 %convolution_convert_fusion.6 = bf16[1024,288]{1,0:T(8,128)(2,1)S(1)} fusion(bf16[1024,2560]{1,0:T(8,128)(2,1)} %bitcast.94, bf16[2560,288]{0,1:T(8,128)(2,1)} %param.14), kind=kOutput, calls=%fused_computation.24 | convolution fusion | flops 1510244352 | bytes 7307264 | tf_op jit(solution)/shard_map/dot_general | solution.py:27
  16.4 6.0 multiply_reduce_fusion
  26.2 7.8 %convolution_convert_fusion.5 = bf16[1024,640]{1,0:T(8,128)(2,1)} fusion(bf16[1024,2560]{1,0:T(8,128)(2,1)} %bitcast.93, bf16[640,2560]{1,0:T(8,128)(2,1)S(1)} %bitcast.70), kind=kOutput, calls=%fused_computation.23 | convolution fusion | flops 3356098560 | bytes 9830400 | tf_op jit(solution)/shard_map/dot_general | solution.py:27
  39.3 37.4 %plane.4 = bf16[8,1024,288]{2,1,0:T(8,128)(2,1)} custom-call(bf16[1024,288]{1,0:T(8,128)(2,1)} %pad_maximum_fusion.5.refs_0_), custom_call_target="tpu_custom_call" | custom-call | flops 30000001024 | bytes 10000000 | tf_op jit(solution)/shard_map/plane/pallas_call | solution.py:356
  79.3 3.7 convolution_convert_fusion.1
  83.0 48.5 %attn.3 = (bf16[2,256,640]{2,1,0:T(8,128)(2,1)}, bf16[2,256,1280]{2,1,0:T(8,128)(2,1)S(1)}, f32[5,256,256]{2,1,0:T(8,128)S(1)}, bf16[8,2,256,288]{3,2,1,0:T(8,128)(2,1)}) custom-call(s32[1]{0:T(128)} %bitcast.r_ref, bf16[4,256,1280]{2,1,0:T(8,128)(2,1)} %bitcast.104, bf16[4,256,640]{2,1,0:T(8,128)(2,1)} %bitcast.107, bf16[256,640]{1,0:T(8,128)(2,1)S(1)} %copy-done.4, ...), custom_call_target="tpu_custom_call" | custom-call | flops 40000000000 | bytes 16000000 | tf_op jit(solution)/shard_map/attn/pallas_call | solution.py:209
  138.6 48.1 %attn.2 = (bf16[2,256,640]{2,1,0:T(8,128)(2,1)S(1)}, bf16[2,256,1280]{2,1,0:T(8,128)(2,1)S(1)}, f32[5,256,256]{2,1,0:T(8,128)S(1)}, bf16[8,2,256,288]{3,2,1,0:T(8,128)(2,1)}) custom-call(s32[1]{0:T(128)} %bitcast.r_ref, bf16[4,256,1280]{2,1,0:T(8,128)(2,1)} %bitcast.105, bf16[4,256,640]{2,1,0:T(8,128)(2,1)} %bitcast.108, bf16[256,640]{1,0:T(8,128)(2,1)S(1)} %copy-done.5, ...), custom_call_target="tpu_custom_call" | custom-call | flops 40000000000 | bytes 16000000 | tf_op jit(solution)/shard_map/attn/pallas_call | solution.py:209
  187.7 5.7 pad_maximum_fusion
  193.4 47.9 %plane.5 = f32[1024,288]{1,0:T(8,128)} custom-call(bf16[8,1024,288]{2,1,0:T(8,128)(2,1)} %bitcast.76), custom_call_target="tpu_custom_call" | custom-call | flops 30000001024 | bytes 10000000 | tf_op jit(solution)/shard_map/plane/pallas_call | solution.py:356
  241.3 2.9 copy.146
  259.8 3.9 copy.167
  263.8 6.0 reshape.272
  271.9 6.3 convolution_convert_fusion.2
  278.2 8.0 %bitcast_convert_fusion = bf16[640,2560]{1,0:T(8,128)(2,1)} fusion(bf16[4,256,2560]{2,1,0:T(8,128)(2,1)} %param.11, bf16[2,256,640]{2,1,0:T(8,128)(2,1)} %get-tuple-element.25, bf16[2,256,640]{2,1,0:T(8,128)(2,1)S(1)} %get-tuple-element.24), kind=kOutput, calls=%fused_computation | convolution fusion | flops 3357736960 | bytes 9830400 | tf_op jit(solution)/shard_map/dot_general | solution.py:27
  286.2 62.9 %plane.7 = (bf16[8,96,1280]{2,1,0:T(8,128)(2,1)}, bf16[8,32,1280]{2,1,0:T(8,128)(2,1)}, bf16[8,80,2560]{2,1,0:T(8,128)(2,1)}) custom-call(bf16[8,96,1280]{2,1,0:T(8,128)(2,1)} %bitcast.106, bf16[8,32,1280]{2,1,0:T(8,128)(2,1)} %convert_element_type.122.refs_1_, bf16[8,80,2560]{2,1,0:T(8,128)(2,1)} %bitcast.103), custom_call_target="tpu_custom_call" | custom-call | flops 30000001024 | bytes 10000000 | tf_op jit(solution)/shard_map/plane/pallas_call | solution.py:356
  349.1 4.9 copy.172
  354.0 6.4 reshape.284
  360.4 3.1 slice.74
  365.5 3.5 pad_maximum_fusion.2
  371.5 2.7 constant_dynamic-slice_fusion
  381.0 5.6 convert.33
  407.3 76.6 %all-reduce = (f32[768]{0:T(1024)}, f32[256]{0:T(256)}) all-reduce(f32[768]{0:T(1024)S(1)} %get-tuple-element.46, f32[256]{0:T(256)S(1)} %get-tuple-element.48), channel_id=1, replica_groups=mesh['tp'=4,'cp'=8] {'tp','cp'}, use_global_device_ids=true, to_apply=%region_7.8 | all-reduce | flops 1024 | bytes 8192 | tf_op jit(solution)/shard_map/psum | solution.py:459
  490.8 3.1 maximum_maximum_fusion
  493.9 21.4 %collective-permute-done.10 = bf16[256,1056]{0,1:T(8,128)(2,1)} collective-permute-done((bf16[256,1056]{0,1:T(8,128)(2,1)}, bf16[256,1056]{0,1:T(8,128)(2,1)}, u32[]{:S(2)}, u32[]{:S(2)}) %collective-permute-start.10) | collective-permute-done | bytes 540704 | tf_op jit(solution)/shard_map/ppermute | solution.py:369
  516.7 4.8 collective-permute-done.11
  525.8 3.2 convolution_convert_fusion.3
  531.3 58.8 %plane.6 = bf16[32,80,1056]{2,1,0:T(8,128)(2,1)} custom-call(bf16[8,80,1056]{2,1,0:T(8,128)(2,1)} %bitcast.85), custom_call_target="tpu_custom_call" | custom-call | flops 30000001024 | bytes 10000000 | tf_op jit(solution)/shard_map/plane/pallas_call | solution.py:356
  590.1 3.4 bitcast_convert_fusion.1
  593.6 3.8 slice.72
  599.6 5.2 copy.179
  604.8 10.7 %fusion.4 = bf16[1024,2560]{1,0:T(8,128)(2,1)} fusion(bf16[2560,288]{1,0:T(8,128)(2,1)S(1)} %copy-done.15, bf16[2560,768]{1,0:T(8,128)(2,1)} %param.12, bf16[256,1056]{1,0:T(8,128)(2,1)} %copy-done.21, bf16[256,1056]{1,0:T(8,128)(2,1)} %copy-done.22, bf16[256,1056]{1,0:T(8,128)(2,1)} %copy-done.23, bf16[256,1056]{1,0:T(8,128)(2,1)S(1)} %get-tuple-element.60), kind=kOutput, calls=%fused_computation.7 | convolution fusion | flops 5558566912 | bytes 12812288 | tf_op jit(solution)/shard_map/dot_general | solution.py:27
  615.6 20.2 %convolution_convert_fusion = bf16[1024,2560]{1,0:T(8,128)(2,1)} fusion(bf16[1024,2560]{1,0:T(8,128)(2,1)} %bitcast.77, bf16[2560,2560]{1,0:T(8,128)(2,1)} %all-gather.2.cloned.1.call-done), kind=kOutput, calls=%fused_computation.8 | convolution fusion | flops 13424394240 | bytes 23592960 | tf_op jit(solution)/shard_map/dot_general | solution.py:27
  (161 shorter events, 88.8 us)
Async XLA Ops:
  7.2 19.0 %copy-start = (bf16[10,64,2560]{2,1,0:T(8,128)(2,1)S(1)}, bf16[10,64,2560]{2,1,0:T(8,128)(2,1)}, u32[]{:S(2)}) copy-start(bf16[10,64,2560]{2,1,0:T(8,128)(2,1)} %param.19) | copy-start | bytes 9830404
  7.2 608.4 %all-gather.2.cloned.1.call-start = ((), (), s32[]{:S(2)}) async-start(), calls=%async_computation | async-start | bytes 13516800 | tf_op jit(solution)/shard_map/all_gather | solution.py:409
  7.3 7.9 %copy-start.28 = (f32[16]{0:T(128)}, f32[16]{0:T(128)S(1)}, u32[]{:S(2)}) copy-start(f32[16]{0:T(128)S(1)} %negate_power_fusion) | copy-start | bytes 196
  7.4 9.0 %slice-start.3 = ((s8[5242880]{0:T(1024)(128)(4,1)}), s8[4194304]{0:T(1024)(128)(4,1)S(1)}, s32[]{:S(2)}) async-start(s8[5242880]{0:T(1024)(128)(4,1)} %bitcast.96), calls=%async_computation.4 | async-start | bytes 8388608
  8.6 7.8 %slice-start.4 = ((s8[5242880]{0:T(1024)(128)(4,1)}), s8[1048576]{0:T(1024)(128)(4,1)S(1)}, s32[]{:S(2)}) async-start(s8[5242880]{0:T(1024)(128)(4,1)} %bitcast.96), calls=%async_computation.5 | async-start | bytes 2097152
  8.7 7.8 %copy-start.31 = (bf16[2560,768]{1,0:T(8,128)(2,1)S(1)}, bf16[2560,768]{1,0:T(8,128)(2,1)}, u32[]{:S(2)}) copy-start(bf16[2560,768]{1,0:T(8,128)(2,1)} %param.12) | copy-start | bytes 11796484
  16.4 6.0 copy-start.30
  26.2 9.6 %copy-start.32 = (bf16[256]{0:T(256)(128)(2,1)S(1)}, bf16[256]{0:T(256)(128)(2,1)}, u32[]{:S(2)}) copy-start(bf16[256]{0:T(256)(128)(2,1)} %param.15) | copy-start | bytes 1540
  39.3 37.5 %slice-start.1 = ((bf16[768,10,96]{0,2,1:T(8,128)(2,1)}), bf16[768,10,32]{0,2,1:T(8,128)(2,1)S(1)}, s32[]{:S(2)}) async-start(bf16[768,10,96]{0,2,1:T(8,128)(2,1)} %param.16), calls=%async_computation.2 | async-start | bytes 983040 | tf_op jit(solution)/shard_map/slice | solution.py:414
  39.3 37.5 %slice-start.2 = ((bf16[768,10,96]{0,2,1:T(8,128)(2,1)}), bf16[768,10,64]{0,2,1:T(8,128)(2,1)S(1)}, s32[]{:S(2)}) async-start(bf16[768,10,96]{0,2,1:T(8,128)(2,1)} %param.16), calls=%async_computation.3 | async-start | bytes 1966080 | tf_op jit(solution)/shard_map/slice | solution.py:414
  77.2 5.8 copy-start.16
  79.3 3.8 copy-start.6
  132.6 272.1 %collective-permute-start.4 = (bf16[2,256,640]{2,1,0:T(8,128)(2,1)}, bf16[2,256,640]{2,1,0:T(8,128)(2,1)}, u32[]{:S(2)}, u32[]{:S(2)}) collective-permute-start(bf16[2,256,640]{2,1,0:T(8,128)(2,1)} %get-tuple-element.25), channel_id=1, source_target_pairs={{0,16},{8,24},{16,0},{24,8},{1,17},{9,25},{17,1},{25,9},{2,18},{10... | collective-permute-start | bytes 1966088 | tf_op jit(solution)/shard_map/ppermute | solution.py:369
  135.2 348.7 %collective-permute-start.5 = (bf16[2,256,640]{2,1,0:T(8,128)(2,1)}, bf16[2,256,640]{2,1,0:T(8,128)(2,1)}, u32[]{:S(2)}, u32[]{:S(2)}) collective-permute-start(bf16[2,256,640]{2,1,0:T(8,128)(2,1)} %get-tuple-element.25), channel_id=1, source_target_pairs={{0,24},{8,0},{16,8},{24,16},{1,25},{9,1},{17,9},{25,17},{2,26},{10... | collective-permute-start | bytes 1966088 | tf_op jit(solution)/shard_map/ppermute | solution.py:369
  138.6 49.2 %copy-start.13 = (bf16[8,2,256,288]{3,2,1,0:T(8,128)(2,1)S(1)}, bf16[8,2,256,288]{3,2,1,0:T(8,128)(2,1)}, u32[]{:S(2)}) copy-start(bf16[8,2,256,288]{3,2,1,0:T(8,128)(2,1)} %get-tuple-element.30) | copy-start | bytes 7077892
  256.9 132.1 %collective-permute-start.8 = (bf16[256,1056]{0,1:T(8,128)(2,1)}, bf16[256,1056]{0,1:T(8,128)(2,1)}, u32[]{:S(2)}, u32[]{:S(2)}) collective-permute-start(bf16[256,1056]{0,1:T(8,128)(2,1)} %get-tuple-element.65), channel_id=1, source_target_pairs={{0,24},{8,0},{16,8},{24,16},{1,25},{9,1},{17,9},{25,17},{2,26},{10... | collective-permute-start | bytes 1622024 | tf_op jit(solution)/shard_map/ppermute | solution.py:369
  256.9 134.6 %collective-permute-start.7 = (bf16[256,1056]{0,1:T(8,128)(2,1)}, bf16[256,1056]{0,1:T(8,128)(2,1)}, u32[]{:S(2)}, u32[]{:S(2)}) collective-permute-start(bf16[256,1056]{0,1:T(8,128)(2,1)} %get-tuple-element.66), channel_id=1, source_target_pairs={{0,16},{8,24},{16,0},{24,8},{1,17},{9,25},{17,1},{25,9},{2,18},{10... | collective-permute-start | bytes 1622024 | tf_op jit(solution)/shard_map/ppermute | solution.py:369
  258.2 137.8 %collective-permute-start.6 = (bf16[256,1056]{0,1:T(8,128)(2,1)}, bf16[256,1056]{0,1:T(8,128)(2,1)}, u32[]{:S(2)}, u32[]{:S(2)}) collective-permute-start(bf16[256,1056]{0,1:T(8,128)(2,1)} %get-tuple-element.64), channel_id=1, source_target_pairs={{0,8},{8,16},{16,24},{24,0},{1,9},{9,17},{17,25},{25,1},{2,10},{10... | collective-permute-start | bytes 1622024 | tf_op jit(solution)/shard_map/ppermute | solution.py:369
  360.4 5.1 slice-start
  365.5 4.5 copy-start.9
  389.0 95.6 %collective-permute-start.3 = (bf16[2,256,640]{2,1,0:T(8,128)(2,1)}, bf16[2,256,640]{2,1,0:T(8,128)(2,1)}, u32[]{:S(2)}, u32[]{:S(2)}) collective-permute-start(bf16[2,256,640]{2,1,0:T(8,128)(2,1)} %get-tuple-element.25), channel_id=1, source_target_pairs={{0,8},{8,16},{16,24},{24,0},{1,9},{9,17},{17,25},{25,1},{2,10},{10... | collective-permute-start | bytes 1966088 | tf_op jit(solution)/shard_map/ppermute | solution.py:369
  391.4 96.9 %collective-permute-start.1 = (bf16[2,256,640]{2,1,0:T(8,128)(2,1)S(1)}, bf16[2,256,640]{2,1,0:T(8,128)(2,1)}, u32[]{:S(2)}, u32[]{:S(2)}) collective-permute-start(bf16[2,256,640]{2,1,0:T(8,128)(2,1)S(1)} %get-tuple-element.24), channel_id=1, source_target_pairs={{0,16},{8,24},{16,0},{24,8},{1,17},{9,25},{17,1},{25,9},{2,18},{10... | collective-permute-start | bytes 1966088 | tf_op jit(solution)/shard_map/ppermute | solution.py:369
  396.0 6.8 %copy-start.27 = (f32[256]{0:T(256)S(1)}, f32[256]{0:T(256)}, u32[]{:S(2)}) copy-start(f32[256]{0:T(256)} %copy-done.26) | copy-start | bytes 3076
  396.0 93.0 %collective-permute-start.2 = (bf16[2,256,640]{2,1,0:T(8,128)(2,1)S(1)}, bf16[2,256,640]{2,1,0:T(8,128)(2,1)}, u32[]{:S(2)}, u32[]{:S(2)}) collective-permute-start(bf16[2,256,640]{2,1,0:T(8,128)(2,1)S(1)} %get-tuple-element.24), channel_id=1, source_target_pairs={{0,24},{8,0},{16,8},{24,16},{1,25},{9,1},{17,9},{25,17},{2,26},{10... | collective-permute-start | bytes 1966088 | tf_op jit(solution)/shard_map/ppermute | solution.py:369
  400.1 4.0 copy-start.25
  400.1 4.1 copy-start.29
  404.7 84.2 %collective-permute-start = (bf16[2,256,640]{2,1,0:T(8,128)(2,1)S(1)}, bf16[2,256,640]{2,1,0:T(8,128)(2,1)}, u32[]{:S(2)}, u32[]{:S(2)}) collective-permute-start(bf16[2,256,640]{2,1,0:T(8,128)(2,1)S(1)} %get-tuple-element.24), channel_id=1, source_target_pairs={{0,8},{8,16},{16,24},{24,0},{1,9},{9,17},{17,25},{25,1},{2,10},{10... | collective-permute-start | bytes 1966088 | tf_op jit(solution)/shard_map/ppermute | solution.py:369
  483.9 31.5 %collective-permute-start.10 = (bf16[256,1056]{0,1:T(8,128)(2,1)}, bf16[256,1056]{0,1:T(8,128)(2,1)}, u32[]{:S(2)}, u32[]{:S(2)}) collective-permute-start(bf16[256,1056]{0,1:T(8,128)(2,1)} %copy.152), channel_id=1, source_target_pairs={{0,16},{8,24},{16,0},{24,8},{1,17},{9,25},{17,1},{25,9},{2,18},{10... | collective-permute-start | bytes 1622024 | tf_op jit(solution)/shard_map/ppermute | solution.py:369
  484.7 36.8 %collective-permute-start.11 = (bf16[256,1056]{0,1:T(8,128)(2,1)}, bf16[256,1056]{0,1:T(8,128)(2,1)}, u32[]{:S(2)}, u32[]{:S(2)}) collective-permute-start(bf16[256,1056]{0,1:T(8,128)(2,1)} %copy.152), channel_id=1, source_target_pairs={{0,24},{8,0},{16,8},{24,16},{1,25},{9,1},{17,9},{25,17},{2,26},{10... | collective-permute-start | bytes 1622024 | tf_op jit(solution)/shard_map/ppermute | solution.py:369
  488.4 34.5 %collective-permute-start.9 = (bf16[256,1056]{0,1:T(8,128)(2,1)}, bf16[256,1056]{0,1:T(8,128)(2,1)}, u32[]{:S(2)}, u32[]{:S(2)}) collective-permute-start(bf16[256,1056]{0,1:T(8,128)(2,1)} %copy.152), channel_id=1, source_target_pairs={{0,8},{8,16},{16,24},{24,0},{1,9},{9,17},{17,25},{25,1},{2,10},{10... | collective-permute-start | bytes 1622024 | tf_op jit(solution)/shard_map/ppermute | solution.py:369
  599.6 5.2 copy-start.15
  615.6 20.2 %copy-start.1 = (bf16[10,64,2560]{2,1,0:T(8,128)(2,1)S(1)}, bf16[10,64,2560]{2,1,0:T(8,128)(2,1)}, u32[]{:S(2)}) copy-start(bf16[10,64,2560]{2,1,0:T(8,128)(2,1)} %param.19) | copy-start | bytes 9830404
  (19 other events, 35.6 us)
Sparse Core Ops, SparseCore 0:
  136.7 133.0 all-gather.1

commit v2 on v1

--- a/solution.py
+++ b/solution.py
@@ -7,6 +7,7 @@
 from jax.experimental import pallas as pl
 from jax.experimental.pallas import tpu as pltpu
 from jax.sharding import PartitionSpec as P
+
 
 EPS = 1e-6
 THETA = 10000.0
@@ -17,9 +18,9 @@
 TN = (((0,), (0,)), ((), ()))
 NN = (((1,), (0,)), ((), ()))
 HB, QB, CH, SEQ = 128, 256, 512, 2048
-HD, KD, LAT, QL = 64, 160, 288, 768
+HD, KD, RD, QL = 64, 160, 32, 768
 NBLK, NCP, NTP, NPAIR = 16, 8, 4, 5
-TOK, DM, HV, QW, ALL = 1024, 2560, 640, 1280, 1056
+TOK, DM, HV, QW, ALL, DWW = 1024, 2560, 640, 1280, 1056, 1152
 RH = 16
 
 
@@ -33,8 +34,10 @@
     return NBLK - 1 - blk, slice(HB, QB)
 
 
-def attn_kernel(r_ref, q_ref, do_ref, wk_ref, wv_ref, cos_ref, sin_ref, *rest):
-    kv_ref, o_ref, dq_ref, dw_ref, dkv_ref, ckv, ckvt, kcat, vv, s_scr, dp_scr, dk_acc, dv_acc, dckv, dkpe, qbd, dobd = rest
+def attn_kernel(b0, n_batch, r_ref, q_ref, do_ref, wk_ref, wv_ref, cos_ref, sin_ref, *rest):
+    kv_ref, kpe_ref = rest[:2]
+    rest = rest[2 if b0 == 0 else 4:]
+    o_ref, dq_ref, dw_ref, dkv_ref, dkpe_ref, ckv, ckvt, kcat, vv, s_scr, dp_scr, dk_acc, dv_acc, dckv, dkpe, qbd, dobd = rest
     b = pl.program_id(0)
     p = pl.program_id(1)
     n_pair = pl.num_programs(1)
@@ -47,17 +50,20 @@
         for blk in range(NBLK):
             rows = slice(blk * HB, (blk + 1) * HB)
             dev, part = owner(blk)
-            ckv[rows, :] = kv_ref[dev, 0, part, 0:QB]
-            kcat[rows, HB:KD] = kv_ref[dev, 0, part, QB:LAT]
+            ckv[rows, :] = kv_ref[dev, 0, part, :]
+            for i in range(n_batch):
+                @pl.when(b == i)
+                def _():
+                    kcat[rows, HB:KD] = kpe_ref[dev, part, (b0 + i) * RD:(b0 + i + 1) * RD]
         for i in range(4):
             ckvt[:, i * CH:(i + 1) * CH] = ckv[i * CH:(i + 1) * CH, :].T
         dckv[...] = jnp.zeros_like(dckv)
         dkpe[...] = jnp.zeros_like(dkpe)
 
-    wkv = jnp.concatenate([wk_ref[...], wv_ref[...]], axis=1)
+    wkv = jnp.concatenate([wk_ref[...], wv_ref[...]], axis=0)
     for i in range(4):
         rows = slice(i * CH, (i + 1) * CH)
-        kv = dot(ckv[rows, :], wkv, NN).astype(BF)
+        kv = dot(ckv[rows, :], wkv, NT).astype(BF)
         kcat[rows, 0:HB] = kv[:, 0:HB]
         vv[rows, :] = kv[:, HB:QB]
 
@@ -167,8 +173,9 @@
         rows = slice(i * CH, (i + 1) * CH)
         dkv = jnp.concatenate([(dk_acc[rows, 0:HB] * scale).astype(BF), dv_acc[rows, :].astype(BF)], axis=1)
         dkpe[rows, :] += dk_acc[rows, HB:KD] * scale
-        dckv[rows, :] += dot(dkv, wkv, NT)
+        dckv[rows, :] += dot(dkv, wkv, NN)
         dwt = dwt + dot(ckvt[:, rows], dkv, NN)
+    dwt = dwt.T
 
     @pl.when(b == 0)
     def _():
@@ -183,49 +190,66 @@
         for blk in range(NBLK):
             rows = slice(blk * HB, (blk + 1) * HB)
             dev, part = owner(blk)
-            dkv_ref[dev, 0, part, 0:QB] = dckv[rows, :].astype(BF)
-            dkv_ref[dev, 0, part, QB:LAT] = dkpe[rows, :].astype(BF)
-
-
-def attention(rank, q, do, wk, wv, cos_t, sin_t, kv, b0, nb):
+            dkv_ref[dev, 0, part, :] = dckv[rows, :].astype(BF)
+            for i in range(n_batch):
+                @pl.when(b == i)
+                def _():
+                    dkpe_ref[dev, part, i * RD:(i + 1) * RD] = dkpe[rows, :].astype(BF)
+
+
+def attention(rank, q, do, wk, wv, cos_t, sin_t, kv, kpe, prev, b0, nb):
     pair_blk = lambda w: pl.BlockSpec((1, QB, w), lambda b, p, *_: (b0 + b, 0, p))
     out_blk = lambda w: pl.BlockSpec((1, QB, w), lambda b, p, *_: (b, 0, p))
-    w_blk = pl.BlockSpec((QB, HB), lambda b, p, *_: (0, p))
+    w_blk = pl.BlockSpec((HB, QB), lambda b, p, *_: (p, 0))
     full = pl.BlockSpec((16, QB), lambda b, p, *_: (0, 0))
-    kv_blk = pl.BlockSpec((NCP, 1, QB, LAT), lambda b, p, *_: (0, b0 + b, 0, 0))
-    dkv_blk = pl.BlockSpec((NCP, 1, QB, LAT), lambda b, p, *_: (0, b, 0, 0))
+    kv_blk = pl.BlockSpec((NCP, 1, QB, QB), lambda b, p, *_: (0, b0 + b, 0, 0))
+    dkv_blk = kv_blk
+    anyspec = [pl.BlockSpec(memory_space=pl.ANY)] * len(prev)
     grid_spec = pltpu.PrefetchScalarGridSpec(
         num_scalar_prefetch=1,
         grid=(nb, NPAIR),
-        in_specs=[pair_blk(QB), pair_blk(HB), w_blk, w_blk, full, full, kv_blk],
-        out_specs=[out_blk(HB), out_blk(QB), pl.BlockSpec((NPAIR, QB, QB), lambda b, p, *_: (0, 0, 0)), dkv_blk],
+        in_specs=[pair_blk(QB), pair_blk(HB), w_blk, w_blk, full, full, kv_blk, pl.BlockSpec((NCP, QB, HB), lambda b, p, *_: (0, 0, 0))] + anyspec,
+        out_specs=[out_blk(HB), pair_blk(QB), pl.BlockSpec((NPAIR, QB, QB), lambda b, p, *_: (0, 0, 0)), dkv_blk,
+                   pl.BlockSpec((NCP, QB, nb * RD), lambda b, p, *_: (0, 0, 0))],
         scratch_shapes=[
             pltpu.VMEM((SEQ, QB), BF), pltpu.VMEM((QB, SEQ), BF), pltpu.VMEM((SEQ, KD), BF), pltpu.VMEM((SEQ, HB), BF),
             pltpu.VMEM((5, CH, QB), F32), pltpu.VMEM((5, CH, QB), F32),
             pltpu.VMEM((SEQ, KD), F32), pltpu.VMEM((SEQ, HB), F32),
-            pltpu.VMEM((SEQ, QB), F32), pltpu.VMEM((SEQ, 32), F32),
+            pltpu.VMEM((SEQ, QB), F32), pltpu.VMEM((SEQ, RD), F32),
             pltpu.VMEM((2, QB, KD), BF), pltpu.VMEM((2, QB, HB), BF),
         ])
     return pl.pallas_call(
-        attn_kernel,
+        functools.partial(attn_kernel, b0, nb),
         grid_spec=grid_spec,
-        out_shape=[jax.ShapeDtypeStruct((nb, QB, HV), BF), jax.ShapeDtypeStruct((nb, QB, QW), BF), jax.ShapeDtypeStruct((NPAIR, QB, QB), F32),
-                   jax.ShapeDtypeStruct((NCP, nb, QB, LAT), BF)],
+        out_shape=[jax.ShapeDtypeStruct((nb, QB, HV), BF), jax.ShapeDtypeStruct((4, QB, QW), BF), jax.ShapeDtypeStruct((NPAIR, QB, QB), F32),
+                   jax.ShapeDtypeStruct((NCP, 4, QB, QB), BF),
+                   jax.ShapeDtypeStruct((NCP, QB, nb * RD), BF)],
         compiler_params=pltpu.CompilerParams(vmem_limit_bytes=50 * 1024 * 1024),
         cost_estimate=pl.CostEstimate(flops=nb * 20_000_000_000, bytes_accessed=nb * 8_000_000, transcendentals=0),
+        input_output_aliases={9: 1, 10: 3} if prev else {},
         name="attn",
-    )(rank, q, do, wk, wv, cos_t, sin_t, kv)
-
-
-def plane_kernel(n_arr, reduce, gather, n_z, *refs):
+    )(rank, q, do, wk, wv, cos_t, sin_t, kv, kpe, *prev)
+
+
+def norm_pull(grad, vals, gain):
+    rr = lax.rsqrt(jnp.mean(vals * vals, axis=-1, keepdims=True) + EPS)
+    h = grad * gain
+    mix = jnp.mean(h * vals, axis=-1, keepdims=True) * (rr * rr * rr)
+    return rr * h - vals * mix, jnp.sum(grad * (vals * rr), axis=0, keepdims=True)
+
+
+def plane_kernel(n_arr, reduce, gather, n_z, with_lat, *refs):
     ins, refs = refs[:n_arr], refs[n_arr:]
+    if with_lat:
+        lat, cq_ref, ckv_ref, gq_ref, gkv_ref, cos_ref, sin_ref, raw, gg = refs[:9]
+        refs = refs[9:]
     outs, refs = refs[:n_arr], refs[n_arr:]
     r = lax.axis_index('cp')
     z = lax.axis_index('tp')
     send, recv, scratch = refs[0], refs[1], refs[2:]
     peers = {1: {'cp': r ^ 1}, 2: {'cp': r ^ 2}, 4: {'cp': r ^ 4}}
     barrier = pltpu.get_barrier_semaphore()
-    targets = list(peers.values()) + [{'tp': lax.rem(z + d, NTP)} for d in range(1, n_z)]
+    targets = list(peers.values()) + [{'tp': lax.rem(z + d, NTP)} for d in range(1, NTP if with_lat else n_z)]
     for t in targets:
         pl.semaphore_signal(barrier, inc=1, device_id=t, device_id_type=pl.DeviceIdType.MESH)
     pl.semaphore_wait(barrier, len(targets))
@@ -250,12 +274,13 @@
             rows = w['rd'].shape[0]
         else:
             rows = ins[i].shape[0]
-        if gather:
-            w['g'] = scratch[0]
-            scratch = scratch[1:]
+        w['g'] = outs[i]
         w['a'] = slice(0, (rows // 2 + RH - 1) // RH * RH)
         w['b'] = slice(w['a'].stop, rows)
         work.append(w)
+    if with_lat:
+        zr = scratch[0]
+        z_in = [copy(lat.at[lax.rem(z + d, NTP)], zr.at[d - 1], {'tp': lax.rem(z + d, NTP)}) for d in range(1, NTP)]
     if reduce:
         for w in work:
             w['c'] = [None] * 4
@@ -307,6 +332,22 @@
                 own = w['g'].at[z * NCP + r]
                 z_copies.append([copy(own, own, {'tp': lax.rem(z + d, NTP)}) for d in range(1, n_z)])
             flows.append([fan(w, z * NCP if n_z > 1 else 0)])
+        if with_lat:
+            for c in z_in:
+                c.wait_recv()
+            for i in range(4):
+                rows = slice(i * HD, (i + 1) * HD)
+                own = lat[z, rows, :].astype(F32)
+                for d in range(NTP - 1):
+                    own = own + zr[d, rows, :].astype(F32)
+                g_cq, part_q = norm_pull(own[:, :QL], cq_ref[rows, :].astype(F32), gq_ref[...])
+                g_ckv, part_kv = norm_pull(own[:, QL:TOK], ckv_ref[rows, :].astype(F32), gkv_ref[...])
+                p1, p2 = own[:, TOK:TOK + RH], own[:, TOK + RH:ALL]
+                cc, ss = cos_ref[rows, :], sin_ref[rows, :]
+                raw[z, rows, :] = jnp.concatenate([g_cq, g_ckv, p1 * cc + p2 * ss, p2 * cc - p1 * ss, jnp.zeros((HD, DWW - ALL), F32)], axis=1).astype(BF)
+                part = jnp.concatenate([part_q, part_kv], axis=1)
+                gg[...] = part if i == 0 else gg[...] + part
+            z_in = [copy(raw.at[z], raw.at[z], {'tp': lax.rem(z + d, NTP)}) for d in range(1, NTP)]
         for d in range(n_z):
             for i, w in enumerate(work):
                 f = flows[i][d]
@@ -332,13 +373,14 @@
                 f = flows[i][d]
                 for name in (1, 'cx', 'cy', 'cd'):
                     f[name].wait_recv()
-        for w in work:
-            w['out'][...] = w['g'][...]
+        if with_lat:
+            for c in z_in:
+                c.wait_recv()
     for c in started:
         c.wait_send()
 
 
-def plane(arrs, cid, reduce, gather, n_z=1):
+def plane(arrs, cid, reduce, gather, n_z=1, extra=()):
     scratch, shapes = [], []
     n_copy = 0
     for v in arrs:
@@ -347,31 +389,33 @@
             scratch += [pltpu.VMEM((4, n, m), BF), pltpu.VMEM((4, n, m), BF)] + [pltpu.VMEM((n, m), BF)] * 3
             n_copy += 10
         if gather:
-            scratch.append(pltpu.VMEM((NCP * n_z, n, m), BF))
             shapes.append(jax.ShapeDtypeStruct((NCP * n_z, n, m), BF))
             n_copy += 8 * n_z + n_z - 1
         else:
             shapes.append(jax.ShapeDtypeStruct((n, m), F32))
     vmem = pl.BlockSpec(memory_space=pltpu.VMEM)
+    if extra:
+        shapes = [jax.ShapeDtypeStruct((4, QB, DWW), BF), jax.ShapeDtypeStruct((1, TOK), F32)] + shapes
+        scratch.append(pltpu.VMEM((3, QB, DWW), BF))
+        n_copy += 6
     return pl.pallas_call(
-        functools.partial(plane_kernel, len(arrs), reduce, gather, n_z),
+        functools.partial(plane_kernel, len(arrs), reduce, gather, n_z, bool(extra)),
         out_shape=shapes,
-        in_specs=[vmem] * len(arrs),
-        out_specs=[vmem] * len(arrs),
+        in_specs=[vmem] * (len(arrs) + len(extra)),
+        out_specs=[vmem] * len(shapes),
         scratch_shapes=[pltpu.SemaphoreType.DMA((n_copy,)), pltpu.SemaphoreType.DMA((n_copy,))] + scratch,
         compiler_params=pltpu.CompilerParams(collective_id=cid, has_side_effects=True, vmem_limit_bytes=60 * TOK * TOK),
         cost_estimate=pl.CostEstimate(flops=30_000_000_000, bytes_accessed=10_000_000, transcendentals=0),
         name="plane",
-    )(*arrs)
+    )(*arrs, *extra)
 
 
 def zshift(v, d):
     return lax.ppermute(v, 'tp', [(i, (i + d) % NTP) for i in range(NTP)])
 
 
-def zgather(v, z):
-    rel = [v] + [zshift(v, d) for d in range(1, NTP)]
-    return [lax.select_n((z - j) % NTP, *rel) for j in range(NTP)]
+def zrel(v):
+    return [v] + [zshift(v, d) for d in range(1, NTP)]
 
 
 def norm_f32(raw_vals, gain_vec):
@@ -401,68 +445,68 @@
         pe = kv_raw[:, QB:].astype(F32).reshape(4, QB, 32)
         pe1, pe2 = pe[..., :half], pe[..., half:]
         k_pe = jnp.concatenate([pe1 * cos_tab - pe2 * sin_tab, pe2 * cos_tab + pe1 * sin_tab], axis=-1).astype(BF)
-        kv, = plane([jnp.concatenate([c_kv, k_pe.reshape(TOK, 32)], axis=-1)], 0, False, True)
-        kv = kv.reshape(NCP, 4, QB, LAT)
+        kv, kpe = plane([c_kv, k_pe.transpose(1, 0, 2).reshape(QB, HB)], 0, False, True)
+        kv = kv.reshape(NCP, 4, QB, QB)
 
         wo2 = w_o.reshape(HV, DM)
-        wo_slice, kv = lax.optimization_barrier((lax.dynamic_slice_in_dim(wo2, rank * 80, 80, 0), kv))
-        wo_all = lax.all_gather(wo_slice, ('tp', 'cp'), axis=0, tiled=True)
+        wo_rel = jnp.stack(zrel(lax.dynamic_slice_in_dim(wo2, rank * 80, 80, 0)))
+        wo_rel, kv = lax.optimization_barrier((wo_rel, kv))
+        wo_rel = lax.all_gather(wo_rel, 'cp', axis=1, tiled=True).reshape(DM, DM)
 
         cq_raw = dot(x2, w_dq, NN).astype(BF)
         cq_f32 = cq_raw.astype(F32)
         c_q = norm_f32(cq_f32, gq).astype(BF)
-        w_q = jnp.concatenate([w_uq[:, :, :HD].reshape(QL, NPAIR, HB), w_uq[:, :, HD:].reshape(QL, NPAIR, HD), jnp.zeros((QL, NPAIR, HD), BF)], axis=2).reshape(QL, QW)
-        q = dot(c_q, w_q, NN).astype(BF).reshape(4, QB, QW)
+        w_qt = w_uq.transpose(1, 2, 0)
+        w_q = jnp.concatenate([w_qt[:, :HD].reshape(NPAIR, HB, QL), w_qt[:, HD:].reshape(NPAIR, HD, QL), jnp.zeros((NPAIR, HD, QL), BF)], axis=1).reshape(QW, QL)
+        q = dot(c_q, w_q, NT).astype(BF).reshape(4, QB, QW)
         do = dot(dy2, wo2, NT).astype(BF).reshape(4, QB, HV)
-        wk = w_uk.reshape(QB, HV)
-        wv = w_uv.reshape(QB, HV)
-
-        n_split = 2
+        wk = w_uk.transpose(1, 2, 0).reshape(HV, QB)
+        wv = w_uv.transpose(1, 2, 0).reshape(HV, QB)
+
+        n_split = 4
         nb = 4 // n_split
-        runs = [attention(rank.reshape(1), q, do, wk, wv, cos_t, sin_t, kv, i * nb, nb) for i in range(n_split)]
-        o_all = [zgather(run[0], z) for run in runs]
-        o_all = jnp.concatenate([jnp.concatenate(parts, axis=2) for parts in o_all], axis=0).reshape(TOK, NTP * HV)
-        attn_out = dot(o_all, wo_all, NN).astype(BF).reshape(4, QB, DM)
+        runs = []
+        for i in range(n_split):
+            prev = [runs[-1][1], runs[-1][3]] if runs else []
+            runs.append(attention(rank.reshape(1), q, do, wk, wv, cos_t, sin_t, kv, kpe, prev, i * nb, nb))
+        o_rel = []
+        for run in runs:
+            parts = [run[0]]
+            for d in range(1, NTP):
+                parts.append(zshift(run[0], d))
+            o_rel.append(jnp.concatenate(parts, axis=2))
+        o_rel = jnp.concatenate(o_rel, axis=0).reshape(TOK, DM)
         o = jnp.concatenate([run[0] for run in runs], axis=0).reshape(TOK, HV)
-        dq = jnp.concatenate([run[1] for run in runs], axis=0).reshape(TOK, QW)
+        dq = runs[-1][1].reshape(TOK, QW)
         dwkv = sum(run[2] for run in runs)
-        dkv = jnp.concatenate([run[3] for run in runs], axis=1).reshape(NCP, TOK, LAT)
-
-        dckv, = plane([dkv], 1, True, False)
-        lat_q = dot(dq, w_q, NT)
-        lat = jnp.concatenate([lat_q, dckv], axis=-1).reshape(4, QB, ALL)
-        lat_bf = lat.astype(BF)
-        own = lax.dynamic_index_in_dim(lat, z, 0, keepdims=False)
-        for d in range(1, NTP):
-            mine = lax.dynamic_index_in_dim(lat_bf, (z + d) % NTP, 0, keepdims=False)
-            own = own + zshift(mine, d).astype(F32)
-
-        cq_own = lax.dynamic_slice_in_dim(cq_f32, z * QB, QB, 0)
-        ckv_own = lax.dynamic_slice_in_dim(ckv_f32, z * QB, QB, 0)
-        g_cq, grad_g_q = jax.vjp(norm_f32, cq_own, gq)[1](own[:, :QL])
-        g_ckv, grad_g_kv = jax.vjp(norm_f32, ckv_own, gkv)[1](own[:, QL:TOK])
-        p1, p2 = own[:, TOK:TOK + half], own[:, TOK + half:]
-        raw = jnp.concatenate([g_cq, g_ckv, p1 * cos_tab + p2 * sin_tab, p2 * cos_tab - p1 * sin_tab], axis=-1).astype(BF)
-        raw_all = jnp.concatenate(zgather(raw, z), axis=0)
-
+
+        dckv, *dkpe = plane([runs[-1][3].reshape(NCP, TOK, QB)] + [run[4] for run in runs], 1, True, False)
+        dkpe = jnp.concatenate(dkpe, axis=1).reshape(QB, 4, RD).transpose(1, 0, 2)
+        lat_q = dot(dq, w_q, NN).reshape(4, QB, QL)
+        lat = jnp.concatenate([lat_q.astype(BF), dckv.reshape(4, QB, QB).astype(BF), dkpe.astype(BF), jnp.zeros((4, QB, DWW - ALL), BF)], axis=-1)
+        cq_own = lax.dynamic_slice_in_dim(cq_raw, z * QB, QB, 0)
+        ckv_own = lax.dynamic_slice_in_dim(kv_raw, z * QB, QB, 0)[:, :QB]
+        dwq = dot(dq, c_q, TN).astype(BF).reshape(NCP, KD, QL)
+        dwkv = dwkv.reshape(NCP, KD, QB).astype(BF)
+        dwo = dot(o, dy2, TN).astype(BF).reshape(NCP, 80, DM)
+        raw, grad_g, dwq, dwkv, dwo = plane([dwq, dwkv, dwo], 3, True, True, 1, [lat, cq_own, ckv_own, gq[None], gkv[None], cos_tab, sin_tab])
+        raw_all = raw.reshape(TOK, DWW)[:, :ALL]
+
+        grad_g = jnp.pad(grad_g.reshape(HB, NCP).astype(BF), ((0, HV - HB), (0, DWW - ALL - NCP)))
         x_slice = lax.dynamic_slice_in_dim(x2, z * HV, HV, 1)
-        dwd = dot(x_slice, raw_all, TN).astype(BF).reshape(NCP, 80, ALL)
+        dwd = jnp.concatenate([dot(x_slice, raw_all, TN).astype(BF), grad_g], axis=1).reshape(NCP, 80, DWW)
         dwd, = plane([dwd], 2, True, True, NTP)
-        dwd = dwd.reshape(DM, ALL).astype(F32)
-        w_d = jnp.concatenate([w_dq, w_dkv], axis=1)
-        grad_hidden = dot(raw_all, w_d, NT).astype(BF).reshape(4, QB, DM)
-
-        dwq = dot(c_q, dq, TN).astype(BF).reshape(NCP, 96, QW)
-        dwkv = dwkv.transpose(1, 0, 2).reshape(NCP, 32, QW).astype(BF)
-        dwo = dot(o, dy2, TN).astype(BF).reshape(NCP, 80, DM)
-        dwq, dwkv, dwo = plane([dwq, dwkv, dwo], 3, True, True)
-        grad_g_q, grad_g_kv = lax.psum((grad_g_q, grad_g_kv), ('tp', 'cp'))
-        dwq = dwq.reshape(QL, NPAIR, QB).astype(F32)
-        grad_uq = jnp.concatenate([dwq[:, :, :HB].reshape(QL, 10, HD), dwq[:, :, HB:HB + HD].reshape(QL, 10, 32)], axis=-1)
-        dwkv = dwkv.reshape(QB, NPAIR, QB).astype(F32)
-        grad_uk = dwkv[:, :, :HB].reshape(QB, 10, HD)
-        grad_uv = dwkv[:, :, HB:].reshape(QB, 10, HD)
-        return (attn_out, grad_hidden, dwd[:, :QL], grad_g_q, dwd[:, QL:], grad_g_kv, grad_uq, grad_uk, grad_uv, dwo.reshape(10, HD, DM).astype(F32))
+        dwd = dwd.reshape(DM, DWW)
+        grad_g = jnp.sum(dwd.reshape(NTP, HV, DWW)[:, :HB, ALL:ALL + NCP].astype(F32), axis=0).reshape(TOK)
+        grad_hidden = (dot(raw_all[:, :QL], w_dq, NT) + dot(raw_all[:, QL:], w_dkv, NT)).astype(BF).reshape(4, QB, DM)
+        attn_out = dot(o_rel, wo_rel, NN).astype(BF).reshape(4, QB, DM)
+
+        dwq = dwq.reshape(NPAIR, QB, QL).astype(F32)
+        grad_uq = jnp.concatenate([dwq[:, :HB].reshape(10, HD, QL), dwq[:, HB:HB + HD].reshape(10, RD, QL)], axis=1).transpose(2, 0, 1)
+        dwkv = dwkv.reshape(NPAIR, QB, QB).astype(F32)
+        grad_uk = dwkv[:, :HB].reshape(10, HD, QB).transpose(2, 0, 1)
+        grad_uv = dwkv[:, HB:].reshape(10, HD, QB).transpose(2, 0, 1)
+        return (attn_out, grad_hidden, dwd[:, :QL].astype(F32), grad_g[:QL], dwd[:, QL:ALL].astype(F32), grad_g[QL:], grad_uq, grad_uk, grad_uv, dwo.reshape(HV, DM).astype(F32).reshape(10, HD, DM))
 
     seq_spec = P(None, 'cp', None)
     full_spec = P()

time: 656 us -> 573 us (0.87)
  blocking collectives: 76.6 us -> 0 us
  local copies, waits for them, and re-layouts: 88.4 us -> 43.3 us
  Pallas kernels: 304 us -> 330 us
  starting transfers between devices: 14.7 us -> 28.2 us
    psum x1 -> x0, blocking collectives: 76.6 us -> none  [per_device(): grad_g_q, grad_g_kv = lax.psum((grad_g_q, grad_g_kv), ('tp', 'cp'))]
    pallas_call x4, Pallas kernels: 207 us -> 227 us  [plane(): pl.pallas_call(functools.partial(plane_kernel, len(arrs), reduce, gather,...]
    convert_element_type x6 -> x3, local copies, waits for them, and re-layouts: 17.5 us -> 0.32 us  [the longest x1 0.17 us: per_device(): dkpe.astype(BF)]
    ppermute x12 -> x15, starting transfers between devices: 14.7 us -> 28.1 us  [zshift(): return lax.ppermute(v, 'tp', [(i, (i + d) % NTP) for i in range(NTP)])]
    reshape x4 -> x1, local copies, waits for them, and re-layouts: 11.3 us -> 0.73 us  [per_device(): k_pe.transpose(1, 0, 2).reshape(QB, HB)]
    ppermute x6 -> x0, local copies, waits for them, and re-layouts: 10.4 us -> none  [zshift(): return lax.ppermute(v, 'tp', [(i, (i + d) % NTP) for i in range(NTP)])]
    convert_element_type x4 -> x6, other arithmetic: 10.3 us -> 20.1 us  [the longest x1 6.1 us: per_device(): dwd[:, :QL].astype(F32)]
    concatenate x7 -> x5, other arithmetic: 16.4 us -> 8.9 us  [the longest x1 6.72 us: per_device(): o_rel = jnp.concatenate(o_rel, axis=0).reshape(TOK, DM)]
  transfers between devices with their start and end apart: 13 -> 16, of which waited for: 2 -> 2; matrix products, arithmetic and copies ran while one was open for 22% -> 22% of each run, Pallas kernels for 34% -> 59%
where the time goes in v2:
time: 573 us; the launch traced here: 563 us
  Pallas kernels  330 us (58%)
  matrix products  74.4 us (13%)
  local copies, waits for them, and re-layouts  43.3 us (8%)
  other arithmetic  42.5 us (7%)
  waiting for transfers between devices  30.4 us (5%)
  starting transfers between devices  28.2 us (5%)
  between operations  14.9 us (3%)
    pallas_call x4, Pallas kernels, plane(): pl.pallas_call(functools.partial(plane_kernel, len(arrs), reduce, gather,...  227 us
    pallas_call x4, Pallas kernels, attention(): pl.pallas_call(functools.partial(attn_kernel, b0, nb), grid_spec=grid_spe...  102 us
    dot_general x11, matrix products, dot(): return lax.dot_general(a, b, dims, preferred_element_type=F32)  74.4 us
    ppermute x15, waiting for transfers between devices, zshift(): return lax.ppermute(v, 'tp', [(i, (i + d) % NTP) for i in range(NTP)])  30.4 us
    ppermute x15, starting transfers between devices, zshift(): return lax.ppermute(v, 'tp', [(i, (i + d) % NTP) for i in range(NTP)])  28.1 us
    unnamed x75, local copies, waits for them, and re-layouts  18.3 us
  transfers between devices with their start and end apart: 16, of which 2 were waited for; matrix products, arithmetic and copies ran while one was open for 22% of the time, Pallas kernels for 59%

profile of v2, /device:TPU:0, one launch (start us, length us, event | category | flops | bytes accessed | tf_op | source)
XLA Modules:
  0.0 563.5 jit_solution(7874895445033665612)
XLA Ops:
  9.9 5.1 collective-permute-start.2
  20.1 5.4 convolution_convert_fusion.7
  29.0 9.0 %fusion = (f32[1024]{0:T(1024)S(1)}, bf16[1024,768]{1,0:T(8,128)(2,1)}) fusion(bf16[1024,2560]{1,0:T(8,128)(2,1)} %bitcast.125, bf16[2560,768]{1,0:T(8,128)(2,1)} %param.12), kind=kOutput, calls=%fused_computation.10 | convolution fusion | flops 4029676544 | bytes 10752000 | tf_op jit(solution)/shard_map/dot_general | solution.py:28
  38.1 7.8 %convolution_convert_fusion.6 = bf16[1024,640]{1,0:T(8,128)(2,1)} fusion(bf16[1024,2560]{1,0:T(8,128)(2,1)} %bitcast.121, bf16[640,2560]{1,0:T(8,128)(2,1)S(1)} %bitcast.79), kind=kOutput, calls=%fused_computation.21 | convolution fusion | flops 3356098560 | bytes 9830400 | tf_op jit(solution)/shard_map/dot_general | solution.py:28
  54.8 26.9 %plane.4 = (bf16[8,1024,256]{2,1,0:T(8,128)(2,1)}, bf16[8,256,128]{2,1,0:T(8,128)(2,1)}) custom-call(bf16[1024,256]{1,0:T(8,128)(2,1)} %fusion.18.refs_0_, bf16[256,128]{1,0:T(8,128)(2,1)} %copy.53.refs_1_), custom_call_target="tpu_custom_call" | custom-call | flops 30000001024 | bytes 10000000 | tf_op jit(solution)/shard_map/plane/pallas_call | solution.py:401
  85.6 3.8 convolution_convert_fusion.1
  96.6 25.6 %attn.4 = (bf16[1,256,640]{2,1,0:T(8,128)(2,1)S(1)}, bf16[4,256,1280]{2,1,0:T(8,128)(2,1)}, f32[5,256,256]{2,1,0:T(8,128)S(1)}, bf16[8,4,256,256]{3,2,1,0:T(8,128)(2,1)}, bf16[8,256,32]{2,1,0:T(8,128)(2,1)S(1)}) custom-call(s32[1]{0:T(128)} %bitcast.r_ref, bf16[4,256,1280]{2,1,0:T(8,128)(2,1)} %bitcast.134, bf16[4,256,640]{2,1,0:T(8,128)(2,1)} %bitcast.140, ...), custom_call_target="tpu_custom_call" | custom-call | flops 20000000000 | bytes 8000000 | tf_op jit(solution)/shard_map/attn/pallas_call | solution.py:221
  123.8 25.5 %attn.5 = (bf16[1,256,640]{2,1,0:T(8,128)(2,1)S(1)}, bf16[4,256,1280]{2,1,0:T(8,128)(2,1)}, f32[5,256,256]{2,1,0:T(8,128)S(1)}, bf16[8,4,256,256]{3,2,1,0:T(8,128)(2,1)}, bf16[8,256,32]{2,1,0:T(8,128)(2,1)S(1)}) custom-call(s32[1]{0:T(128)} %bitcast.r_ref, bf16[4,256,1280]{2,1,0:T(8,128)(2,1)} %bitcast.135, ...), custom_call_target="tpu_custom_call", output_to_operand_aliasing={{1}: (9, {}), {3}: (10, {})} | custom-call | flops 20000000000 | bytes 8000000 | tf_op jit(solution)/shard_map/attn/pallas_call | solution.py:221
  150.1 25.8 %attn.6 = (bf16[1,256,640]{2,1,0:T(8,128)(2,1)}, bf16[4,256,1280]{2,1,0:T(8,128)(2,1)}, f32[5,256,256]{2,1,0:T(8,128)S(1)}, bf16[8,4,256,256]{3,2,1,0:T(8,128)(2,1)}, bf16[8,256,32]{2,1,0:T(8,128)(2,1)S(1)}) custom-call(s32[1]{0:T(128)} %bitcast.r_ref, bf16[4,256,1280]{2,1,0:T(8,128)(2,1)} %bitcast.136, ...), custom_call_target="tpu_custom_call", output_to_operand_aliasing={{1}: (9, {}), {3}: (10, {})} | custom-call | flops 20000000000 | bytes 8000000 | tf_op jit(solution)/shard_map/attn/pallas_call | solution.py:221
  177.8 25.4 %attn.7 = (bf16[1,256,640]{2,1,0:T(8,128)(2,1)}, bf16[4,256,1280]{2,1,0:T(8,128)(2,1)}, f32[5,256,256]{2,1,0:T(8,128)S(1)}, bf16[8,4,256,256]{3,2,1,0:T(8,128)(2,1)}, bf16[8,256,32]{2,1,0:T(8,128)(2,1)S(1)}) custom-call(s32[1]{0:T(128)} %bitcast.r_ref, bf16[4,256,1280]{2,1,0:T(8,128)(2,1)} %bitcast.137, ...), custom_call_target="tpu_custom_call", output_to_operand_aliasing={{1}: (9, {}), {3}: (10, {})} | custom-call | flops 20000000000 | bytes 8000000 | tf_op jit(solution)/shard_map/attn/pallas_call | solution.py:221
  205.1 2.8 collective-permute-start.14
  209.0 4.0 collective-permute-start.11
  213.0 35.3 %plane.5 = (f32[1024,256]{1,0:T(8,128)}, f32[256,32]{1,0:T(8,128)}, f32[256,32]{1,0:T(8,128)}, f32[256,32]{1,0:T(8,128)}, f32[256,32]{1,0:T(8,128)}) custom-call(bf16[8,1024,256]{2,1,0:T(8,128)(2,1)} %bitcast.132, bf16[8,256,32]{2,1,0:T(8,128)(2,1)} %copy-done.17, bf16[8,256,32]{2,1,0:T(8,128)(2,1)} %copy-done.14, bf16[8,256,32]{2,1,0:T(8,128)(2,1)} %copy-done.15, ...), custom_call_target="tpu_custom_call" | custom-call | flops 30000001024 | bytes 10000000 | tf_op jit(solution)/shard_map/plane/pallas_call | solution.py:401
  253.6 5.7 %convolution_convert_fusion.4 = bf16[4,256,768]{2,1,0:T(8,128)(2,1)} fusion(bf16[4,256,1280]{2,1,0:T(8,128)(2,1)} %get-tuple-element.58, bf16[1280,768,1]{1,0,2:T(8,128)(2,1)} %bitcast.105), kind=kOutput, calls=%fused_computation.18 | convolution fusion | flops 2014052352 | bytes 6160384 | tf_op jit(solution)/shard_map/dot_general | solution.py:28
  260.0 4.4 concatenate.47.refs_3_
  264.5 3.0 add_convert_fusion.1
  267.5 3.8 convolution_convert_fusion.2
  271.3 6.1 %bitcast_convert_fusion = bf16[640,2560]{1,0:T(8,128)(2,1)} fusion(bf16[4,256,2560]{2,1,0:T(8,128)(2,1)S(1)} %bitcast.123, bf16[1,256,640]{2,1,0:T(8,128)(2,1)} %get-tuple-element.56, bf16[1,256,640]{2,1,0:T(8,128)(2,1)} %get-tuple-element.53, bf16[1,256,640]{2,1,0:T(8,128)(2,1)S(1)} %copy-done.7, bf16[1,256,640]{2,1,0:T(8,128)(2,1)S(1)} %copy-done.5), kind=kOutput, calls=%fused_computation.1 | convolution fusion | flops 3359047680 | bytes 9830400 | tf_op jit(solution)/shard_map/dot_general | solution.py:28
  277.4 101.8 %plane.6 = (bf16[4,256,1152]{2,1,0:T(8,128)(2,1)}, f32[1,1024]{1,0:T(1,128)}, bf16[8,160,768]{2,1,0:T(8,128)(2,1)}, bf16[8,160,256]{2,1,0:T(8,128)(2,1)}, bf16[8,80,2560]{2,1,0:T(8,128)(2,1)}) custom-call(bf16[8,160,768]{2,1,0:T(8,128)(2,1)} %bitcast.139, bf16[8,160,256]{2,1,0:T(8,128)(2,1)} %bitcast.113, bf16[8,80,2560]{2,1,0:T(8,128)(2,1)} %bitcast.133, ...), custom_call_target="tpu_custom_call" | custom-call | flops 30000001024 | bytes 10000000 | tf_op jit(solution)/shard_map/plane/pallas_call | solution.py:401
  380.0 4.0 convolution_convert_fusion.3
  386.4 63.4 %plane.7 = bf16[32,80,1152]{2,1,0:T(8,128)(2,1)} custom-call(bf16[8,80,1152]{2,1,0:T(8,128)(2,1)} %bitcast.109), custom_call_target="tpu_custom_call" | custom-call | flops 30000001024 | bytes 10000000 | tf_op jit(solution)/shard_map/plane/pallas_call | solution.py:401
  449.9 6.1 %slice_convert_fusion = f32[2560,768]{1,0:T(8,128)} fusion(bf16[2560,1152]{1,0:T(8,128)(2,1)} %bitcast.92), kind=kLoop, calls=%fused_computation.4 | loop fusion | flops 1966080 | bytes 11796480 | tf_op jit(solution)/shard_map/convert_element_type | solution.py:509
  456.0 4.3 fusion.5
  460.9 4.0 collective-permute-start.8
  464.8 4.6 add_convert_fusion
  478.0 2.8 collective-permute-start.4
  485.0 3.4 copy.65
  488.4 3.3 convert_element_type.138
  492.4 5.7 %convert.31 = f32[10,64,2560]{2,1,0:T(8,128)} convert(bf16[10,64,2560]{2,1,0:T(8,128)(2,1)} %bitcast.101) | non-fusion elementwise | flops 1638400 | bytes 9830400 | tf_op jit(solution)/shard_map/convert_element_type | solution.py:509
  501.7 27.8 %collective-permute-done.4 = bf16[1,256,640]{2,1,0:T(8,128)(2,1)} collective-permute-done((bf16[1,256,640]{2,1,0:T(8,128)(2,1)S(1)}, bf16[1,256,640]{2,1,0:T(8,128)(2,1)}, u32[]{:S(2)}, u32[]{:S(2)}) %collective-permute-start.4) | collective-permute-done | bytes 327712 | tf_op jit(solution)/shard_map/ppermute | solution.py:414
  529.6 6.7 %maximum_maximum_fusion = bf16[4,256,2560]{2,1,0:T(8,128)(2,1)} fusion(bf16[1,256,640]{2,1,0:T(8,128)(2,1)} %collective-permute-done.14, bf16[1,256,640]{2,1,0:T(8,128)(2,1)} %collective-permute-done.13, bf16[1,256,640]{2,1,0:T(8,128)(2,1)} %collective-permute-done.12, bf16[1,256,640]{2,1,0:T(8,128)(2,1)} %get-tuple-element.56, ...), kind=kLoop, calls=%fused_computation.3 | loop fusion | flops 83886080 | bytes 10485760 | tf_op jit(solution)/shard_map/concatenate | solution.py:478
  536.3 19.9 %convolution_convert_fusion = bf16[1024,2560]{1,0:T(8,128)(2,1)} fusion(bf16[1024,2560]{1,0:T(8,128)(2,1)} %bitcast.95, bf16[2560,2560]{1,0:T(8,128)(2,1)} %bitcast.120), kind=kOutput, calls=%fused_computation.2 | convolution fusion | flops 13424394240 | bytes 23592960 | tf_op jit(solution)/shard_map/dot_general | solution.py:28
  (154 shorter events, 65.3 us)
Async XLA Ops:
  7.2 529.1 %all-gather.2.cloned.1.call-start = ((), (), s32[]{:S(2)}) async-start(), calls=%async_computation | async-start | bytes 14745600 | tf_op jit(solution)/shard_map/all_gather | solution.py:454
  9.1 10.9 %copy-start.23 = (bf16[2560,288]{0,1:T(8,128)(2,1)S(1)}, bf16[2560,288]{0,1:T(8,128)(2,1)}, u32[]{:S(2)}) copy-start(bf16[2560,288]{0,1:T(8,128)(2,1)} %param.14) | copy-start | bytes 4423684
  9.9 81.1 %collective-permute-start.2 = (bf16[80,2560]{1,0:T(8,128)(2,1)}, bf16[80,2560]{1,0:T(8,128)(2,1)}, u32[]{:S(2)}, u32[]{:S(2)}) collective-permute-start(bf16[80,2560]{1,0:T(8,128)(2,1)} %constant_dynamic-slice_fusion.2), channel_id=1, source_target_pairs={{0,24},{8,0},{16,8},{24,16},{1,25},{9,1},{17,9},{25,17},{2,26},{10... | collective-permute-start | bytes 1228808 | tf_op jit(solution)/shard_map/ppermute | solution.py:414
  15.0 76.0 %collective-permute-start.1 = (bf16[80,2560]{1,0:T(8,128)(2,1)}, bf16[80,2560]{1,0:T(8,128)(2,1)}, u32[]{:S(2)}, u32[]{:S(2)}) collective-permute-start(bf16[80,2560]{1,0:T(8,128)(2,1)} %constant_dynamic-slice_fusion.2), channel_id=1, source_target_pairs={{0,16},{8,24},{16,0},{24,8},{1,17},{9,25},{17,1},{25,9},{2,18},{10... | collective-permute-start | bytes 1228808 | tf_op jit(solution)/shard_map/ppermute | solution.py:414
  15.0 76.0 %collective-permute-start = (bf16[80,2560]{1,0:T(8,128)(2,1)}, bf16[80,2560]{1,0:T(8,128)(2,1)}, u32[]{:S(2)}, u32[]{:S(2)}) collective-permute-start(bf16[80,2560]{1,0:T(8,128)(2,1)} %constant_dynamic-slice_fusion.2), channel_id=1, source_target_pairs={{0,8},{8,16},{16,24},{24,0},{1,9},{9,17},{17,25},{25,1},{2,10},{10... | collective-permute-start | bytes 1228808 | tf_op jit(solution)/shard_map/ppermute | solution.py:414
  20.1 8.3 %copy-start.29 = (bf16[768]{0:T(1024)(128)(2,1)S(1)}, bf16[768]{0:T(1024)(128)(2,1)}, u32[]{:S(2)}) copy-start(bf16[768]{0:T(1024)(128)(2,1)} %param.13) | copy-start | bytes 4612
  28.4 22.6 %copy-start.25 = (f32[256,16]{1,0:T(8,128)}, f32[256,16]{1,0:T(8,128)S(1)}, u32[]{:S(2)}) copy-start(f32[256,16]{1,0:T(8,128)S(1)} %get-tuple-element.84.refs_8_) | copy-start | bytes 49156
  38.1 7.8 %copy-start.32 = (bf16[256]{0:T(256)(128)(2,1)S(1)}, bf16[256]{0:T(256)(128)(2,1)}, u32[]{:S(2)}) copy-start(bf16[256]{0:T(256)(128)(2,1)} %param.15) | copy-start | bytes 1540
  38.1 7.9 %copy-start.18 = (bf16[1024,32]{1,0:T(8,128)(2,1)S(1)}, bf16[1024,32]{1,0:T(8,128)(2,1)}, u32[]{:S(2)}) copy-start(bf16[1024,32]{1,0:T(8,128)(2,1)} %slice.89) | copy-start | bytes 196612
  45.9 35.9 %copy-start.30 = (f32[256]{0:T(256)}, f32[256]{0:T(256)S(1)}, u32[]{:S(2)}) copy-start(f32[256]{0:T(256)S(1)} %convert_element_type.120) | copy-start | bytes 3076
  96.6 27.2 %copy-start.9 = (bf16[256,10,64]{0,2,1:T(8,128)(2,1)S(1)}, bf16[256,10,64]{0,2,1:T(8,128)(2,1)}, u32[]{:S(2)}) copy-start(bf16[256,10,64]{0,2,1:T(8,128)(2,1)} %param.17) | copy-start | bytes 983044
  96.6 27.2 %copy-start.11 = (bf16[256,10,64]{0,2,1:T(8,128)(2,1)S(1)}, bf16[256,10,64]{0,2,1:T(8,128)(2,1)}, u32[]{:S(2)}) copy-start(bf16[256,10,64]{0,2,1:T(8,128)(2,1)} %param.18) | copy-start | bytes 983044
  96.6 27.2 %copy-start.13 = (bf16[8,256,128]{2,1,0:T(8,128)(2,1)S(1)}, bf16[8,256,128]{2,1,0:T(8,128)(2,1)}, u32[]{:S(2)}) copy-start(bf16[8,256,128]{2,1,0:T(8,128)(2,1)} %get-tuple-element.46.rest_1_) | copy-start | bytes 1572868
  150.1 25.8 %copy-start.14 = (bf16[8,256,32]{2,1,0:T(8,128)(2,1)}, bf16[8,256,32]{2,1,0:T(8,128)(2,1)S(1)}, u32[]{:S(2)}) copy-start(bf16[8,256,32]{2,1,0:T(8,128)(2,1)S(1)} %get-tuple-element.65.refs_2_) | copy-start | bytes 393220
  205.1 255.2 %collective-permute-start.14 = (bf16[1,256,640]{2,1,0:T(8,128)(2,1)}, bf16[1,256,640]{2,1,0:T(8,128)(2,1)}, u32[]{:S(2)}, u32[]{:S(2)}) collective-permute-start(bf16[1,256,640]{2,1,0:T(8,128)(2,1)} %get-tuple-element.56), channel_id=1, source_target_pairs={{0,24},{8,0},{16,8},{24,16},{1,25},{9,1},{17,9},{25,17},{2,26},{10... | collective-permute-start | bytes 983048 | tf_op jit(solution)/shard_map/ppermute | solution.py:414
  207.9 253.0 %collective-permute-start.13 = (bf16[1,256,640]{2,1,0:T(8,128)(2,1)}, bf16[1,256,640]{2,1,0:T(8,128)(2,1)}, u32[]{:S(2)}, u32[]{:S(2)}) collective-permute-start(bf16[1,256,640]{2,1,0:T(8,128)(2,1)} %get-tuple-element.56), channel_id=1, source_target_pairs={{0,16},{8,24},{16,0},{24,8},{1,17},{9,25},{17,1},{25,9},{2,18},{10... | collective-permute-start | bytes 983048 | tf_op jit(solution)/shard_map/ppermute | solution.py:414
  209.0 264.7 %collective-permute-start.12 = (bf16[1,256,640]{2,1,0:T(8,128)(2,1)}, bf16[1,256,640]{2,1,0:T(8,128)(2,1)}, u32[]{:S(2)}, u32[]{:S(2)}) collective-permute-start(bf16[1,256,640]{2,1,0:T(8,128)(2,1)} %get-tuple-element.56), channel_id=1, source_target_pairs={{0,8},{8,16},{16,24},{24,0},{1,9},{9,17},{17,25},{25,1},{2,10},{10... | collective-permute-start | bytes 983048 | tf_op jit(solution)/shard_map/ppermute | solution.py:414
  209.0 265.2 %collective-permute-start.11 = (bf16[1,256,640]{2,1,0:T(8,128)(2,1)}, bf16[1,256,640]{2,1,0:T(8,128)(2,1)}, u32[]{:S(2)}, u32[]{:S(2)}) collective-permute-start(bf16[1,256,640]{2,1,0:T(8,128)(2,1)} %get-tuple-element.53), channel_id=1, source_target_pairs={{0,24},{8,0},{16,8},{24,16},{1,25},{9,1},{17,9},{25,17},{2,26},{10... | collective-permute-start | bytes 983048 | tf_op jit(solution)/shard_map/ppermute | solution.py:414
  213.0 263.2 %collective-permute-start.10 = (bf16[1,256,640]{2,1,0:T(8,128)(2,1)}, bf16[1,256,640]{2,1,0:T(8,128)(2,1)}, u32[]{:S(2)}, u32[]{:S(2)}) collective-permute-start(bf16[1,256,640]{2,1,0:T(8,128)(2,1)} %get-tuple-element.53), channel_id=1, source_target_pairs={{0,16},{8,24},{16,0},{24,8},{1,17},{9,25},{17,1},{25,9},{2,18},{10... | collective-permute-start | bytes 983048 | tf_op jit(solution)/shard_map/ppermute | solution.py:414
  264.5 6.8 %slice-start = ((s8[5242880]{0:T(1024)(128)(4,1)}), s8[4194304]{0:T(1024)(128)(4,1)S(1)}, s32[]{:S(2)}) async-start(s8[5242880]{0:T(1024)(128)(4,1)} %bitcast.122), calls=%async_computation.1 | async-start | bytes 8388608
  449.8 6.1 %copy-start.26 = (bf16[4,256,1152]{2,1,0:T(8,128)(2,1)S(1)}, bf16[4,256,1152]{2,1,0:T(8,128)(2,1)}, u32[]{:S(2)}) copy-start(bf16[4,256,1152]{2,1,0:T(8,128)(2,1)} %get-tuple-element.73) | copy-start | bytes 7077892
  449.8 6.1 %copy-start.31 = (bf16[2560,768]{1,0:T(8,128)(2,1)S(1)}, bf16[2560,768]{1,0:T(8,128)(2,1)}, u32[]{:S(2)}) copy-start(bf16[2560,768]{1,0:T(8,128)(2,1)} %param.12) | copy-start | bytes 11796484
  456.0 8.9 %copy-start.24 = (bf16[2560,288]{0,1:T(8,128)(2,1)S(1)}, bf16[2560,288]{0,1:T(8,128)(2,1)}, u32[]{:S(2)}) copy-start(bf16[2560,288]{0,1:T(8,128)(2,1)} %param.14) | copy-start | bytes 4423684
  460.2 17.8 %collective-permute-start.9 = (bf16[1,256,640]{2,1,0:T(8,128)(2,1)}, bf16[1,256,640]{2,1,0:T(8,128)(2,1)S(1)}, u32[]{:S(2)}, u32[]{:S(2)}) collective-permute-start(bf16[1,256,640]{2,1,0:T(8,128)(2,1)} %get-tuple-element.53), channel_id=1, source_target_pairs={{0,8},{8,16},{16,24},{24,0},{1,9},{9,17},{17,25},{25,1},{2,10},{10... | collective-permute-start | bytes 983048 | tf_op jit(solution)/shard_map/ppermute | solution.py:414
  460.9 20.0 %collective-permute-start.8 = (bf16[1,256,640]{2,1,0:T(8,128)(2,1)S(1)}, bf16[1,256,640]{2,1,0:T(8,128)(2,1)S(1)}, u32[]{:S(2)}, u32[]{:S(2)}) collective-permute-start(bf16[1,256,640]{2,1,0:T(8,128)(2,1)S(1)} %copy-done.7), channel_id=1, source_target_pairs={{0,24},{8,0},{16,8},{24,16},{1,25},{9,1},{17,9},{25,17},{2,26},{10... | collective-permute-start | bytes 983048 | tf_op jit(solution)/shard_map/ppermute | solution.py:414
  473.7 28.0 %collective-permute-start.7 = (bf16[1,256,640]{2,1,0:T(8,128)(2,1)S(1)}, bf16[1,256,640]{2,1,0:T(8,128)(2,1)}, u32[]{:S(2)}, u32[]{:S(2)}) collective-permute-start(bf16[1,256,640]{2,1,0:T(8,128)(2,1)S(1)} %copy-done.7), channel_id=1, source_target_pairs={{0,16},{8,24},{16,0},{24,8},{1,17},{9,25},{17,1},{25,9},{2,18},{10... | collective-permute-start | bytes 983048 | tf_op jit(solution)/shard_map/ppermute | solution.py:414
  474.2 27.5 %collective-permute-start.6 = (bf16[1,256,640]{2,1,0:T(8,128)(2,1)S(1)}, bf16[1,256,640]{2,1,0:T(8,128)(2,1)}, u32[]{:S(2)}, u32[]{:S(2)}) collective-permute-start(bf16[1,256,640]{2,1,0:T(8,128)(2,1)S(1)} %copy-done.7), channel_id=1, source_target_pairs={{0,8},{8,16},{16,24},{24,0},{1,9},{9,17},{17,25},{25,1},{2,10},{10... | collective-permute-start | bytes 983048 | tf_op jit(solution)/shard_map/ppermute | solution.py:414
  476.2 25.5 %collective-permute-start.5 = (bf16[1,256,640]{2,1,0:T(8,128)(2,1)S(1)}, bf16[1,256,640]{2,1,0:T(8,128)(2,1)}, u32[]{:S(2)}, u32[]{:S(2)}) collective-permute-start(bf16[1,256,640]{2,1,0:T(8,128)(2,1)S(1)} %copy-done.5), channel_id=1, source_target_pairs={{0,24},{8,0},{16,8},{24,16},{1,25},{9,1},{17,9},{25,17},{2,26},{10... | collective-permute-start | bytes 983048 | tf_op jit(solution)/shard_map/ppermute | solution.py:414
  478.0 51.5 %collective-permute-start.4 = (bf16[1,256,640]{2,1,0:T(8,128)(2,1)S(1)}, bf16[1,256,640]{2,1,0:T(8,128)(2,1)}, u32[]{:S(2)}, u32[]{:S(2)}) collective-permute-start(bf16[1,256,640]{2,1,0:T(8,128)(2,1)S(1)} %copy-done.5), channel_id=1, source_target_pairs={{0,16},{8,24},{16,0},{24,8},{1,17},{9,25},{17,1},{25,9},{2,18},{10... | collective-permute-start | bytes 983048 | tf_op jit(solution)/shard_map/ppermute | solution.py:414
  480.9 48.7 %collective-permute-start.3 = (bf16[1,256,640]{2,1,0:T(8,128)(2,1)S(1)}, bf16[1,256,640]{2,1,0:T(8,128)(2,1)}, u32[]{:S(2)}, u32[]{:S(2)}) collective-permute-start(bf16[1,256,640]{2,1,0:T(8,128)(2,1)S(1)} %copy-done.5), channel_id=1, source_target_pairs={{0,8},{8,16},{16,24},{24,0},{1,9},{9,17},{17,25},{25,1},{2,10},{10... | collective-permute-start | bytes 983048 | tf_op jit(solution)/shard_map/ppermute | solution.py:414
  492.4 5.7 %copy-start.21 = (bf16[8,160,256]{2,1,0:T(8,128)(2,1)S(1)}, bf16[8,160,256]{2,1,0:T(8,128)(2,1)}, u32[]{:S(2)}) copy-start(bf16[8,160,256]{2,1,0:T(8,128)(2,1)} %get-tuple-element.76) | copy-start | bytes 1966084
  536.3 19.9 %copy-start.1 = (bf16[10,64,2560]{2,1,0:T(8,128)(2,1)S(1)}, bf16[10,64,2560]{2,1,0:T(8,128)(2,1)}, u32[]{:S(2)}) copy-start(bf16[10,64,2560]{2,1,0:T(8,128)(2,1)} %param.19) | copy-start | bytes 9830404
  (20 other events, 37.1 us)
Sparse Core Ops, SparseCore 0:
  93.8 73.7 all-gather.1

commit v3 on v2

--- a/solution.py
+++ b/solution.py
@@ -22,6 +22,7 @@
 NBLK, NCP, NTP, NPAIR = 16, 8, 4, 5
 TOK, DM, HV, QW, ALL, DWW = 1024, 2560, 640, 1280, 1056, 1152
 RH = 16
+HOPS = range(1, NTP)
 
 
 def dot(a, b, dims):
@@ -34,9 +35,11 @@
     return NBLK - 1 - blk, slice(HB, QB)
 
 
-def attn_kernel(b0, n_batch, r_ref, q_ref, do_ref, wk_ref, wv_ref, cos_ref, sin_ref, *rest):
+def attn_kernel(b0, r_ref, q_ref, do_ref, wk_ref, wv_ref, cos_ref, sin_ref, *rest):
     kv_ref, kpe_ref = rest[:2]
-    rest = rest[2 if b0 == 0 else 4:]
+    if b0 > 0:
+        old_ref = rest[2]
+    rest = rest[2 if b0 == 0 else 5:]
     o_ref, dq_ref, dw_ref, dkv_ref, dkpe_ref, ckv, ckvt, kcat, vv, s_scr, dp_scr, dk_acc, dv_acc, dckv, dkpe, qbd, dobd = rest
     b = pl.program_id(0)
     p = pl.program_id(1)
@@ -51,10 +54,7 @@
             rows = slice(blk * HB, (blk + 1) * HB)
             dev, part = owner(blk)
             ckv[rows, :] = kv_ref[dev, 0, part, :]
-            for i in range(n_batch):
-                @pl.when(b == i)
-                def _():
-                    kcat[rows, HB:KD] = kpe_ref[dev, part, (b0 + i) * RD:(b0 + i + 1) * RD]
+            kcat[rows, HB:KD] = kpe_ref[dev, part, b0 * RD:(b0 + 1) * RD]
         for i in range(4):
             ckvt[:, i * CH:(i + 1) * CH] = ckv[i * CH:(i + 1) * CH, :].T
         dckv[...] = jnp.zeros_like(dckv)
@@ -191,10 +191,10 @@
             rows = slice(blk * HB, (blk + 1) * HB)
             dev, part = owner(blk)
             dkv_ref[dev, 0, part, :] = dckv[rows, :].astype(BF)
-            for i in range(n_batch):
-                @pl.when(b == i)
-                def _():
-                    dkpe_ref[dev, part, i * RD:(i + 1) * RD] = dkpe[rows, :].astype(BF)
+            piece = dkpe[rows, :].astype(BF)
+            if b0 > 0:
+                dkpe_ref[dev, part, :] = old_ref[dev, part, :]
+            dkpe_ref[dev, part, b0 * RD:(b0 + 1) * RD] = piece
 
 
 def attention(rank, q, do, wk, wv, cos_t, sin_t, kv, kpe, prev, b0, nb):
@@ -204,13 +204,14 @@
     full = pl.BlockSpec((16, QB), lambda b, p, *_: (0, 0))
     kv_blk = pl.BlockSpec((NCP, 1, QB, QB), lambda b, p, *_: (0, b0 + b, 0, 0))
     dkv_blk = kv_blk
-    anyspec = [pl.BlockSpec(memory_space=pl.ANY)] * len(prev)
+    pe_blk = pl.BlockSpec((NCP, QB, HB), lambda b, p, *_: (0, 0, 0))
+    anyspec = [pe_blk] + [pl.BlockSpec(memory_space=pl.ANY)] * 2 if prev else []
     grid_spec = pltpu.PrefetchScalarGridSpec(
         num_scalar_prefetch=1,
         grid=(nb, NPAIR),
-        in_specs=[pair_blk(QB), pair_blk(HB), w_blk, w_blk, full, full, kv_blk, pl.BlockSpec((NCP, QB, HB), lambda b, p, *_: (0, 0, 0))] + anyspec,
+        in_specs=[pair_blk(QB), pair_blk(HB), w_blk, w_blk, full, full, kv_blk, pe_blk] + anyspec,
         out_specs=[out_blk(HB), pair_blk(QB), pl.BlockSpec((NPAIR, QB, QB), lambda b, p, *_: (0, 0, 0)), dkv_blk,
-                   pl.BlockSpec((NCP, QB, nb * RD), lambda b, p, *_: (0, 0, 0))],
+                   pe_blk],
         scratch_shapes=[
             pltpu.VMEM((SEQ, QB), BF), pltpu.VMEM((QB, SEQ), BF), pltpu.VMEM((SEQ, KD), BF), pltpu.VMEM((SEQ, HB), BF),
             pltpu.VMEM((5, CH, QB), F32), pltpu.VMEM((5, CH, QB), F32),
@@ -219,14 +220,14 @@
             pltpu.VMEM((2, QB, KD), BF), pltpu.VMEM((2, QB, HB), BF),
         ])
     return pl.pallas_call(
-        functools.partial(attn_kernel, b0, nb),
+        functools.partial(attn_kernel, b0),
         grid_spec=grid_spec,
         out_shape=[jax.ShapeDtypeStruct((nb, QB, HV), BF), jax.ShapeDtypeStruct((4, QB, QW), BF), jax.ShapeDtypeStruct((NPAIR, QB, QB), F32),
                    jax.ShapeDtypeStruct((NCP, 4, QB, QB), BF),
-                   jax.ShapeDtypeStruct((NCP, QB, nb * RD), BF)],
-        compiler_params=pltpu.CompilerParams(vmem_limit_bytes=50 * 1024 * 1024),
+                   jax.ShapeDtypeStruct((NCP, QB, HB), BF)],
+        compiler_params=pltpu.CompilerParams(vmem_limit_bytes=50 * TOK * TOK),
         cost_estimate=pl.CostEstimate(flops=nb * 20_000_000_000, bytes_accessed=nb * 8_000_000, transcendentals=0),
-        input_output_aliases={9: 1, 10: 3} if prev else {},
+        input_output_aliases={10: 1, 11: 3} if prev else {},
         name="attn",
     )(rank, q, do, wk, wv, cos_t, sin_t, kv, kpe, *prev)
 
@@ -238,16 +239,72 @@
     return rr * h - vals * mix, jnp.sum(grad * (vals * rr), axis=0, keepdims=True)
 
 
-def plane_kernel(n_arr, reduce, gather, n_z, with_lat, *refs):
+class Filler:
+    def __init__(self, filler, refs):
+        n_in, n_out, n_extra = len(filler.args), len(filler.outs), len(filler.extra)
+        src, self.outs, refs = refs[:n_in], refs[n_in:n_in + n_out], refs[n_in + n_out:]
+        self.bufs, sems, extra = refs[:n_in], refs[n_in], refs[n_in + 1:n_in + 1 + n_extra]
+        self.loads = [pltpu.make_async_copy(a, b, sems.at[i]) for i, (a, b) in enumerate(zip(src, self.bufs))]
+        for c in self.loads:
+            c.start()
+        self.ready = [False] * n_in
+        self.groups = [list(g) for g in filler.groups(self, self.bufs, self.outs, extra)]
+
+    def need(self, which):
+        for i in which:
+            if not self.ready[i]:
+                self.ready[i] = True
+                self.loads[i].wait()
+
+    def run(self, k):
+        while k > 0 and self.groups:
+            which, prep, body, lo, hi = self.groups[0]
+            self.need(which)
+            if prep is not None:
+                prep()
+            n = min(k, hi - lo)
+
+            def step(t, carry):
+                body(t)
+                return carry
+
+            lax.fori_loop(lo, lo + n, step, 0)
+            k -= n
+            if lo + n == hi:
+                self.groups.pop(0)
+            else:
+                self.groups[0] = [which, None, body, lo + n, hi]
+
+
+class NoFill:
+    def run(self, k):
+        return None
+
+
+class Spec:
+    def __init__(self, args, outs, extra, groups):
+        self.args, self.outs, self.extra, self.groups = args, outs, extra, groups
+
+
+def tile(t, n):
+    return pl.ds(pl.multiple_of(t * n, n), n)
+
+
+def plane_kernel(n_arr, reduce, gather, n_z, with_lat, filler, *refs):
     ins, refs = refs[:n_arr], refs[n_arr:]
+    n_fill = len(filler.args) if filler else 0
     if with_lat:
-        lat, cq_ref, ckv_ref, gq_ref, gkv_ref, cos_ref, sin_ref, raw, gg = refs[:9]
-        refs = refs[9:]
+        lat, cq_ref, ckv_ref, gq_ref, gkv_ref, cos_ref, sin_ref = refs[:7]
+        refs = refs[7:]
+    fill_src, refs = refs[:n_fill], refs[n_fill:]
+    if with_lat:
+        (raw, gg), refs = refs[:2], refs[2:]
     outs, refs = refs[:n_arr], refs[n_arr:]
+    fill_out, refs = (refs[:len(filler.outs)], refs[len(filler.outs):]) if filler else ((), refs)
     r = lax.axis_index('cp')
     z = lax.axis_index('tp')
     send, recv, scratch = refs[0], refs[1], refs[2:]
-    peers = {1: {'cp': r ^ 1}, 2: {'cp': r ^ 2}, 4: {'cp': r ^ 4}}
+    peers = {m: {'cp': r ^ m} for m in (1, 2, 4)}
     barrier = pltpu.get_barrier_semaphore()
     targets = list(peers.values()) + [{'tp': lax.rem(z + d, NTP)} for d in range(1, NTP if with_lat else n_z)]
     for t in targets:
@@ -255,6 +312,8 @@
     pl.semaphore_wait(barrier, len(targets))
     count = [0]
     started = []
+    n_tail = (len(filler.args) + 1 + len(filler.extra)) if filler else 0
+    fill = Filler(filler, list(fill_src) + list(fill_out) + list(scratch[len(scratch) - n_tail:])) if filler else NoFill()
 
     def copy(src, dst, target):
         k = count[0]
@@ -280,7 +339,7 @@
         work.append(w)
     if with_lat:
         zr = scratch[0]
-        z_in = [copy(lat.at[lax.rem(z + d, NTP)], zr.at[d - 1], {'tp': lax.rem(z + d, NTP)}) for d in range(1, NTP)]
+        z_in = [copy(lat.at[lax.rem(z + d, NTP)], zr.at[d - 1], {'tp': lax.rem(z + d, NTP)}) for d in HOPS]
     if reduce:
         for w in work:
             w['c'] = [None] * 4
@@ -288,6 +347,8 @@
             for w in work:
                 w['c'][k] = copy(w['in'].at[r ^ (2 * k + 1)], w['rc'].at[k], peers[1])
 
+        fill.run(8)
+
         def local(w, k):
             w['c'][k].wait_recv()
             return w['in'][r ^ (2 * k)].astype(F32) + w['rc'][k].astype(F32)
@@ -296,11 +357,13 @@
             w['sb'][3] = local(w, 3).astype(BF)
             w['da'] = copy(w['sb'].at[3, w['a']], w['rd'].at[w['a']], peers[2])
             w['db'] = copy(w['sb'].at[3, w['b']], w['rd'].at[w['b']], peers[4])
+        fill.run(4)
         for w in work:
             w['sb'][1] = local(w, 1).astype(BF)
             w['xa'] = copy(w['sb'].at[1, w['a']], w['rx'].at[w['a']], peers[2])
             w['sb'][2] = local(w, 2).astype(BF)
             w['yb'] = copy(w['sb'].at[2, w['b']], w['ry'].at[w['b']], peers[4])
+        fill.run(4)
         for w in work:
             w['da'].wait_recv()
             w['sb'][2, w['a']] = (w['sb'][2, w['a']].astype(F32) + w['rd'][w['a']].astype(F32)).astype(BF)
@@ -308,6 +371,7 @@
             w['db'].wait_recv()
             w['sb'][1, w['b']] = (w['sb'][1, w['b']].astype(F32) + w['rd'][w['b']].astype(F32)).astype(BF)
             w['xb'] = copy(w['sb'].at[1, w['b']], w['rx'].at[w['b']], peers[2])
+        fill.run(6)
         for w in work:
             base = local(w, 0)
             for name in ('xa', 'yb', 'ya', 'xb'):
@@ -333,6 +397,7 @@
                 z_copies.append([copy(own, own, {'tp': lax.rem(z + d, NTP)}) for d in range(1, n_z)])
             flows.append([fan(w, z * NCP if n_z > 1 else 0)])
         if with_lat:
+            fill.run(10)
             for c in z_in:
                 c.wait_recv()
             for i in range(4):
@@ -347,8 +412,9 @@
                 raw[z, rows, :] = jnp.concatenate([g_cq, g_ckv, p1 * cc + p2 * ss, p2 * cc - p1 * ss, jnp.zeros((HD, DWW - ALL), F32)], axis=1).astype(BF)
                 part = jnp.concatenate([part_q, part_kv], axis=1)
                 gg[...] = part if i == 0 else gg[...] + part
-            z_in = [copy(raw.at[z], raw.at[z], {'tp': lax.rem(z + d, NTP)}) for d in range(1, NTP)]
+            z_in = [copy(raw.at[z], raw.at[z], {'tp': lax.rem(z + d, NTP)}) for d in HOPS]
         for d in range(n_z):
+            fill.run(4)
             for i, w in enumerate(work):
                 f = flows[i][d]
                 gx, gy = w['g'].at[f['zz'] + (r ^ 2)], w['g'].at[f['zz'] + (r ^ 4)]
@@ -361,6 +427,7 @@
                 if d + 1 < n_z:
                     z_copies[i][d].wait_recv()
                     flows[i].append(fan(w, lax.rem(z + NTP - (d + 1), NTP) * NCP))
+        fill.run(3)
         for d in range(n_z):
             for i, w in enumerate(work):
                 f = flows[i][d]
@@ -368,6 +435,7 @@
                 f['dx'].wait_recv()
                 gd = w['g'].at[f['zz'] + (r ^ 6)]
                 f['cd'] = copy(gd, gd, peers[1])
+        fill.run(QB)
         for d in range(n_z):
             for i, w in enumerate(work):
                 f = flows[i][d]
@@ -376,11 +444,12 @@
         if with_lat:
             for c in z_in:
                 c.wait_recv()
+    fill.run(QB)
     for c in started:
         c.wait_send()
 
 
-def plane(arrs, cid, reduce, gather, n_z=1, extra=()):
+def plane(arrs, cid, reduce, gather, n_z=1, extra=(), filler=None):
     scratch, shapes = [], []
     n_copy = 0
     for v in arrs:
@@ -398,16 +467,103 @@
         shapes = [jax.ShapeDtypeStruct((4, QB, DWW), BF), jax.ShapeDtypeStruct((1, TOK), F32)] + shapes
         scratch.append(pltpu.VMEM((3, QB, DWW), BF))
         n_copy += 6
+    anyspec = []
+    fill_args = ()
+    if filler:
+        fill_args = filler.args
+        shapes += filler.outs
+        anyspec = [pl.BlockSpec(memory_space=pl.ANY)] * len(filler.args)
+        scratch += [pltpu.VMEM(a.shape, BF) for a in filler.args] + [pltpu.SemaphoreType.DMA((len(filler.args),))] + filler.extra
     return pl.pallas_call(
-        functools.partial(plane_kernel, len(arrs), reduce, gather, n_z, bool(extra)),
+        functools.partial(plane_kernel, len(arrs), reduce, gather, n_z, bool(extra), filler),
         out_shape=shapes,
-        in_specs=[vmem] * (len(arrs) + len(extra)),
+        in_specs=[vmem] * (len(arrs) + len(extra)) + anyspec,
         out_specs=[vmem] * len(shapes),
         scratch_shapes=[pltpu.SemaphoreType.DMA((n_copy,)), pltpu.SemaphoreType.DMA((n_copy,))] + scratch,
         compiler_params=pltpu.CompilerParams(collective_id=cid, has_side_effects=True, vmem_limit_bytes=60 * TOK * TOK),
-        cost_estimate=pl.CostEstimate(flops=30_000_000_000, bytes_accessed=10_000_000, transcendentals=0),
+        cost_estimate=pl.CostEstimate(flops=30_000_000_000, bytes_accessed=TOK * TOK, transcendentals=0),
         name="plane",
-    )(*arrs, *extra)
+    )(*arrs, *extra, *fill_args)
+
+
+def sds(*shape):
+    return jax.ShapeDtypeStruct(shape, BF)
+
+
+def front_fill(x2, w_dq, gq, dy2, wo2, w_q):
+    def groups(f, bufs, outs, extra):
+        x, wd, dy, wo, wq, gain = bufs
+        do, cq_raw, c_q, q = outs
+
+        def do_body(t):
+            do[tile(t, QB), :] = dot(dy[tile(t, QB), :], wo[...], NT).astype(BF)
+
+        def q_body(t):
+            u = dot(x[tile(t, QB), :], wd[...], NN).astype(BF)
+            cq_raw[tile(t, QB), :] = u
+            c = norm_f32(u.astype(F32), gain[...].astype(F32)).astype(BF)
+            c_q[tile(t, QB), :] = c
+            q[tile(t, QB), :] = dot(c, wq[...], NT).astype(BF)
+
+        return [((2, 3), None, do_body, 0, 4), ((0, 1, 4, 5), None, q_body, 0, 4)]
+
+    return Spec([x2, w_dq, dy2, wo2, w_q, gq[None]], [sds(TOK, HV), sds(TOK, QL), sds(TOK, QL), sds(TOK, QW)], [], groups)
+
+
+def mid_fill(dq, w_q, o, dy2, c_q):
+    def groups(f, bufs, outs, extra):
+        dqv, wq, ov, dy, cq = bufs
+        lat_q, dwo, dwq = outs
+        ot, dqt = extra
+
+        def lat_body(t):
+            lat_q[tile(t, QB), :] = dot(dqv[tile(t, QB), :], wq[...], NN).astype(BF)
+
+        def turn_o(t):
+            ot[:, tile(t, QB)] = ov[tile(t, QB), :].T
+
+        def dwo_body(t):
+            dwo[:, tile(t, QB)] = dot(ot[...], dy[:, tile(t, QB)], NN).astype(BF)
+
+        def turn_dq(t):
+            dqt[:, tile(t, QB)] = dqv[tile(t, QB), :].T
+
+        def dwq_body(t):
+            dwq[:, tile(t, QB)] = dot(dqt[...], cq[:, tile(t, QB)], NN).astype(BF)
+
+        return [((0, 1), None, lat_body, 0, 4), ((2,), None, turn_o, 0, 4), ((3,), None, dwo_body, 0, 10),
+                ((), None, turn_dq, 0, 4), ((4,), None, dwq_body, 0, 3)]
+
+    return Spec([dq, w_q, o, dy2, c_q], [sds(TOK, QL), sds(HV, DM), sds(QW, QL)], [pltpu.VMEM((HV, TOK), BF), pltpu.VMEM((QW, TOK), BF)], groups)
+
+
+def y_fill(o_rel, wo_rel):
+    def groups(f, bufs, outs, extra):
+        ov, wo = bufs
+        y, = outs
+
+        def y_body(t):
+            rows, cols = tile(lax.rem(t, 2), CH), tile(lax.div(t, 2), QB)
+            y[rows, cols] = dot(ov[rows, :], wo[:, cols], NN).astype(BF)
+
+        return [((0, 1), None, y_body, 0, 20)]
+
+    return Spec([o_rel, wo_rel], [sds(TOK, DM)], [], groups)
+
+
+def last_fill(raw, w_dq, w_dkvt):
+    def groups(f, bufs, outs, extra):
+        rawv, wd, wk = bufs
+        dx, = outs
+
+        def dx_body(t):
+            rows, cols = tile(lax.rem(t, 2), CH), tile(lax.div(t, 2), QB)
+            g = dot(rawv[rows, :QL], wd[cols, :], NT) + dot(rawv[rows, QL:ALL], wk[:, cols], NN)
+            dx[rows, cols] = g.astype(BF)
+
+        return [((0, 1, 2), None, dx_body, 0, 20)]
+
+    return Spec([raw, w_dq, w_dkvt], [sds(TOK, DM)], [], groups)
 
 
 def zshift(v, d):
@@ -415,7 +571,7 @@
 
 
 def zrel(v):
-    return [v] + [zshift(v, d) for d in range(1, NTP)]
+    return [v] + [zshift(v, d) for d in HOPS]
 
 
 def norm_f32(raw_vals, gain_vec):
@@ -430,7 +586,7 @@
         x2 = hidden.reshape(TOK, DM)
         dy2 = grad_out.reshape(TOK, DM)
         half = 16
-        inv_freq = 1.0 / (THETA ** (jnp.arange(half, dtype=F32) * 2.0 / 32))
+        inv_freq = 1.0 / (THETA ** (jnp.arange(half, dtype=F32) * 2.0 / RD))
         idx = jnp.arange(QB, dtype=jnp.int32)
         positions = jnp.where(idx < HB, rank, NBLK - 1 - rank) * HB + idx % HB
         angles = positions.astype(F32)[:, None] * inv_freq[None, :]
@@ -442,24 +598,21 @@
         kv_raw = dot(x2, w_dkv, NN).astype(BF)
         ckv_f32 = kv_raw[:, :QB].astype(F32)
         c_kv = norm_f32(ckv_f32, gkv).astype(BF)
-        pe = kv_raw[:, QB:].astype(F32).reshape(4, QB, 32)
+        pe = kv_raw[:, QB:].astype(F32).reshape(4, QB, RD)
         pe1, pe2 = pe[..., :half], pe[..., half:]
         k_pe = jnp.concatenate([pe1 * cos_tab - pe2 * sin_tab, pe2 * cos_tab + pe1 * sin_tab], axis=-1).astype(BF)
-        kv, kpe = plane([c_kv, k_pe.transpose(1, 0, 2).reshape(QB, HB)], 0, False, True)
+        wo2 = w_o.reshape(HV, DM)
+        w_qt = w_uq.transpose(1, 2, 0)
+        w_q = jnp.concatenate([w_qt[:, :HD].reshape(NPAIR, HB, QL), w_qt[:, HD:].reshape(NPAIR, HD, QL), jnp.zeros((NPAIR, HD, QL), BF)], axis=1).reshape(QW, QL)
+        kv, kpe, do, cq_raw, c_q, q = plane([c_kv, k_pe.transpose(1, 0, 2).reshape(QB, HB)], 0, False, True, filler=front_fill(x2, w_dq, g_q, dy2, wo2, w_q))
+        q = q.reshape(4, QB, QW)
+        do = do.reshape(4, QB, HV)
         kv = kv.reshape(NCP, 4, QB, QB)
 
-        wo2 = w_o.reshape(HV, DM)
         wo_rel = jnp.stack(zrel(lax.dynamic_slice_in_dim(wo2, rank * 80, 80, 0)))
         wo_rel, kv = lax.optimization_barrier((wo_rel, kv))
         wo_rel = lax.all_gather(wo_rel, 'cp', axis=1, tiled=True).reshape(DM, DM)
 
-        cq_raw = dot(x2, w_dq, NN).astype(BF)
-        cq_f32 = cq_raw.astype(F32)
-        c_q = norm_f32(cq_f32, gq).astype(BF)
-        w_qt = w_uq.transpose(1, 2, 0)
-        w_q = jnp.concatenate([w_qt[:, :HD].reshape(NPAIR, HB, QL), w_qt[:, HD:].reshape(NPAIR, HD, QL), jnp.zeros((NPAIR, HD, QL), BF)], axis=1).reshape(QW, QL)
-        q = dot(c_q, w_q, NT).astype(BF).reshape(4, QB, QW)
-        do = dot(dy2, wo2, NT).astype(BF).reshape(4, QB, HV)
         wk = w_uk.transpose(1, 2, 0).reshape(HV, QB)
         wv = w_uv.transpose(1, 2, 0).reshape(HV, QB)
 
@@ -467,12 +620,12 @@
         nb = 4 // n_split
         runs = []
         for i in range(n_split):
-            prev = [runs[-1][1], runs[-1][3]] if runs else []
+            prev = [runs[-1][4], runs[-1][1], runs[-1][3]] if runs else []
             runs.append(attention(rank.reshape(1), q, do, wk, wv, cos_t, sin_t, kv, kpe, prev, i * nb, nb))
         o_rel = []
         for run in runs:
             parts = [run[0]]
-            for d in range(1, NTP):
+            for d in HOPS:
                 parts.append(zshift(run[0], d))
             o_rel.append(jnp.concatenate(parts, axis=2))
         o_rel = jnp.concatenate(o_rel, axis=0).reshape(TOK, DM)
@@ -480,27 +633,24 @@
         dq = runs[-1][1].reshape(TOK, QW)
         dwkv = sum(run[2] for run in runs)
 
-        dckv, *dkpe = plane([runs[-1][3].reshape(NCP, TOK, QB)] + [run[4] for run in runs], 1, True, False)
-        dkpe = jnp.concatenate(dkpe, axis=1).reshape(QB, 4, RD).transpose(1, 0, 2)
-        lat_q = dot(dq, w_q, NN).reshape(4, QB, QL)
-        lat = jnp.concatenate([lat_q.astype(BF), dckv.reshape(4, QB, QB).astype(BF), dkpe.astype(BF), jnp.zeros((4, QB, DWW - ALL), BF)], axis=-1)
+        dckv, dkpe, lat_q, dwo, dwq = plane([runs[-1][3].reshape(NCP, TOK, QB), runs[-1][4]], 1, True, False, filler=mid_fill(dq, w_q, o, dy2, c_q))
+        dkpe = dkpe.reshape(QB, 4, RD).transpose(1, 0, 2)
+        lat = jnp.concatenate([lat_q.reshape(4, QB, QL), dckv.reshape(4, QB, QB).astype(BF), dkpe.astype(BF), jnp.zeros((4, QB, DWW - ALL), BF)], axis=-1)
         cq_own = lax.dynamic_slice_in_dim(cq_raw, z * QB, QB, 0)
         ckv_own = lax.dynamic_slice_in_dim(kv_raw, z * QB, QB, 0)[:, :QB]
-        dwq = dot(dq, c_q, TN).astype(BF).reshape(NCP, KD, QL)
+        dwq = dwq.reshape(NCP, KD, QL)
         dwkv = dwkv.reshape(NCP, KD, QB).astype(BF)
-        dwo = dot(o, dy2, TN).astype(BF).reshape(NCP, 80, DM)
-        raw, grad_g, dwq, dwkv, dwo = plane([dwq, dwkv, dwo], 3, True, True, 1, [lat, cq_own, ckv_own, gq[None], gkv[None], cos_tab, sin_tab])
-        raw_all = raw.reshape(TOK, DWW)[:, :ALL]
-
-        grad_g = jnp.pad(grad_g.reshape(HB, NCP).astype(BF), ((0, HV - HB), (0, DWW - ALL - NCP)))
+        dwo = dwo.reshape(NCP, 80, DM)
+        raw, grad_g, dwq, dwkv, dwo, attn_out = plane([dwq, dwkv, dwo], 3, True, True, 1, [lat, cq_own, ckv_own, gq[None], gkv[None], cos_tab, sin_tab], y_fill(o_rel, wo_rel))
+        raw_all = raw.reshape(TOK, DWW)
+
         x_slice = lax.dynamic_slice_in_dim(x2, z * HV, HV, 1)
-        dwd = jnp.concatenate([dot(x_slice, raw_all, TN).astype(BF), grad_g], axis=1).reshape(NCP, 80, DWW)
-        dwd, = plane([dwd], 2, True, True, NTP)
+        dwd = lax.dynamic_update_slice(dot(x_slice, raw_all, TN).astype(BF), grad_g.reshape(HB, NCP).astype(BF), (0, ALL)).reshape(NCP, 80, DWW)
+        dwd, grad_hidden = plane([dwd], 2, True, True, NTP, filler=last_fill(raw.reshape(TOK, DWW), w_dq, w_dkv.T))
+        grad_hidden = grad_hidden.reshape(4, QB, DM)
+        attn_out = attn_out.reshape(4, QB, DM)
         dwd = dwd.reshape(DM, DWW)
         grad_g = jnp.sum(dwd.reshape(NTP, HV, DWW)[:, :HB, ALL:ALL + NCP].astype(F32), axis=0).reshape(TOK)
-        grad_hidden = (dot(raw_all[:, :QL], w_dq, NT) + dot(raw_all[:, QL:], w_dkv, NT)).astype(BF).reshape(4, QB, DM)
-        attn_out = dot(o_rel, wo_rel, NN).astype(BF).reshape(4, QB, DM)
-
         dwq = dwq.reshape(NPAIR, QB, QL).astype(F32)
         grad_uq = jnp.concatenate([dwq[:, :HB].reshape(10, HD, QL), dwq[:, HB:HB + HD].reshape(10, RD, QL)], axis=1).transpose(2, 0, 1)
         dwkv = dwkv.reshape(NPAIR, QB, QB).astype(F32)

time: 573 us -> 547 us (0.955)
  matrix products: 74.4 us -> 9.91 us
  Pallas kernels: 330 us -> 351 us
  waiting for transfers between devices: 30.4 us -> 50.1 us
  starting transfers between devices: 28.2 us -> 40 us
    dot_general x11 -> x2, matrix products: 74.4 us -> 9.91 us  [dot(): return lax.dot_general(a, b, dims, preferred_element_type=F32)]
    pallas_call x4, Pallas kernels: 227 us -> 248 us  [plane(): pl.pallas_call(functools.partial(plane_kernel, len(arrs), reduce, gather,...]
    ppermute x15, waiting for transfers between devices: 30.4 us -> 50 us  [zshift(): return lax.ppermute(v, 'tp', [(i, (i + d) % NTP) for i in range(NTP)])]
    ppermute x15, starting transfers between devices: 28.1 us -> 39.9 us  [zshift(): return lax.ppermute(v, 'tp', [(i, (i + d) % NTP) for i in range(NTP)])]
    unnamed x75 -> x57, local copies, waits for them, and re-layouts: 18.3 us -> 15.3 us
  transfers between devices with their start and end apart: 16 -> 16, of which waited for: 2 -> 5; matrix products, arithmetic and copies ran while one was open for 22% -> 7% of each run, Pallas kernels for 59% -> 32%
where the time goes in v3:
time: 547 us; the launch traced here: 542 us
  Pallas kernels  351 us (64%)
  waiting for transfers between devices  50.1 us (9%)
  starting transfers between devices  40 us (7%)
  local copies, waits for them, and re-layouts  38.6 us (7%)
  other arithmetic  37.3 us (7%)
  between operations  14.9 us (3%)
  matrix products  9.91 us (2%)
    pallas_call x4, Pallas kernels, plane(): pl.pallas_call(functools.partial(plane_kernel, len(arrs), reduce, gather,...  248 us
    pallas_call x4, Pallas kernels, attention(): pl.pallas_call(functools.partial(attn_kernel, b0), grid_spec=grid_spec, o...  103 us
    ppermute x15, waiting for transfers between devices, zshift(): return lax.ppermute(v, 'tp', [(i, (i + d) % NTP) for i in range(NTP)])  50 us
    ppermute x15, starting transfers between devices, zshift(): return lax.ppermute(v, 'tp', [(i, (i + d) % NTP) for i in range(NTP)])  39.9 us
    unnamed x57, local copies, waits for them, and re-layouts  15.3 us
  transfers between devices with their start and end apart: 16, of which 5 were waited for; matrix products, arithmetic and copies ran while one was open for 7% of the time, Pallas kernels for 32%

profile of v3, /device:TPU:0, one launch (start us, length us, event | category | flops | bytes accessed | tf_op | source)
XLA Modules:
  0.0 541.9 jit_solution(3652232231592178697)
XLA Ops:
  9.0 3.1 collective-permute-start
  12.1 2.6 collective-permute-start.1
  16.0 5.9 %convolution_convert_fusion.1 = bf16[1024,288]{1,0:T(8,128)(2,1)S(1)} fusion(bf16[1024,2560]{1,0:T(8,128)(2,1)} %bitcast.111, bf16[2560,288]{0,1:T(8,128)(2,1)} %param.14), kind=kOutput, calls=%fused_computation.6 | convolution fusion | flops 1510244352 | bytes 7307264 | tf_op jit(solution)/shard_map/dot_general | solution.py:29
  27.3 2.8 maximum_maximum_fusion.1
  30.1 31.5 %plane.4 = (bf16[8,1024,256]{2,1,0:T(8,128)(2,1)}, bf16[8,256,128]{2,1,0:T(8,128)(2,1)}, bf16[1024,640]{1,0:T(8,128)(2,1)}, bf16[1024,768]{1,0:T(8,128)(2,1)}, b...) custom-call(bf16[1024,256]{1,0:T(8,128)(2,1)} %fusion.3.refs_0_, bf16[256,128]{1,0:T(8,128)(2,1)} %copy.44.refs_1_, ...), custom_call_target="tpu_custom_call" | custom-call | flops 30000001024 | bytes 1048576 | tf_op jit(solution)/shard_map/plane/pallas_call | solution.py:477
  62.8 2.6 pad_maximum_fusion
  67.2 25.3 %attn.4 = (bf16[1,256,640]{2,1,0:T(8,128)(2,1)S(1)}, bf16[4,256,1280]{2,1,0:T(8,128)(2,1)}, f32[5,256,256]{2,1,0:T(8,128)S(1)}, bf16[8,4,256,256]{3,2,1,0:T(8,128)(2,1)}, bf16[8,256,128]{2,1,0:T(8,128)(2,1)S(1)}) custom-call(s32[1]{0:T(128)} %bitcast.r_ref, bf16[4,256,1280]{2,1,0:T(8,128)(2,1)} %bitcast.122, bf16[4,256,640]{2,1,0:T(8,128)(2,1)} %bitcast.130, ...), custom_call_target="tpu_custom_call" | custom-call | flops 20000000000 | bytes 8000000 | tf_op jit(solution)/shard_map/attn/pallas_call | solution.py:222
  92.5 25.9 %attn.5 = (bf16[1,256,640]{2,1,0:T(8,128)(2,1)S(1)}, bf16[4,256,1280]{2,1,0:T(8,128)(2,1)}, f32[5,256,256]{2,1,0:T(8,128)S(1)}, bf16[8,4,256,256]{3,2,1,0:T(8,128)(2,1)}, bf16[8,256,128]{2,1,0:T(8,128)(2,1)S(1)}) custom-call(s32[1]{0:T(128)} %bitcast.r_ref, bf16[4,256,1280]{2,1,0:T(8,128)(2,1)} %bitcast.123, ...), custom_call_target="tpu_custom_call", output_to_operand_aliasing={{1}: (10, {}), {3}: (11, {})} | custom-call | flops 20000000000 | bytes 8000000 | tf_op jit(solution)/shard_map/attn/pallas_call | solution.py:222
  119.5 25.7 %attn.6 = (bf16[1,256,640]{2,1,0:T(8,128)(2,1)S(1)}, bf16[4,256,1280]{2,1,0:T(8,128)(2,1)}, f32[5,256,256]{2,1,0:T(8,128)S(1)}, bf16[8,4,256,256]{3,2,1,0:T(8,128)(2,1)}, bf16[8,256,128]{2,1,0:T(8,128)(2,1)S(1)}) custom-call(s32[1]{0:T(128)} %bitcast.r_ref, bf16[4,256,1280]{2,1,0:T(8,128)(2,1)} %bitcast.124, ...), custom_call_target="tpu_custom_call", output_to_operand_aliasing={{1}: (10, {}), {3}: (11, {})} | custom-call | flops 20000000000 | bytes 8000000 | tf_op jit(solution)/shard_map/attn/pallas_call | solution.py:222
  146.3 25.9 %attn.7 = (bf16[1,256,640]{2,1,0:T(8,128)(2,1)S(1)}, bf16[4,256,1280]{2,1,0:T(8,128)(2,1)}, f32[5,256,256]{2,1,0:T(8,128)S(1)}, bf16[8,4,256,256]{3,2,1,0:T(8,128)(2,1)}, bf16[8,256,128]{2,1,0:T(8,128)(2,1)S(1)}) custom-call(s32[1]{0:T(128)} %bitcast.r_ref, bf16[4,256,1280]{2,1,0:T(8,128)(2,1)} %bitcast.125, ...), custom_call_target="tpu_custom_call", output_to_operand_aliasing={{1}: (10, {}), {3}: (11, {})} | custom-call | flops 20000000000 | bytes 8000000 | tf_op jit(solution)/shard_map/attn/pallas_call | solution.py:222
  175.5 2.9 collective-permute-start.14
  182.6 2.1 collective-permute-done.12
  184.7 14.1 %collective-permute-done.13 = bf16[1,256,640]{2,1,0:T(8,128)(2,1)S(1)} collective-permute-done((bf16[1,256,640]{2,1,0:T(8,128)(2,1)S(1)}, bf16[1,256,640]{2,1,0:T(8,128)(2,1)S(1)}, u32[]{:S(2)}, u32[]{:S(2)}) %collective-permute-start.13) | collective-permute-done | bytes 327712 | tf_op jit(solution)/shard_map/ppermute | solution.py:570
  198.8 17.5 %collective-permute-start.6 = (bf16[1,256,640]{2,1,0:T(8,128)(2,1)S(1)}, bf16[1,256,640]{2,1,0:T(8,128)(2,1)}, u32[]{:S(2)}, u32[]{:S(2)}) collective-permute-start(bf16[1,256,640]{2,1,0:T(8,128)(2,1)S(1)} %get-tuple-element.69), channel_id=1, source_target_pairs={{0,8},{8,16},{16,24},{24,0},{1,9},{9,17},{17,25},{25,1},{2,10},{10... | collective-permute-start | bytes 983048 | tf_op jit(solution)/shard_map/ppermute | solution.py:570
  216.3 37.4 %plane.5 = (f32[1024,256]{1,0:T(8,128)}, f32[256,128]{1,0:T(8,128)}, bf16[1024,768]{1,0:T(8,128)(2,1)}, bf16[640,2560]{1,0:T(8,128)(2,1)}, bf16[1280,768]{1,0:T(8,128)(2,1)}) custom-call(bf16[8,1024,256]{2,1,0:T(8,128)(2,1)} %bitcast.120, bf16[8,256,128]{2,1,0:T(8,128)(2,1)} %copy-done.7, bf16[1024,1280]{1,0:T(8,128)(2,1)} %bitcast.126, ...), custom_call_target="tpu_custom_call" | custom-call | flops 30000001024 | bytes 1048576 | tf_op jit(solution)/shard_map/plane/pallas_call | solution.py:477
  257.0 4.4 concatenate.34.refs_3_
  261.4 3.5 collective-permute-start.7
  267.1 2.9 collective-permute-start.5
  270.0 3.2 add_convert_fusion
  273.2 7.5 %collective-permute-done.7 = bf16[1,256,640]{2,1,0:T(8,128)(2,1)S(1)} collective-permute-done((bf16[1,256,640]{2,1,0:T(8,128)(2,1)S(1)}, bf16[1,256,640]{2,1,0:T(8,128)(2,1)S(1)}, u32[]{:S(2)}, u32[]{:S(2)}) %collective-permute-start.7) | collective-permute-done | bytes 327712 | tf_op jit(solution)/shard_map/ppermute | solution.py:570
  280.7 8.5 %collective-permute-done.8 = bf16[1,256,640]{2,1,0:T(8,128)(2,1)S(1)} collective-permute-done((bf16[1,256,640]{2,1,0:T(8,128)(2,1)S(1)}, bf16[1,256,640]{2,1,0:T(8,128)(2,1)S(1)}, u32[]{:S(2)}, u32[]{:S(2)}) %collective-permute-start.8) | collective-permute-done | bytes 327712 | tf_op jit(solution)/shard_map/ppermute | solution.py:570
  289.2 17.8 %collective-permute-done.4 = bf16[1,256,640]{2,1,0:T(8,128)(2,1)S(1)} collective-permute-done((bf16[1,256,640]{2,1,0:T(8,128)(2,1)S(1)}, bf16[1,256,640]{2,1,0:T(8,128)(2,1)S(1)}, u32[]{:S(2)}, u32[]{:S(2)}) %collective-permute-start.4) | collective-permute-done | bytes 327712 | tf_op jit(solution)/shard_map/ppermute | solution.py:570
  307.1 6.2 %maximum_maximum_fusion = bf16[4,256,2560]{2,1,0:T(8,128)(2,1)} fusion(bf16[1,256,640]{2,1,0:T(8,128)(2,1)} %collective-permute-done.14, bf16[1,256,640]{2,1,0:T(8,128)(2,1)S(1)} %copy-done.18, bf16[1,256,640]{2,1,0:T(8,128)(2,1)S(1)} %copy-done.16, bf16[1,256,640]{2,1,0:T(8,128)(2,1)S(1)} %get-tuple-element.71, ...), kind=kLoop, calls=%fused_computation | loop fusion | flops 83886080 | bytes 10485760 | tf_op jit(solution)/shard_map/concatenate | solution.py:631
  313.2 109.0 %plane.6 = (bf16[4,256,1152]{2,1,0:T(8,128)(2,1)}, f32[1,1024]{1,0:T(1,128)}, bf16[8,160,768]{2,1,0:T(8,128)(2,1)}, bf16[8,160,256]{2,1,0:T(8,128)(2,1)}, bf16[8...) custom-call(bf16[8,160,768]{2,1,0:T(8,128)(2,1)} %bitcast.129, bf16[8,160,256]{2,1,0:T(8,128)(2,1)} %bitcast.101, ...), custom_call_target="tpu_custom_call" | custom-call | flops 30000001024 | bytes 1048576 | tf_op jit(solution)/shard_map/plane/pallas_call | solution.py:477
  425.2 4.0 convolution_convert_fusion
  431.3 70.5 %plane.7 = (bf16[32,80,1152]{2,1,0:T(8,128)(2,1)}, bf16[1024,2560]{1,0:T(8,128)(2,1)}) custom-call(bf16[8,80,1152]{2,1,0:T(8,128)(2,1)} %bitcast.115, bf16[1024,1152]{1,0:T(8,128)(2,1)} %bitcast.128, bf16[2560,768]{1,0:T(8,128)(2,1)} %refs_2_.1, bf16[288,2560]{1,0:T(8,128)(2,1)} %bitcast.114), custom_call_target="tpu_custom_call" | custom-call | flops 30000001024 | bytes 1048576 | tf_op jit(solution)/shard_map/plane/pallas_call | solution.py:477
  501.8 5.9 %slice_convert_fusion = f32[2560,768]{1,0:T(8,128)} fusion(bf16[2560,1152]{1,0:T(8,128)(2,1)} %bitcast.76), kind=kLoop, calls=%fused_computation.1 | loop fusion | flops 1966080 | bytes 11796480 | tf_op jit(solution)/shard_map/convert_element_type | solution.py:659
  507.7 3.0 slice.81
  511.8 2.8 copy.51
  517.8 5.7 %convert.16 = f32[10,64,2560]{2,1,0:T(8,128)} convert(bf16[10,64,2560]{2,1,0:T(8,128)(2,1)} %bitcast.88) | non-fusion elementwise | flops 1638400 | bytes 9830400 | tf_op jit(solution)/shard_map/convert_element_type | solution.py:659
  526.6 5.6 %copy.61 = bf16[4,256,2560]{2,1,0:T(8,128)(2,1)} copy(bf16[4,256,2560]{2,1,0:T(8,128)(2,1)} %bitcast.79) | data formatting | bytes 10485760
  532.3 2.4 copy.62
  (121 shorter events, 38.9 us)
Async XLA Ops:
  7.2 306.0 %all-gather.2.cloned.1.call-start = ((), (), s32[]{:S(2)}) async-start(), calls=%async_computation | async-start | bytes 14745600 | tf_op jit(solution)/shard_map/all_gather | solution.py:614
  9.0 53.8 %collective-permute-start = (bf16[80,2560]{1,0:T(8,128)(2,1)}, bf16[80,2560]{1,0:T(8,128)(2,1)}, u32[]{:S(2)}, u32[]{:S(2)}) collective-permute-start(bf16[80,2560]{1,0:T(8,128)(2,1)} %constant_dynamic-slice_fusion.2), channel_id=1, source_target_pairs={{0,8},{8,16},{16,24},{24,0},{1,9},{9,17},{17,25},{25,1},{2,10},{10... | collective-permute-start | bytes 1228808 | tf_op jit(solution)/shard_map/ppermute | solution.py:570
  12.1 50.7 %collective-permute-start.1 = (bf16[80,2560]{1,0:T(8,128)(2,1)}, bf16[80,2560]{1,0:T(8,128)(2,1)}, u32[]{:S(2)}, u32[]{:S(2)}) collective-permute-start(bf16[80,2560]{1,0:T(8,128)(2,1)} %constant_dynamic-slice_fusion.2), channel_id=1, source_target_pairs={{0,16},{8,24},{16,0},{24,8},{1,17},{9,25},{17,1},{25,9},{2,18},{10... | collective-permute-start | bytes 1228808 | tf_op jit(solution)/shard_map/ppermute | solution.py:570
  14.7 48.2 %collective-permute-start.2 = (bf16[80,2560]{1,0:T(8,128)(2,1)}, bf16[80,2560]{1,0:T(8,128)(2,1)}, u32[]{:S(2)}, u32[]{:S(2)}) collective-permute-start(bf16[80,2560]{1,0:T(8,128)(2,1)} %constant_dynamic-slice_fusion.2), channel_id=1, source_target_pairs={{0,24},{8,0},{16,8},{24,16},{1,25},{9,1},{17,9},{25,17},{2,26},{10... | collective-permute-start | bytes 1228808 | tf_op jit(solution)/shard_map/ppermute | solution.py:570
  16.0 6.2 %copy-start.12 = (bf16[768,10,96]{0,2,1:T(8,128)(2,1)S(1)}, bf16[768,10,96]{0,2,1:T(8,128)(2,1)}, u32[]{:S(2)}) copy-start(bf16[768,10,96]{0,2,1:T(8,128)(2,1)} %param.16) | copy-start | bytes 4423684
  25.7 4.4 copy-start.21
  61.6 5.6 %copy-start.3 = (bf16[256,10,64]{0,2,1:T(8,128)(2,1)S(1)}, bf16[256,10,64]{0,2,1:T(8,128)(2,1)}, u32[]{:S(2)}) copy-start(bf16[256,10,64]{0,2,1:T(8,128)(2,1)} %param.17) | copy-start | bytes 983044
  61.6 5.5 %copy-start.4 = (bf16[256,10,64]{0,2,1:T(8,128)(2,1)S(1)}, bf16[256,10,64]{0,2,1:T(8,128)(2,1)}, u32[]{:S(2)}) copy-start(bf16[256,10,64]{0,2,1:T(8,128)(2,1)} %param.18) | copy-start | bytes 983044
  61.6 5.5 %copy-start.5 = (bf16[8,256,128]{2,1,0:T(8,128)(2,1)S(1)}, bf16[8,256,128]{2,1,0:T(8,128)(2,1)}, u32[]{:S(2)}) copy-start(bf16[8,256,128]{2,1,0:T(8,128)(2,1)} %get-tuple-element.55.rest_1_) | copy-start | bytes 1572868
  92.5 27.0 %copy-start.6 = (bf16[8,256,128]{2,1,0:T(8,128)(2,1)S(1)}, bf16[8,256,128]{2,1,0:T(8,128)(2,1)}, u32[]{:S(2)}) copy-start(bf16[8,256,128]{2,1,0:T(8,128)(2,1)} %get-tuple-element.55.rest_1_) | copy-start | bytes 1572868
  172.2 26.6 %copy-start.2 = (f32[5,256,256]{2,1,0:T(8,128)}, f32[5,256,256]{2,1,0:T(8,128)S(1)}, u32[]{:S(2)}) copy-start(f32[5,256,256]{2,1,0:T(8,128)S(1)} %get-tuple-element.77) | copy-start | bytes 3932164
  172.2 44.2 %copy-start.7 = (bf16[8,256,128]{2,1,0:T(8,128)(2,1)}, bf16[8,256,128]{2,1,0:T(8,128)(2,1)S(1)}, u32[]{:S(2)}) copy-start(bf16[8,256,128]{2,1,0:T(8,128)(2,1)S(1)} %get-tuple-element.66.refs_1_) | copy-start | bytes 1572868
  172.2 12.5 %collective-permute-start.12 = (bf16[1,256,640]{2,1,0:T(8,128)(2,1)S(1)}, bf16[1,256,640]{2,1,0:T(8,128)(2,1)S(1)}, u32[]{:S(2)}, u32[]{:S(2)}) collective-permute-start(bf16[1,256,640]{2,1,0:T(8,128)(2,1)S(1)} %get-tuple-element.71), channel_id=1, source_target_pairs={{0,8},{8,16},{16,24},{24,0},{1,9},{9,17},{17,25},{25,1},{2,10},{10... | collective-permute-start | bytes 983048 | tf_op jit(solution)/shard_map/ppermute | solution.py:570
  172.9 25.9 %collective-permute-start.13 = (bf16[1,256,640]{2,1,0:T(8,128)(2,1)S(1)}, bf16[1,256,640]{2,1,0:T(8,128)(2,1)S(1)}, u32[]{:S(2)}, u32[]{:S(2)}) collective-permute-start(bf16[1,256,640]{2,1,0:T(8,128)(2,1)S(1)} %get-tuple-element.71), channel_id=1, source_target_pairs={{0,16},{8,24},{16,0},{24,8},{1,17},{9,25},{17,1},{25,9},{2,18},{10... | collective-permute-start | bytes 983048 | tf_op jit(solution)/shard_map/ppermute | solution.py:570
  175.5 85.8 %collective-permute-start.14 = (bf16[1,256,640]{2,1,0:T(8,128)(2,1)S(1)}, bf16[1,256,640]{2,1,0:T(8,128)(2,1)}, u32[]{:S(2)}, u32[]{:S(2)}) collective-permute-start(bf16[1,256,640]{2,1,0:T(8,128)(2,1)S(1)} %get-tuple-element.71), channel_id=1, source_target_pairs={{0,24},{8,0},{16,8},{24,16},{1,25},{9,1},{17,9},{25,17},{2,26},{10... | collective-permute-start | bytes 983048 | tf_op jit(solution)/shard_map/ppermute | solution.py:570
  178.4 86.5 %collective-permute-start.10 = (bf16[1,256,640]{2,1,0:T(8,128)(2,1)S(1)}, bf16[1,256,640]{2,1,0:T(8,128)(2,1)}, u32[]{:S(2)}, u32[]{:S(2)}) collective-permute-start(bf16[1,256,640]{2,1,0:T(8,128)(2,1)S(1)} %get-tuple-element.70), channel_id=1, source_target_pairs={{0,16},{8,24},{16,0},{24,8},{1,17},{9,25},{17,1},{25,9},{2,18},{10... | collective-permute-start | bytes 983048 | tf_op jit(solution)/shard_map/ppermute | solution.py:570
  180.4 84.7 %collective-permute-start.11 = (bf16[1,256,640]{2,1,0:T(8,128)(2,1)S(1)}, bf16[1,256,640]{2,1,0:T(8,128)(2,1)}, u32[]{:S(2)}, u32[]{:S(2)}) collective-permute-start(bf16[1,256,640]{2,1,0:T(8,128)(2,1)S(1)} %get-tuple-element.70), channel_id=1, source_target_pairs={{0,24},{8,0},{16,8},{24,16},{1,25},{9,1},{17,9},{25,17},{2,26},{10... | collective-permute-start | bytes 983048 | tf_op jit(solution)/shard_map/ppermute | solution.py:570
  184.7 31.6 %copy-start.15 = (bf16[1,256,640]{2,1,0:T(8,128)(2,1)}, bf16[1,256,640]{2,1,0:T(8,128)(2,1)S(1)}, u32[]{:S(2)}) copy-start(bf16[1,256,640]{2,1,0:T(8,128)(2,1)S(1)} %collective-permute-done.12) | copy-start | bytes 983044
  184.7 82.2 %collective-permute-start.9 = (bf16[1,256,640]{2,1,0:T(8,128)(2,1)S(1)}, bf16[1,256,640]{2,1,0:T(8,128)(2,1)}, u32[]{:S(2)}, u32[]{:S(2)}) collective-permute-start(bf16[1,256,640]{2,1,0:T(8,128)(2,1)S(1)} %get-tuple-element.70), channel_id=1, source_target_pairs={{0,8},{8,16},{16,24},{24,0},{1,9},{9,17},{17,25},{25,1},{2,10},{10... | collective-permute-start | bytes 983048 | tf_op jit(solution)/shard_map/ppermute | solution.py:570
  198.8 17.5 %copy-start.17 = (bf16[1,256,640]{2,1,0:T(8,128)(2,1)}, bf16[1,256,640]{2,1,0:T(8,128)(2,1)S(1)}, u32[]{:S(2)}) copy-start(bf16[1,256,640]{2,1,0:T(8,128)(2,1)S(1)} %collective-permute-done.13) | copy-start | bytes 983044
  198.8 68.3 %collective-permute-start.6 = (bf16[1,256,640]{2,1,0:T(8,128)(2,1)S(1)}, bf16[1,256,640]{2,1,0:T(8,128)(2,1)}, u32[]{:S(2)}, u32[]{:S(2)}) collective-permute-start(bf16[1,256,640]{2,1,0:T(8,128)(2,1)S(1)} %get-tuple-element.69), channel_id=1, source_target_pairs={{0,8},{8,16},{16,24},{24,0},{1,9},{9,17},{17,25},{25,1},{2,10},{10... | collective-permute-start | bytes 983048 | tf_op jit(solution)/shard_map/ppermute | solution.py:570
  261.4 45.7 %copy-start.16 = (bf16[1,256,640]{2,1,0:T(8,128)(2,1)S(1)}, bf16[1,256,640]{2,1,0:T(8,128)(2,1)}, u32[]{:S(2)}) copy-start(bf16[1,256,640]{2,1,0:T(8,128)(2,1)} %copy-done.15) | copy-start | bytes 983044
  261.4 45.7 %copy-start.18 = (bf16[1,256,640]{2,1,0:T(8,128)(2,1)S(1)}, bf16[1,256,640]{2,1,0:T(8,128)(2,1)}, u32[]{:S(2)}) copy-start(bf16[1,256,640]{2,1,0:T(8,128)(2,1)} %copy-done.17) | copy-start | bytes 983044
  261.4 19.4 %collective-permute-start.7 = (bf16[1,256,640]{2,1,0:T(8,128)(2,1)S(1)}, bf16[1,256,640]{2,1,0:T(8,128)(2,1)S(1)}, u32[]{:S(2)}, u32[]{:S(2)}) collective-permute-start(bf16[1,256,640]{2,1,0:T(8,128)(2,1)S(1)} %get-tuple-element.69), channel_id=1, source_target_pairs={{0,16},{8,24},{16,0},{24,8},{1,17},{9,25},{17,1},{25,9},{2,18},{10... | collective-permute-start | bytes 983048 | tf_op jit(solution)/shard_map/ppermute | solution.py:570
  264.9 24.4 %collective-permute-start.8 = (bf16[1,256,640]{2,1,0:T(8,128)(2,1)S(1)}, bf16[1,256,640]{2,1,0:T(8,128)(2,1)S(1)}, u32[]{:S(2)}, u32[]{:S(2)}) collective-permute-start(bf16[1,256,640]{2,1,0:T(8,128)(2,1)S(1)} %get-tuple-element.69), channel_id=1, source_target_pairs={{0,24},{8,0},{16,8},{24,16},{1,25},{9,1},{17,9},{25,17},{2,26},{10... | collective-permute-start | bytes 983048 | tf_op jit(solution)/shard_map/ppermute | solution.py:570
  265.1 24.1 %collective-permute-start.3 = (bf16[1,256,640]{2,1,0:T(8,128)(2,1)S(1)}, bf16[1,256,640]{2,1,0:T(8,128)(2,1)S(1)}, u32[]{:S(2)}, u32[]{:S(2)}) collective-permute-start(bf16[1,256,640]{2,1,0:T(8,128)(2,1)S(1)} %get-tuple-element.68), channel_id=1, source_target_pairs={{0,8},{8,16},{16,24},{24,0},{1,9},{9,17},{17,25},{25,1},{2,10},{10... | collective-permute-start | bytes 983048 | tf_op jit(solution)/shard_map/ppermute | solution.py:570
  266.9 40.1 %collective-permute-start.4 = (bf16[1,256,640]{2,1,0:T(8,128)(2,1)S(1)}, bf16[1,256,640]{2,1,0:T(8,128)(2,1)S(1)}, u32[]{:S(2)}, u32[]{:S(2)}) collective-permute-start(bf16[1,256,640]{2,1,0:T(8,128)(2,1)S(1)} %get-tuple-element.68), channel_id=1, source_target_pairs={{0,16},{8,24},{16,0},{24,8},{1,17},{9,25},{17,1},{25,9},{2,18},{10... | collective-permute-start | bytes 983048 | tf_op jit(solution)/shard_map/ppermute | solution.py:570
  267.1 39.9 %collective-permute-start.5 = (bf16[1,256,640]{2,1,0:T(8,128)(2,1)S(1)}, bf16[1,256,640]{2,1,0:T(8,128)(2,1)S(1)}, u32[]{:S(2)}, u32[]{:S(2)}) collective-permute-start(bf16[1,256,640]{2,1,0:T(8,128)(2,1)S(1)} %get-tuple-element.68), channel_id=1, source_target_pairs={{0,24},{8,0},{16,8},{24,16},{1,25},{9,1},{17,9},{25,17},{2,26},{10... | collective-permute-start | bytes 983048 | tf_op jit(solution)/shard_map/ppermute | solution.py:570
  517.8 5.7 %copy-start.11 = (bf16[8,160,256]{2,1,0:T(8,128)(2,1)S(1)}, bf16[8,160,256]{2,1,0:T(8,128)(2,1)}, u32[]{:S(2)}) copy-start(bf16[8,160,256]{2,1,0:T(8,128)(2,1)} %get-tuple-element.90) | copy-start | bytes 1966084
  517.8 6.9 %copy-start.9 = (f32[5,64,768]{2,1,0:T(8,128)S(1)}, f32[5,64,768]{2,1,0:T(8,128)}, u32[]{:S(2)}) copy-start(f32[5,64,768]{2,1,0:T(8,128)} %slice.84) | copy-start | bytes 2949124
  524.8 7.5 %slice-start = ((s8[5242880]{0:T(1024)(128)(4,1)}), s8[4194304]{0:T(1024)(128)(4,1)S(1)}, s32[]{:S(2)}) async-start(s8[5242880]{0:T(1024)(128)(4,1)} %bitcast.81), calls=%async_computation.1 | async-start | bytes 8388608
  526.6 5.7 %slice-start.1 = ((s8[5242880]{0:T(1024)(128)(4,1)}), s8[1048576]{0:T(1024)(128)(4,1)S(1)}, s32[]{:S(2)}) async-start(s8[5242880]{0:T(1024)(128)(4,1)} %bitcast.81), calls=%async_computation.2 | async-start | bytes 2097152
  (10 other events, 21.0 us)
Sparse Core Ops, SparseCore 0:
  65.6 72.7 all-gather.1

commit v4 on v3

--- a/solution.py
+++ b/solution.py
@@ -19,10 +19,14 @@
 NN = (((1,), (0,)), ((), ()))
 HB, QB, CH, SEQ = 128, 256, 512, 2048
 HD, KD, RD, QL = 64, 160, 32, 768
-NBLK, NCP, NTP, NPAIR = 16, 8, 4, 5
+NBLK, NCP, NTP, NPAIR, NBAT = 16, 8, 4, 5, 4
 TOK, DM, HV, QW, ALL, DWW = 1024, 2560, 640, 1280, 1056, 1152
 RH = 16
 HOPS = range(1, NTP)
+
+
+def cost(flops):
+    return pl.CostEstimate(flops=flops, bytes_accessed=TOK * TOK, transcendentals=0)
 
 
 def dot(a, b, dims):
@@ -55,13 +59,13 @@
             dev, part = owner(blk)
             ckv[rows, :] = kv_ref[dev, 0, part, :]
             kcat[rows, HB:KD] = kpe_ref[dev, part, b0 * RD:(b0 + 1) * RD]
-        for i in range(4):
+        for i in range(NBAT):
             ckvt[:, i * CH:(i + 1) * CH] = ckv[i * CH:(i + 1) * CH, :].T
         dckv[...] = jnp.zeros_like(dckv)
         dkpe[...] = jnp.zeros_like(dkpe)
 
     wkv = jnp.concatenate([wk_ref[...], wv_ref[...]], axis=0)
-    for i in range(4):
+    for i in range(NBAT):
         rows = slice(i * CH, (i + 1) * CH)
         kv = dot(ckv[rows, :], wkv, NT).astype(BF)
         kcat[rows, 0:HB] = kv[:, 0:HB]
@@ -169,7 +173,7 @@
         dq_ref[0, rows, HB:QB] = jnp.concatenate(pe + [jnp.zeros((HD, HB), F32)], axis=0).T.astype(BF)
 
     dwt = jnp.zeros((QB, QB), F32)
-    for i in range(4):
+    for i in range(NBAT):
         rows = slice(i * CH, (i + 1) * CH)
         dkv = jnp.concatenate([(dk_acc[rows, 0:HB] * scale).astype(BF), dv_acc[rows, :].astype(BF)], axis=1)
         dkpe[rows, :] += dk_acc[rows, HB:KD] * scale
@@ -222,11 +226,11 @@
     return pl.pallas_call(
         functools.partial(attn_kernel, b0),
         grid_spec=grid_spec,
-        out_shape=[jax.ShapeDtypeStruct((nb, QB, HV), BF), jax.ShapeDtypeStruct((4, QB, QW), BF), jax.ShapeDtypeStruct((NPAIR, QB, QB), F32),
+        out_shape=[jax.ShapeDtypeStruct((nb, QB, HV), BF), jax.ShapeDtypeStruct((NBAT, QB, QW), BF), jax.ShapeDtypeStruct((NPAIR, QB, QB), F32),
                    jax.ShapeDtypeStruct((NCP, 4, QB, QB), BF),
                    jax.ShapeDtypeStruct((NCP, QB, HB), BF)],
         compiler_params=pltpu.CompilerParams(vmem_limit_bytes=50 * TOK * TOK),
-        cost_estimate=pl.CostEstimate(flops=nb * 20_000_000_000, bytes_accessed=nb * 8_000_000, transcendentals=0),
+        cost_estimate=cost(nb * 20_000_000_000),
         input_output_aliases={10: 1, 11: 3} if prev else {},
         name="attn",
     )(rank, q, do, wk, wv, cos_t, sin_t, kv, kpe, *prev)
@@ -243,8 +247,9 @@
     def __init__(self, filler, refs):
         n_in, n_out, n_extra = len(filler.args), len(filler.outs), len(filler.extra)
         src, self.outs, refs = refs[:n_in], refs[n_in:n_in + n_out], refs[n_in + n_out:]
-        self.bufs, sems, extra = refs[:n_in], refs[n_in], refs[n_in + 1:n_in + 1 + n_extra]
-        self.loads = [pltpu.make_async_copy(a, b, sems.at[i]) for i, (a, b) in enumerate(zip(src, self.bufs))]
+        n_buf = len(filler.bufs)
+        self.bufs, sems, extra = refs[:n_buf], refs[n_buf], refs[n_buf + 1:n_buf + 1 + n_extra]
+        self.loads = [pltpu.make_async_copy(a, b, sems.at[i]) for i, (a, b) in enumerate(filler.place(src, self.bufs))]
         for c in self.loads:
             c.start()
         self.ready = [False] * n_in
@@ -282,8 +287,10 @@
 
 
 class Spec:
-    def __init__(self, args, outs, extra, groups):
+    def __init__(self, args, outs, extra, groups, bufs=(), place=zip):
         self.args, self.outs, self.extra, self.groups = args, outs, extra, groups
+        self.bufs = bufs or [a.shape for a in args]
+        self.place = place
 
 
 def tile(t, n):
@@ -294,8 +301,9 @@
     ins, refs = refs[:n_arr], refs[n_arr:]
     n_fill = len(filler.args) if filler else 0
     if with_lat:
-        lat, cq_ref, ckv_ref, gq_ref, gkv_ref, cos_ref, sin_ref = refs[:7]
-        refs = refs[7:]
+        lats, refs = refs[:3], refs[3:]
+        cq_ref, ckv_ref, gq_ref, gkv_ref, cos_ref, sin_ref = refs[:6]
+        refs = refs[6:]
     fill_src, refs = refs[:n_fill], refs[n_fill:]
     if with_lat:
         (raw, gg), refs = refs[:2], refs[2:]
@@ -304,15 +312,15 @@
     r = lax.axis_index('cp')
     z = lax.axis_index('tp')
     send, recv, scratch = refs[0], refs[1], refs[2:]
-    peers = {m: {'cp': r ^ m} for m in (1, 2, 4)}
+    pc, px, py = [{'cp': r ^ m} for m in (1, 2, 4)]
     barrier = pltpu.get_barrier_semaphore()
-    targets = list(peers.values()) + [{'tp': lax.rem(z + d, NTP)} for d in range(1, NTP if with_lat else n_z)]
+    targets = [pc, px, py] + [{'tp': lax.rem(z + d, NTP)} for d in range(1, NTP if with_lat else n_z)]
     for t in targets:
         pl.semaphore_signal(barrier, inc=1, device_id=t, device_id_type=pl.DeviceIdType.MESH)
     pl.semaphore_wait(barrier, len(targets))
     count = [0]
     started = []
-    n_tail = (len(filler.args) + 1 + len(filler.extra)) if filler else 0
+    n_tail = (len(filler.bufs) + 1 + len(filler.extra)) if filler else 0
     fill = Filler(filler, list(fill_src) + list(fill_out) + list(scratch[len(scratch) - n_tail:])) if filler else NoFill()
 
     def copy(src, dst, target):
@@ -323,6 +331,39 @@
         c.start()
         started.append(c)
         return c
+
+    hop_base = count[0]
+    if with_lat:
+        count[0] += 2 * NTP
+
+    def line(right, h):
+        blk = raw.at[lax.rem(z + (NTP + 1 - h if right else NTP + h - 1), NTP)]
+        k = hop_base + h + (0 if right else NTP)
+        c = pltpu.make_async_remote_copy(src_ref=blk, dst_ref=blk, send_sem=send.at[k], recv_sem=recv.at[k],
+                                         device_id={'tp': lax.rem(z + (1 if right else NTP - 1), NTP)}, device_id_type=pl.DeviceIdType.MESH)
+        on = jnp.logical_and(z < NTP - 1, z >= h - 1) if right else jnp.logical_and(z > 0, z <= NTP - h)
+        return c, on
+
+    def hop(h):
+        for right in (True, False):
+            c, on = line(right, h)
+
+            @pl.when(on)
+            def _():
+                if h > 1:
+                    line(right, h - 1)[0].wait_recv()
+                c.start()
+
+    def hop_end():
+        for right in (True, False):
+            @pl.when(z == (NTP - 1 if right else 0))
+            def _():
+                for h in HOPS:
+                    line(right, h)[0].wait_recv()
+
+            for h in HOPS:
+                c, on = line(right, h)
+                pl.when(on)(c.wait_send)
 
     work = []
     for i in range(n_arr):
@@ -338,16 +379,16 @@
         w['b'] = slice(w['a'].stop, rows)
         work.append(w)
     if with_lat:
-        zr = scratch[0]
-        z_in = [copy(lat.at[lax.rem(z + d, NTP)], zr.at[d - 1], {'tp': lax.rem(z + d, NTP)}) for d in HOPS]
+        zrs = scratch[:3]
+        z_in = [copy(a.at[lax.rem(z + d, NTP)], b.at[d - 1], {'tp': lax.rem(z + d, NTP)}) for d in HOPS for a, b in zip(lats, zrs)]
     if reduce:
         for w in work:
             w['c'] = [None] * 4
         for k in (3, 1, 2, 0):
             for w in work:
-                w['c'][k] = copy(w['in'].at[r ^ (2 * k + 1)], w['rc'].at[k], peers[1])
-
-        fill.run(8)
+                w['c'][k] = copy(w['in'].at[r ^ (2 * k + 1)], w['rc'].at[k], pc)
+
+        fill.run(2 if n_z > 1 else 8)
 
         def local(w, k):
             w['c'][k].wait_recv()
@@ -355,22 +396,22 @@
 
         for w in work:
             w['sb'][3] = local(w, 3).astype(BF)
-            w['da'] = copy(w['sb'].at[3, w['a']], w['rd'].at[w['a']], peers[2])
-            w['db'] = copy(w['sb'].at[3, w['b']], w['rd'].at[w['b']], peers[4])
-        fill.run(4)
+            w['da'] = copy(w['sb'].at[3, w['a']], w['rd'].at[w['a']], px)
+            w['db'] = copy(w['sb'].at[3, w['b']], w['rd'].at[w['b']], py)
+        fill.run(NTP // n_z)
         for w in work:
             w['sb'][1] = local(w, 1).astype(BF)
-            w['xa'] = copy(w['sb'].at[1, w['a']], w['rx'].at[w['a']], peers[2])
+            w['xa'] = copy(w['sb'].at[1, w['a']], w['rx'].at[w['a']], px)
             w['sb'][2] = local(w, 2).astype(BF)
-            w['yb'] = copy(w['sb'].at[2, w['b']], w['ry'].at[w['b']], peers[4])
+            w['yb'] = copy(w['sb'].at[2, w['b']], w['ry'].at[w['b']], py)
         fill.run(4)
         for w in work:
             w['da'].wait_recv()
             w['sb'][2, w['a']] = (w['sb'][2, w['a']].astype(F32) + w['rd'][w['a']].astype(F32)).astype(BF)
-            w['ya'] = copy(w['sb'].at[2, w['a']], w['ry'].at[w['a']], peers[4])
+            w['ya'] = copy(w['sb'].at[2, w['a']], w['ry'].at[w['a']], py)
             w['db'].wait_recv()
             w['sb'][1, w['b']] = (w['sb'][1, w['b']].astype(F32) + w['rd'][w['b']].astype(F32)).astype(BF)
-            w['xb'] = copy(w['sb'].at[1, w['b']], w['rx'].at[w['b']], peers[2])
+            w['xb'] = copy(w['sb'].at[1, w['b']], w['rx'].at[w['b']], px)
         fill.run(6)
         for w in work:
             base = local(w, 0)
@@ -380,14 +421,14 @@
             if gather:
                 w['g'][z * NCP * (n_z > 1) + r] = total.astype(BF)
             else:
-                w['out'][...] = total
+                w['out'][...] = total.astype(BF)
     elif gather:
         for w in work:
             w['g'][r] = w['in'][...]
     if gather:
         def fan(w, zz):
             own = w['g'].at[zz + r]
-            return {'zz': zz, 2: copy(own, own, peers[2]), 4: copy(own, own, peers[4]), 1: copy(own, own, peers[1])}
+            return {'zz': zz, 'x': copy(own, own, px), 'y': copy(own, own, py), 'c': copy(own, own, pc)}
 
         flows = []
         z_copies = []
@@ -400,50 +441,56 @@
             fill.run(10)
             for c in z_in:
                 c.wait_recv()
-            for i in range(4):
+            for i in range(NBAT):
                 rows = slice(i * HD, (i + 1) * HD)
-                own = lat[z, rows, :].astype(F32)
-                for d in range(NTP - 1):
-                    own = own + zr[d, rows, :].astype(F32)
-                g_cq, part_q = norm_pull(own[:, :QL], cq_ref[rows, :].astype(F32), gq_ref[...])
-                g_ckv, part_kv = norm_pull(own[:, QL:TOK], ckv_ref[rows, :].astype(F32), gkv_ref[...])
-                p1, p2 = own[:, TOK:TOK + RH], own[:, TOK + RH:ALL]
+                own = []
+                for a, b in zip(lats, zrs):
+                    t = a[z, rows, :].astype(F32)
+                    for d in range(NTP - 1):
+                        t = t + b[d, rows, :].astype(F32)
+                    own.append(t)
+                g_cq, part_q = norm_pull(own[0], cq_ref[rows, :].astype(F32), gq_ref[...])
+                g_ckv, part_kv = norm_pull(own[1], ckv_ref[rows, :].astype(F32), gkv_ref[...])
+                p1, p2 = own[2][:, :RH], own[2][:, RH:RD]
                 cc, ss = cos_ref[rows, :], sin_ref[rows, :]
                 raw[z, rows, :] = jnp.concatenate([g_cq, g_ckv, p1 * cc + p2 * ss, p2 * cc - p1 * ss, jnp.zeros((HD, DWW - ALL), F32)], axis=1).astype(BF)
                 part = jnp.concatenate([part_q, part_kv], axis=1)
                 gg[...] = part if i == 0 else gg[...] + part
-            z_in = [copy(raw.at[z], raw.at[z], {'tp': lax.rem(z + d, NTP)}) for d in HOPS]
+            hop(1)
         for d in range(n_z):
             fill.run(4)
             for i, w in enumerate(work):
                 f = flows[i][d]
                 gx, gy = w['g'].at[f['zz'] + (r ^ 2)], w['g'].at[f['zz'] + (r ^ 4)]
-                f[2].wait_recv()
-                f['dy'] = copy(gx.at[w['b']], gx.at[w['b']], peers[4])
-                f['cx'] = copy(gx, gx, peers[1])
-                f[4].wait_recv()
-                f['dx'] = copy(gy.at[w['a']], gy.at[w['a']], peers[2])
-                f['cy'] = copy(gy, gy, peers[1])
+                f['x'].wait_recv()
+                f['dy'] = copy(gx.at[w['b']], gx.at[w['b']], py)
+                f['cx'] = copy(gx, gx, pc)
+                f['y'].wait_recv()
+                f['dx'] = copy(gy.at[w['a']], gy.at[w['a']], px)
+                f['cy'] = copy(gy, gy, pc)
                 if d + 1 < n_z:
                     z_copies[i][d].wait_recv()
                     flows[i].append(fan(w, lax.rem(z + NTP - (d + 1), NTP) * NCP))
         fill.run(3)
+        if with_lat:
+            hop(2)
         for d in range(n_z):
             for i, w in enumerate(work):
                 f = flows[i][d]
                 f['dy'].wait_recv()
                 f['dx'].wait_recv()
                 gd = w['g'].at[f['zz'] + (r ^ 6)]
-                f['cd'] = copy(gd, gd, peers[1])
+                f['cd'] = copy(gd, gd, pc)
         fill.run(QB)
+        if with_lat:
+            hop(3)
         for d in range(n_z):
             for i, w in enumerate(work):
                 f = flows[i][d]
-                for name in (1, 'cx', 'cy', 'cd'):
+                for name in ('c', 'cx', 'cy', 'cd'):
                     f[name].wait_recv()
         if with_lat:
-            for c in z_in:
-                c.wait_recv()
+            hop_end()
     fill.run(QB)
     for c in started:
         c.wait_send()
@@ -461,19 +508,19 @@
             shapes.append(jax.ShapeDtypeStruct((NCP * n_z, n, m), BF))
             n_copy += 8 * n_z + n_z - 1
         else:
-            shapes.append(jax.ShapeDtypeStruct((n, m), F32))
+            shapes.append(jax.ShapeDtypeStruct((n, m), BF))
     vmem = pl.BlockSpec(memory_space=pltpu.VMEM)
     if extra:
-        shapes = [jax.ShapeDtypeStruct((4, QB, DWW), BF), jax.ShapeDtypeStruct((1, TOK), F32)] + shapes
-        scratch.append(pltpu.VMEM((3, QB, DWW), BF))
-        n_copy += 6
+        shapes = [jax.ShapeDtypeStruct((NBAT, QB, DWW), BF), jax.ShapeDtypeStruct((1, TOK), F32)] + shapes
+        scratch += [pltpu.VMEM((3,) + a.shape[1:], BF) for a in extra[:3]]
+        n_copy += 18
     anyspec = []
     fill_args = ()
     if filler:
         fill_args = filler.args
         shapes += filler.outs
         anyspec = [pl.BlockSpec(memory_space=pl.ANY)] * len(filler.args)
-        scratch += [pltpu.VMEM(a.shape, BF) for a in filler.args] + [pltpu.SemaphoreType.DMA((len(filler.args),))] + filler.extra
+        scratch += [pltpu.VMEM(shape, BF) for shape in filler.bufs] + [pltpu.SemaphoreType.DMA((len(filler.args),))] + filler.extra
     return pl.pallas_call(
         functools.partial(plane_kernel, len(arrs), reduce, gather, n_z, bool(extra), filler),
         out_shape=shapes,
@@ -481,7 +528,7 @@
         out_specs=[vmem] * len(shapes),
         scratch_shapes=[pltpu.SemaphoreType.DMA((n_copy,)), pltpu.SemaphoreType.DMA((n_copy,))] + scratch,
         compiler_params=pltpu.CompilerParams(collective_id=cid, has_side_effects=True, vmem_limit_bytes=60 * TOK * TOK),
-        cost_estimate=pl.CostEstimate(flops=30_000_000_000, bytes_accessed=TOK * TOK, transcendentals=0),
+        cost_estimate=cost(30_000_000_000),
         name="plane",
     )(*arrs, *extra, *fill_args)
 
@@ -537,7 +584,14 @@
     return Spec([dq, w_q, o, dy2, c_q], [sds(TOK, QL), sds(HV, DM), sds(QW, QL)], [pltpu.VMEM((HV, TOK), BF), pltpu.VMEM((QW, TOK), BF)], groups)
 
 
-def y_fill(o_rel, wo_rel):
+def y_fill(o_parts, wo_rel):
+    def place(src, bufs):
+        pairs = []
+        for i in range(NBAT):
+            for d in range(NTP):
+                pairs.append((src[len(pairs)].at[0], bufs[0].at[i * QB:(i + 1) * QB, d * HV:(d + 1) * HV]))
+        return pairs + [(src[len(pairs)], bufs[1])]
+
     def groups(f, bufs, outs, extra):
         ov, wo = bufs
         y, = outs
@@ -546,9 +600,9 @@
             rows, cols = tile(lax.rem(t, 2), CH), tile(lax.div(t, 2), QB)
             y[rows, cols] = dot(ov[rows, :], wo[:, cols], NN).astype(BF)
 
-        return [((0, 1), None, y_body, 0, 20)]
-
-    return Spec([o_rel, wo_rel], [sds(TOK, DM)], [], groups)
+        return [(range(len(o_parts) + 1), None, y_body, 0, 20)]
+
+    return Spec(o_parts + [wo_rel], [sds(TOK, DM)], [], groups, [(TOK, DM), (DM, DM)], place)
 
 
 def last_fill(raw, w_dq, w_dkvt):
@@ -585,7 +639,7 @@
         z = lax.axis_index('tp')
         x2 = hidden.reshape(TOK, DM)
         dy2 = grad_out.reshape(TOK, DM)
-        half = 16
+        half = RH
         inv_freq = 1.0 / (THETA ** (jnp.arange(half, dtype=F32) * 2.0 / RD))
         idx = jnp.arange(QB, dtype=jnp.int32)
         positions = jnp.where(idx < HB, rank, NBLK - 1 - rank) * HB + idx % HB
@@ -598,15 +652,15 @@
         kv_raw = dot(x2, w_dkv, NN).astype(BF)
         ckv_f32 = kv_raw[:, :QB].astype(F32)
         c_kv = norm_f32(ckv_f32, gkv).astype(BF)
-        pe = kv_raw[:, QB:].astype(F32).reshape(4, QB, RD)
+        pe = kv_raw[:, QB:].astype(F32).reshape(NBAT, QB, RD)
         pe1, pe2 = pe[..., :half], pe[..., half:]
         k_pe = jnp.concatenate([pe1 * cos_tab - pe2 * sin_tab, pe2 * cos_tab + pe1 * sin_tab], axis=-1).astype(BF)
         wo2 = w_o.reshape(HV, DM)
         w_qt = w_uq.transpose(1, 2, 0)
         w_q = jnp.concatenate([w_qt[:, :HD].reshape(NPAIR, HB, QL), w_qt[:, HD:].reshape(NPAIR, HD, QL), jnp.zeros((NPAIR, HD, QL), BF)], axis=1).reshape(QW, QL)
         kv, kpe, do, cq_raw, c_q, q = plane([c_kv, k_pe.transpose(1, 0, 2).reshape(QB, HB)], 0, False, True, filler=front_fill(x2, w_dq, g_q, dy2, wo2, w_q))
-        q = q.reshape(4, QB, QW)
-        do = do.reshape(4, QB, HV)
+        q = q.reshape(NBAT, QB, QW)
+        do = do.reshape(NBAT, QB, HV)
         kv = kv.reshape(NCP, 4, QB, QB)
 
         wo_rel = jnp.stack(zrel(lax.dynamic_slice_in_dim(wo2, rank * 80, 80, 0)))
@@ -616,39 +670,37 @@
         wk = w_uk.transpose(1, 2, 0).reshape(HV, QB)
         wv = w_uv.transpose(1, 2, 0).reshape(HV, QB)
 
-        n_split = 4
-        nb = 4 // n_split
+        n_split = NBAT
+        nb = NBAT // n_split
         runs = []
         for i in range(n_split):
             prev = [runs[-1][4], runs[-1][1], runs[-1][3]] if runs else []
             runs.append(attention(rank.reshape(1), q, do, wk, wv, cos_t, sin_t, kv, kpe, prev, i * nb, nb))
-        o_rel = []
+        o_parts = []
         for run in runs:
-            parts = [run[0]]
+            o_parts.append(run[0])
             for d in HOPS:
-                parts.append(zshift(run[0], d))
-            o_rel.append(jnp.concatenate(parts, axis=2))
-        o_rel = jnp.concatenate(o_rel, axis=0).reshape(TOK, DM)
+                o_parts.append(zshift(run[0], d))
         o = jnp.concatenate([run[0] for run in runs], axis=0).reshape(TOK, HV)
         dq = runs[-1][1].reshape(TOK, QW)
         dwkv = sum(run[2] for run in runs)
 
         dckv, dkpe, lat_q, dwo, dwq = plane([runs[-1][3].reshape(NCP, TOK, QB), runs[-1][4]], 1, True, False, filler=mid_fill(dq, w_q, o, dy2, c_q))
         dkpe = dkpe.reshape(QB, 4, RD).transpose(1, 0, 2)
-        lat = jnp.concatenate([lat_q.reshape(4, QB, QL), dckv.reshape(4, QB, QB).astype(BF), dkpe.astype(BF), jnp.zeros((4, QB, DWW - ALL), BF)], axis=-1)
+        lats = [lat_q.reshape(NBAT, QB, QL), dckv.reshape(NBAT, QB, QB), jnp.pad(dkpe, ((0, 0), (0, 0), (0, HB - RD)))]
         cq_own = lax.dynamic_slice_in_dim(cq_raw, z * QB, QB, 0)
         ckv_own = lax.dynamic_slice_in_dim(kv_raw, z * QB, QB, 0)[:, :QB]
         dwq = dwq.reshape(NCP, KD, QL)
         dwkv = dwkv.reshape(NCP, KD, QB).astype(BF)
         dwo = dwo.reshape(NCP, 80, DM)
-        raw, grad_g, dwq, dwkv, dwo, attn_out = plane([dwq, dwkv, dwo], 3, True, True, 1, [lat, cq_own, ckv_own, gq[None], gkv[None], cos_tab, sin_tab], y_fill(o_rel, wo_rel))
+        raw, grad_g, dwq, dwkv, dwo, attn_out = plane([dwq, dwkv, dwo], 3, True, True, 1, lats + [cq_own, ckv_own, gq[None], gkv[None], cos_tab, sin_tab], y_fill(o_parts, wo_rel))
         raw_all = raw.reshape(TOK, DWW)
 
         x_slice = lax.dynamic_slice_in_dim(x2, z * HV, HV, 1)
         dwd = lax.dynamic_update_slice(dot(x_slice, raw_all, TN).astype(BF), grad_g.reshape(HB, NCP).astype(BF), (0, ALL)).reshape(NCP, 80, DWW)
         dwd, grad_hidden = plane([dwd], 2, True, True, NTP, filler=last_fill(raw.reshape(TOK, DWW), w_dq, w_dkv.T))
-        grad_hidden = grad_hidden.reshape(4, QB, DM)
-        attn_out = attn_out.reshape(4, QB, DM)
+        grad_hidden = grad_hidden.reshape(NBAT, QB, DM)
+        attn_out = attn_out.reshape(NBAT, QB, DM)
         dwd = dwd.reshape(DM, DWW)
         grad_g = jnp.sum(dwd.reshape(NTP, HV, DWW)[:, :HB, ALL:ALL + NCP].astype(F32), axis=0).reshape(TOK)
         dwq = dwq.reshape(NPAIR, QB, QL).astype(F32)

time: 547 us -> 522 us (0.954)
  Pallas kernels: 351 us -> 337 us
  other arithmetic: 37.3 us -> 29.5 us
    pallas_call x4, Pallas kernels: 248 us -> 234 us  [plane(): pl.pallas_call(functools.partial(plane_kernel, len(arrs), reduce, gather,...]
    concatenate x1 -> x0, other arithmetic: 6.16 us -> none  [per_device(): o_rel = jnp.concatenate(o_rel, axis=0).reshape(TOK, DM)]
    unnamed x57 -> x67, local copies, waits for them, and re-layouts: 15.3 us -> 16.4 us
  transfers between devices with their start and end apart: 16 -> 16, of which waited for: 5 -> 5; matrix products, arithmetic and copies ran while one was open for 7% -> 5% of each run, Pallas kernels for 32% -> 33%
where the time goes in v4:
time: 522 us; the launch traced here: 518 us
  Pallas kernels  337 us (65%)
  waiting for transfers between devices  49.5 us (9%)
  starting transfers between devices  39.9 us (8%)
  local copies, waits for them, and re-layouts  37.5 us (7%)
  other arithmetic  29.5 us (6%)
  between operations  14.9 us (3%)
  matrix products  9.91 us (2%)
    pallas_call x4, Pallas kernels, plane(): pl.pallas_call(functools.partial(plane_kernel, len(arrs), reduce, gather,...  234 us
    pallas_call x4, Pallas kernels, attention(): pl.pallas_call(functools.partial(attn_kernel, b0), grid_spec=grid_spec, o...  103 us
    ppermute x15, waiting for transfers between devices, zshift(): return lax.ppermute(v, 'tp', [(i, (i + d) % NTP) for i in range(NTP)])  49.5 us
    ppermute x15, starting transfers between devices, zshift(): return lax.ppermute(v, 'tp', [(i, (i + d) % NTP) for i in range(NTP)])  39.9 us
    unnamed x67, local copies, waits for them, and re-layouts  16.4 us
  transfers between devices with their start and end apart: 16, of which 5 were waited for; matrix products, arithmetic and copies ran while one was open for 5% of the time, Pallas kernels for 33%

profile of v4, /device:TPU:0, one launch (start us, length us, event | category | flops | bytes accessed | tf_op | source)
XLA Modules:
  0.0 518.1 jit_solution(6071568752907311767)
XLA Ops:
  9.0 3.1 collective-permute-start
  12.1 2.6 collective-permute-start.1
  16.0 5.9 %convolution_convert_fusion.1 = bf16[1024,288]{1,0:T(8,128)(2,1)S(1)} fusion(bf16[1024,2560]{1,0:T(8,128)(2,1)} %bitcast.108, bf16[2560,288]{0,1:T(8,128)(2,1)} %param.14), kind=kOutput, calls=%fused_computation.5 | convolution fusion | flops 1510244352 | bytes 7307264 | tf_op jit(solution)/shard_map/dot_general | solution.py:33
  27.3 2.8 maximum_maximum_fusion
  30.1 31.6 %plane.4 = (bf16[8,1024,256]{2,1,0:T(8,128)(2,1)}, bf16[8,256,128]{2,1,0:T(8,128)(2,1)}, bf16[1024,640]{1,0:T(8,128)(2,1)}, bf16[1024,768]{1,0:T(8,128)(2,1)}, b...) custom-call(bf16[1024,256]{1,0:T(8,128)(2,1)} %fusion.3.refs_0_, bf16[256,128]{1,0:T(8,128)(2,1)} %copy.44.refs_1_, ...), custom_call_target="tpu_custom_call" | custom-call | flops 30000001024 | bytes 1048576 | tf_op jit(solution)/shard_map/plane/pallas_call | solution.py:524
  62.7 2.6 pad_maximum_fusion
  67.1 25.4 %attn.4 = (bf16[1,256,640]{2,1,0:T(8,128)(2,1)S(1)}, bf16[4,256,1280]{2,1,0:T(8,128)(2,1)}, f32[5,256,256]{2,1,0:T(8,128)S(1)}, bf16[8,4,256,256]{3,2,1,0:T(8,128)(2,1)}, bf16[8,256,128]{2,1,0:T(8,128)(2,1)S(1)}) custom-call(s32[1]{0:T(128)} %bitcast.r_ref, bf16[4,256,1280]{2,1,0:T(8,128)(2,1)} %bitcast.119, bf16[4,256,640]{2,1,0:T(8,128)(2,1)} %bitcast.128, ...), custom_call_target="tpu_custom_call" | custom-call | flops 20000000000 | bytes 1048576 | tf_op jit(solution)/shard_map/attn/pallas_call | solution.py:226
  92.5 25.9 %attn.5 = (bf16[1,256,640]{2,1,0:T(8,128)(2,1)S(1)}, bf16[4,256,1280]{2,1,0:T(8,128)(2,1)}, f32[5,256,256]{2,1,0:T(8,128)S(1)}, bf16[8,4,256,256]{3,2,1,0:T(8,128)(2,1)}, bf16[8,256,128]{2,1,0:T(8,128)(2,1)S(1)}) custom-call(s32[1]{0:T(128)} %bitcast.r_ref, bf16[4,256,1280]{2,1,0:T(8,128)(2,1)} %bitcast.120, ...), custom_call_target="tpu_custom_call", output_to_operand_aliasing={{1}: (10, {}), {3}: (11, {})} | custom-call | flops 20000000000 | bytes 1048576 | tf_op jit(solution)/shard_map/attn/pallas_call | solution.py:226
  118.4 25.7 %attn.6 = (bf16[1,256,640]{2,1,0:T(8,128)(2,1)}, bf16[4,256,1280]{2,1,0:T(8,128)(2,1)}, f32[5,256,256]{2,1,0:T(8,128)S(1)}, bf16[8,4,256,256]{3,2,1,0:T(8,128)(2,1)}, bf16[8,256,128]{2,1,0:T(8,128)(2,1)S(1)}) custom-call(s32[1]{0:T(128)} %bitcast.r_ref, bf16[4,256,1280]{2,1,0:T(8,128)(2,1)} %bitcast.121, ...), custom_call_target="tpu_custom_call", output_to_operand_aliasing={{1}: (10, {}), {3}: (11, {})} | custom-call | flops 20000000000 | bytes 1048576 | tf_op jit(solution)/shard_map/attn/pallas_call | solution.py:226
  145.2 25.8 %attn.7 = (bf16[1,256,640]{2,1,0:T(8,128)(2,1)}, bf16[4,256,1280]{2,1,0:T(8,128)(2,1)}, f32[5,256,256]{2,1,0:T(8,128)S(1)}, bf16[8,4,256,256]{3,2,1,0:T(8,128)(2,1)}, bf16[8,256,128]{2,1,0:T(8,128)(2,1)S(1)}) custom-call(s32[1]{0:T(128)} %bitcast.r_ref, bf16[4,256,1280]{2,1,0:T(8,128)(2,1)} %bitcast.122, ...), custom_call_target="tpu_custom_call", output_to_operand_aliasing={{1}: (10, {}), {3}: (11, {})} | custom-call | flops 20000000000 | bytes 1048576 | tf_op jit(solution)/shard_map/attn/pallas_call | solution.py:226
  175.5 2.8 collective-permute-start.14
  178.3 2.0 collective-permute-start.10
  181.2 2.3 pad_maximum_fusion.1
  184.8 14.1 %collective-permute-done.13.refs_26_ = bf16[1,256,640]{2,1,0:T(8,128)(2,1)S(1)} collective-permute-done((bf16[1,256,640]{2,1,0:T(8,128)(2,1)}, bf16[1,256,640]{2,1,0:T(8,128)(2,1)S(1)}, u32[]{:S(2)}, u32[]{:S(2)}) %collective-permute-start.13) | collective-permute-done | bytes 327712 | tf_op jit(solution)/shard_map/ppermute | solution.py:624
  198.9 17.7 %collective-permute-start.6 = (bf16[1,256,640]{2,1,0:T(8,128)(2,1)S(1)}, bf16[1,256,640]{2,1,0:T(8,128)(2,1)}, u32[]{:S(2)}, u32[]{:S(2)}) collective-permute-start(bf16[1,256,640]{2,1,0:T(8,128)(2,1)S(1)} %get-tuple-element.69.refs_16_), channel_id=1, source_target_pairs={{0,8},{8,16},{16,24},{24,0},{1,9},{9,17},{17,25},{25,1},{2,10},{10... | collective-permute-start | bytes 983048 | tf_op jit(solution)/shard_map/ppermute | solution.py:624
  216.6 37.1 %plane.5 = (bf16[1024,256]{1,0:T(8,128)(2,1)}, bf16[256,128]{1,0:T(8,128)(2,1)}, bf16[1024,768]{1,0:T(8,128)(2,1)}, bf16[640,2560]{1,0:T(8,128)(2,1)}, bf16[1280,768]{1,0:T(8,128)(2,1)}) custom-call(bf16[8,1024,256]{2,1,0:T(8,128)(2,1)} %bitcast.117, bf16[8,256,128]{2,1,0:T(8,128)(2,1)} %copy-done.10, bf16[1024,1280]{1,0:T(8,128)(2,1)} %bitcast.123, ...), custom_call_target="tpu_custom_call" | custom-call | flops 30000001024 | bytes 1048576 | tf_op jit(solution)/shard_map/plane/pallas_call | solution.py:524
  257.0 3.3 collective-permute-start.7
  262.6 2.9 collective-permute-start.5
  265.5 2.8 add_convert_fusion
  268.3 7.9 %collective-permute-done.7.refs_18_ = bf16[1,256,640]{2,1,0:T(8,128)(2,1)S(1)} collective-permute-done((bf16[1,256,640]{2,1,0:T(8,128)(2,1)S(1)}, bf16[1,256,640]{2,1,0:T(8,128)(2,1)S(1)}, u32[]{:S(2)}, u32[]{:S(2)}) %collective-permute-start.7) | collective-permute-done | bytes 327712 | tf_op jit(solution)/shard_map/ppermute | solution.py:624
  276.2 8.5 %collective-permute-done.8.refs_19_ = bf16[1,256,640]{2,1,0:T(8,128)(2,1)S(1)} collective-permute-done((bf16[1,256,640]{2,1,0:T(8,128)(2,1)S(1)}, bf16[1,256,640]{2,1,0:T(8,128)(2,1)S(1)}, u32[]{:S(2)}, u32[]{:S(2)}) %collective-permute-start.8) | collective-permute-done | bytes 327712 | tf_op jit(solution)/shard_map/ppermute | solution.py:624
  284.7 17.8 %collective-permute-done.4.refs_14_ = bf16[1,256,640]{2,1,0:T(8,128)(2,1)S(1)} collective-permute-done((bf16[1,256,640]{2,1,0:T(8,128)(2,1)S(1)}, bf16[1,256,640]{2,1,0:T(8,128)(2,1)S(1)}, u32[]{:S(2)}, u32[]{:S(2)}) %collective-permute-start.4) | collective-permute-done | bytes 327712 | tf_op jit(solution)/shard_map/ppermute | solution.py:624
  303.2 109.6 %plane.6 = (bf16[4,256,1152]{2,1,0:T(8,128)(2,1)}, f32[1,1024]{1,0:T(1,128)}, bf16[8,160,768]{2,1,0:T(8,128)(2,1)}, bf16[8,160,256]{2,1,0:T(8,128)(2,1)}, bf16[8...) custom-call(bf16[8,160,768]{2,1,0:T(8,128)(2,1)} %bitcast.126, bf16[8,160,256]{2,1,0:T(8,128)(2,1)} %bitcast.97, ...), custom_call_target="tpu_custom_call" | custom-call | flops 30000001024 | bytes 1048576 | tf_op jit(solution)/shard_map/plane/pallas_call | solution.py:524
  415.8 4.0 convolution_convert_fusion
  421.8 55.7 %plane.7 = (bf16[32,80,1152]{2,1,0:T(8,128)(2,1)}, bf16[1024,2560]{1,0:T(8,128)(2,1)}) custom-call(bf16[8,80,1152]{2,1,0:T(8,128)(2,1)} %bitcast.112, bf16[1024,1152]{1,0:T(8,128)(2,1)} %bitcast.125, bf16[2560,768]{1,0:T(8,128)(2,1)} %refs_2_.1, bf16[288,2560]{1,0:T(8,128)(2,1)} %bitcast.111), custom_call_target="tpu_custom_call" | custom-call | flops 30000001024 | bytes 1048576 | tf_op jit(solution)/shard_map/plane/pallas_call | solution.py:524
  477.6 5.9 %slice_convert_fusion = f32[2560,768]{1,0:T(8,128)} fusion(bf16[2560,1152]{1,0:T(8,128)(2,1)} %bitcast.75), kind=kLoop, calls=%fused_computation | loop fusion | flops 1966080 | bytes 11796480 | tf_op jit(solution)/shard_map/convert_element_type | solution.py:711
  483.5 3.0 slice.81
  487.6 2.8 copy.51
  490.4 2.0 convert_element_type.78
  493.7 5.7 %convert.16 = f32[10,64,2560]{2,1,0:T(8,128)} convert(bf16[10,64,2560]{2,1,0:T(8,128)(2,1)} %bitcast.86) | non-fusion elementwise | flops 1638400 | bytes 9830400 | tf_op jit(solution)/shard_map/convert_element_type | solution.py:711
  502.8 5.6 %copy.61 = bf16[4,256,2560]{2,1,0:T(8,128)(2,1)} copy(bf16[4,256,2560]{2,1,0:T(8,128)(2,1)} %bitcast.78) | data formatting | bytes 10485760
  508.5 2.4 copy.62
  (127 shorter events, 36.0 us)
Async XLA Ops:
  7.2 296.0 %all-gather.2.cloned.1.call-start = ((), (), s32[]{:S(2)}) async-start(), calls=%async_computation | async-start | bytes 14745600 | tf_op jit(solution)/shard_map/all_gather | solution.py:668
  9.0 53.7 %collective-permute-start = (bf16[80,2560]{1,0:T(8,128)(2,1)}, bf16[80,2560]{1,0:T(8,128)(2,1)S(1)}, u32[]{:S(2)}, u32[]{:S(2)}) collective-permute-start(bf16[80,2560]{1,0:T(8,128)(2,1)} %constant_dynamic-slice_fusion.2), channel_id=1, source_target_pairs={{0,8},{8,16},{16,24},{24,0},{1,9},{9,17},{17,25},{25,1},{2,10},{10... | collective-permute-start | bytes 1228808 | tf_op jit(solution)/shard_map/ppermute | solution.py:624
  12.1 50.6 %collective-permute-start.1 = (bf16[80,2560]{1,0:T(8,128)(2,1)}, bf16[80,2560]{1,0:T(8,128)(2,1)}, u32[]{:S(2)}, u32[]{:S(2)}) collective-permute-start(bf16[80,2560]{1,0:T(8,128)(2,1)} %constant_dynamic-slice_fusion.2), channel_id=1, source_target_pairs={{0,16},{8,24},{16,0},{24,8},{1,17},{9,25},{17,1},{25,9},{2,18},{10... | collective-permute-start | bytes 1228808 | tf_op jit(solution)/shard_map/ppermute | solution.py:624
  14.7 48.0 %collective-permute-start.2 = (bf16[80,2560]{1,0:T(8,128)(2,1)}, bf16[80,2560]{1,0:T(8,128)(2,1)}, u32[]{:S(2)}, u32[]{:S(2)}) collective-permute-start(bf16[80,2560]{1,0:T(8,128)(2,1)} %constant_dynamic-slice_fusion.2), channel_id=1, source_target_pairs={{0,24},{8,0},{16,8},{24,16},{1,25},{9,1},{17,9},{25,17},{2,26},{10... | collective-permute-start | bytes 1228808 | tf_op jit(solution)/shard_map/ppermute | solution.py:624
  16.0 6.2 %copy-start.15 = (bf16[768,10,96]{0,2,1:T(8,128)(2,1)S(1)}, bf16[768,10,96]{0,2,1:T(8,128)(2,1)}, u32[]{:S(2)}) copy-start(bf16[768,10,96]{0,2,1:T(8,128)(2,1)} %param.16) | copy-start | bytes 4423684
  25.6 4.4 copy-start.20
  67.1 25.4 %copy-start.5 = (bf16[256,10,64]{0,2,1:T(8,128)(2,1)S(1)}, bf16[256,10,64]{0,2,1:T(8,128)(2,1)}, u32[]{:S(2)}) copy-start(bf16[256,10,64]{0,2,1:T(8,128)(2,1)} %param.17) | copy-start | bytes 983044
  67.1 25.4 %copy-start.7 = (bf16[256,10,64]{0,2,1:T(8,128)(2,1)S(1)}, bf16[256,10,64]{0,2,1:T(8,128)(2,1)}, u32[]{:S(2)}) copy-start(bf16[256,10,64]{0,2,1:T(8,128)(2,1)} %param.18) | copy-start | bytes 983044
  67.1 25.4 %copy-start.9 = (bf16[8,256,128]{2,1,0:T(8,128)(2,1)S(1)}, bf16[8,256,128]{2,1,0:T(8,128)(2,1)}, u32[]{:S(2)}) copy-start(bf16[8,256,128]{2,1,0:T(8,128)(2,1)} %get-tuple-element.55.rest_1_) | copy-start | bytes 1572868
  92.5 170.1 %copy-start.2 = (bf16[1,256,640]{2,1,0:T(8,128)(2,1)}, bf16[1,256,640]{2,1,0:T(8,128)(2,1)S(1)}, u32[]{:S(2)}) copy-start(bf16[1,256,640]{2,1,0:T(8,128)(2,1)S(1)} %get-tuple-element.68.refs_12_) | copy-start | bytes 983044
  118.4 141.9 %copy-start.3 = (bf16[1,256,640]{2,1,0:T(8,128)(2,1)}, bf16[1,256,640]{2,1,0:T(8,128)(2,1)S(1)}, u32[]{:S(2)}) copy-start(bf16[1,256,640]{2,1,0:T(8,128)(2,1)S(1)} %get-tuple-element.69.refs_16_) | copy-start | bytes 983044
  172.1 12.7 %copy-start.10 = (bf16[8,256,128]{2,1,0:T(8,128)(2,1)}, bf16[8,256,128]{2,1,0:T(8,128)(2,1)S(1)}, u32[]{:S(2)}) copy-start(bf16[8,256,128]{2,1,0:T(8,128)(2,1)S(1)} %get-tuple-element.66.refs_1_) | copy-start | bytes 1572868
  172.1 12.7 %collective-permute-start.12 = (bf16[1,256,640]{2,1,0:T(8,128)(2,1)}, bf16[1,256,640]{2,1,0:T(8,128)(2,1)S(1)}, u32[]{:S(2)}, u32[]{:S(2)}) collective-permute-start(bf16[1,256,640]{2,1,0:T(8,128)(2,1)} %get-tuple-element.71.refs_24_), channel_id=1, source_target_pairs={{0,8},{8,16},{16,24},{24,0},{1,9},{9,17},{17,25},{25,1},{2,10},{10... | collective-permute-start | bytes 983048 | tf_op jit(solution)/shard_map/ppermute | solution.py:624
  172.8 26.1 %collective-permute-start.13 = (bf16[1,256,640]{2,1,0:T(8,128)(2,1)}, bf16[1,256,640]{2,1,0:T(8,128)(2,1)S(1)}, u32[]{:S(2)}, u32[]{:S(2)}) collective-permute-start(bf16[1,256,640]{2,1,0:T(8,128)(2,1)} %get-tuple-element.71.refs_24_), channel_id=1, source_target_pairs={{0,16},{8,24},{16,0},{24,8},{1,17},{9,25},{17,1},{25,9},{2,18},{10... | collective-permute-start | bytes 983048 | tf_op jit(solution)/shard_map/ppermute | solution.py:624
  175.5 81.5 %collective-permute-start.14 = (bf16[1,256,640]{2,1,0:T(8,128)(2,1)}, bf16[1,256,640]{2,1,0:T(8,128)(2,1)}, u32[]{:S(2)}, u32[]{:S(2)}) collective-permute-start(bf16[1,256,640]{2,1,0:T(8,128)(2,1)} %get-tuple-element.71.refs_24_), channel_id=1, source_target_pairs={{0,24},{8,0},{16,8},{24,16},{1,25},{9,1},{17,9},{25,17},{2,26},{10... | collective-permute-start | bytes 983048 | tf_op jit(solution)/shard_map/ppermute | solution.py:624
  178.3 82.1 %collective-permute-start.10 = (bf16[1,256,640]{2,1,0:T(8,128)(2,1)}, bf16[1,256,640]{2,1,0:T(8,128)(2,1)}, u32[]{:S(2)}, u32[]{:S(2)}) collective-permute-start(bf16[1,256,640]{2,1,0:T(8,128)(2,1)} %get-tuple-element.70.refs_20_), channel_id=1, source_target_pairs={{0,16},{8,24},{16,0},{24,8},{1,17},{9,25},{17,1},{25,9},{2,18},{10... | collective-permute-start | bytes 983048 | tf_op jit(solution)/shard_map/ppermute | solution.py:624
  180.3 80.3 %collective-permute-start.11 = (bf16[1,256,640]{2,1,0:T(8,128)(2,1)}, bf16[1,256,640]{2,1,0:T(8,128)(2,1)}, u32[]{:S(2)}, u32[]{:S(2)}) collective-permute-start(bf16[1,256,640]{2,1,0:T(8,128)(2,1)} %get-tuple-element.70.refs_20_), channel_id=1, source_target_pairs={{0,24},{8,0},{16,8},{24,16},{1,25},{9,1},{17,9},{25,17},{2,26},{10... | collective-permute-start | bytes 983048 | tf_op jit(solution)/shard_map/ppermute | solution.py:624
  184.8 14.1 %copy-start.22 = (bf16[1,256,640]{2,1,0:T(8,128)(2,1)}, bf16[1,256,640]{2,1,0:T(8,128)(2,1)S(1)}, u32[]{:S(2)}) copy-start(bf16[1,256,640]{2,1,0:T(8,128)(2,1)S(1)} %collective-permute-done.12.refs_25_) | copy-start | bytes 983044
  184.8 77.6 %collective-permute-start.9 = (bf16[1,256,640]{2,1,0:T(8,128)(2,1)}, bf16[1,256,640]{2,1,0:T(8,128)(2,1)}, u32[]{:S(2)}, u32[]{:S(2)}) collective-permute-start(bf16[1,256,640]{2,1,0:T(8,128)(2,1)} %get-tuple-element.70.refs_20_), channel_id=1, source_target_pairs={{0,8},{8,16},{16,24},{24,0},{1,9},{9,17},{17,25},{25,1},{2,10},{10... | collective-permute-start | bytes 983048 | tf_op jit(solution)/shard_map/ppermute | solution.py:624
  198.9 17.7 %copy-start.23 = (bf16[1,256,640]{2,1,0:T(8,128)(2,1)}, bf16[1,256,640]{2,1,0:T(8,128)(2,1)S(1)}, u32[]{:S(2)}) copy-start(bf16[1,256,640]{2,1,0:T(8,128)(2,1)S(1)} %collective-permute-done.13.refs_26_) | copy-start | bytes 983044
  198.9 63.7 %collective-permute-start.6 = (bf16[1,256,640]{2,1,0:T(8,128)(2,1)S(1)}, bf16[1,256,640]{2,1,0:T(8,128)(2,1)}, u32[]{:S(2)}, u32[]{:S(2)}) collective-permute-start(bf16[1,256,640]{2,1,0:T(8,128)(2,1)S(1)} %get-tuple-element.69.refs_16_), channel_id=1, source_target_pairs={{0,8},{8,16},{16,24},{24,0},{1,9},{9,17},{17,25},{25,1},{2,10},{10... | collective-permute-start | bytes 983048 | tf_op jit(solution)/shard_map/ppermute | solution.py:624
  257.0 19.2 %collective-permute-start.7 = (bf16[1,256,640]{2,1,0:T(8,128)(2,1)S(1)}, bf16[1,256,640]{2,1,0:T(8,128)(2,1)S(1)}, u32[]{:S(2)}, u32[]{:S(2)}) collective-permute-start(bf16[1,256,640]{2,1,0:T(8,128)(2,1)S(1)} %get-tuple-element.69.refs_16_), channel_id=1, source_target_pairs={{0,16},{8,24},{16,0},{24,8},{1,17},{9,25},{17,1},{25,9},{2,18},{10... | collective-permute-start | bytes 983048 | tf_op jit(solution)/shard_map/ppermute | solution.py:624
  260.3 24.4 %collective-permute-start.8 = (bf16[1,256,640]{2,1,0:T(8,128)(2,1)S(1)}, bf16[1,256,640]{2,1,0:T(8,128)(2,1)S(1)}, u32[]{:S(2)}, u32[]{:S(2)}) collective-permute-start(bf16[1,256,640]{2,1,0:T(8,128)(2,1)S(1)} %get-tuple-element.69.refs_16_), channel_id=1, source_target_pairs={{0,24},{8,0},{16,8},{24,16},{1,25},{9,1},{17,9},{25,17},{2,26},{10... | collective-permute-start | bytes 983048 | tf_op jit(solution)/shard_map/ppermute | solution.py:624
  260.6 24.1 %collective-permute-start.3 = (bf16[1,256,640]{2,1,0:T(8,128)(2,1)S(1)}, bf16[1,256,640]{2,1,0:T(8,128)(2,1)S(1)}, u32[]{:S(2)}, u32[]{:S(2)}) collective-permute-start(bf16[1,256,640]{2,1,0:T(8,128)(2,1)S(1)} %get-tuple-element.68.refs_12_), channel_id=1, source_target_pairs={{0,8},{8,16},{16,24},{24,0},{1,9},{9,17},{17,25},{25,1},{2,10},{10... | collective-permute-start | bytes 983048 | tf_op jit(solution)/shard_map/ppermute | solution.py:624
  262.4 40.1 %collective-permute-start.4 = (bf16[1,256,640]{2,1,0:T(8,128)(2,1)S(1)}, bf16[1,256,640]{2,1,0:T(8,128)(2,1)S(1)}, u32[]{:S(2)}, u32[]{:S(2)}) collective-permute-start(bf16[1,256,640]{2,1,0:T(8,128)(2,1)S(1)} %get-tuple-element.68.refs_12_), channel_id=1, source_target_pairs={{0,16},{8,24},{16,0},{24,8},{1,17},{9,25},{17,1},{25,9},{2,18},{10... | collective-permute-start | bytes 983048 | tf_op jit(solution)/shard_map/ppermute | solution.py:624
  262.6 40.6 %collective-permute-start.5 = (bf16[1,256,640]{2,1,0:T(8,128)(2,1)S(1)}, bf16[1,256,640]{2,1,0:T(8,128)(2,1)}, u32[]{:S(2)}, u32[]{:S(2)}) collective-permute-start(bf16[1,256,640]{2,1,0:T(8,128)(2,1)S(1)} %get-tuple-element.68.refs_12_), channel_id=1, source_target_pairs={{0,24},{8,0},{16,8},{24,16},{1,25},{9,1},{17,9},{25,17},{2,26},{10... | collective-permute-start | bytes 983048 | tf_op jit(solution)/shard_map/ppermute | solution.py:624
  276.2 26.3 %copy-start.24 = (bf16[1,256,640]{2,1,0:T(8,128)(2,1)}, bf16[1,256,640]{2,1,0:T(8,128)(2,1)S(1)}, u32[]{:S(2)}) copy-start(bf16[1,256,640]{2,1,0:T(8,128)(2,1)S(1)} %collective-permute-done.7.refs_18_) | copy-start | bytes 983044
  284.7 17.8 %copy-start.25 = (bf16[1,256,640]{2,1,0:T(8,128)(2,1)}, bf16[1,256,640]{2,1,0:T(8,128)(2,1)S(1)}, u32[]{:S(2)}) copy-start(bf16[1,256,640]{2,1,0:T(8,128)(2,1)S(1)} %collective-permute-done.8.refs_19_) | copy-start | bytes 983044
  284.7 17.8 %copy-start.26 = (bf16[1,256,640]{2,1,0:T(8,128)(2,1)}, bf16[1,256,640]{2,1,0:T(8,128)(2,1)S(1)}, u32[]{:S(2)}) copy-start(bf16[1,256,640]{2,1,0:T(8,128)(2,1)S(1)} %collective-permute-done.3.refs_13_) | copy-start | bytes 983044
  493.7 5.7 %copy-start.14 = (bf16[8,160,256]{2,1,0:T(8,128)(2,1)S(1)}, bf16[8,160,256]{2,1,0:T(8,128)(2,1)}, u32[]{:S(2)}) copy-start(bf16[8,160,256]{2,1,0:T(8,128)(2,1)} %get-tuple-element.90) | copy-start | bytes 1966084
  500.9 7.5 %slice-start = ((s8[5242880]{0:T(1024)(128)(4,1)}), s8[4194304]{0:T(1024)(128)(4,1)S(1)}, s32[]{:S(2)}) async-start(s8[5242880]{0:T(1024)(128)(4,1)} %bitcast.79), calls=%async_computation.1 | async-start | bytes 8388608
  502.8 5.7 %slice-start.1 = ((s8[5242880]{0:T(1024)(128)(4,1)}), s8[1048576]{0:T(1024)(128)(4,1)S(1)}, s32[]{:S(2)}) async-start(s8[5242880]{0:T(1024)(128)(4,1)} %bitcast.79), calls=%async_computation.2 | async-start | bytes 2097152
  (15 other events, 30.9 us)
Sparse Core Ops, SparseCore 0:
  65.5 72.8 all-gather.1
